TPU v7x, 32 devices: a whole 2x2x4 slice. The times are simulated.
32 devices in a mesh: sub: 8 (over z, x), slab: 4 (over y, core).
Axes of the slice: x: 2, y: 2, z: 4, core: 2. Of those that a mesh axis runs over, the one named last changes fastest.
Arguments:
- residual: float32 [8, 4, 128, 1024], P('sub', 'slab'), may hold values from -6 to 6
- inverse_slab: float32 [8, 4, 1024, 1024], P('sub', 'slab'), may hold values from -1 to 2, as said below
- diagonal: float32 [8, 4, 1024], P('sub', 'slab'), may hold values from 0.2 to 0.6
- primal_index: int32 [8, 4, 32], P('sub', 'slab'), may hold values from 0 to 1023
- coarse_map: int32 [8, 32], P('sub'), may hold values from 0 to 127
- schur_small: float32 [8, 32, 32], P('sub'), may hold values from -1 to 2, as said below
- constraint_basis: float32 [8, 4, 32, 1024], P('sub', 'slab'), may hold values from -0.75 to 0.75
- coarse_basis: float32 [8, 4, 32, 1024], P('sub', 'slab'), may hold values from -0.75 to 0.75
- coarse_inverse: float32 [128, 128], P(None, 'sub'), may hold values from -1 to 2, as said below
Outputs:
- preconditioned: float32 [8, 4, 128, 1024], P('sub', 'slab')
Inputs may be any that keep to these rules, and one draw needn't show every extreme that they name: `inverse_slab`: A diagonal near 0.5 with full off-diagonal entries of moderate size. `schur_small`: A diagonal near 1 with full off-diagonal entries of moderate size. `coarse_inverse`: A diagonal near 1 with full off-diagonal entries of moderate size.
All inputs are finite; a program needn't handle non-finite values.
Results may differ from a plain program's by a relative error of at most 0.0001.
Values sent between devices are 32-bit elements; how exact they have to be, the bound alone decides.
No kernel may reach another device: no remote copies, remote signals or barrier semaphores. Data moves between devices by JAX's collectives and lax.ppermute only.
A program may use at most 64 MiB of HBM per device.

v0:
```python
import jax
import jax.numpy as jnp
from jax import lax
from jax.sharding import PartitionSpec as P

highest = lax.Precision.HIGHEST


def passed_along(array, axis, by):
    peers = lax.axis_size(axis)
    pairs = [(i, i + by) for i in range(peers) if 0 <= i + by < peers]
    return lax.ppermute(array, axis, pairs)


def product(left, right):
    return jnp.dot(left, right, precision=highest, preferred_element_type=jnp.float32)


def eliminate_chain(vector, inverse, levels):
    forward = product(vector, inverse)
    for level in range(levels - 1):
        carried = passed_along(forward, "slab", 1)
        forward = product(vector + carried, inverse)
    backward = forward
    for level in range(levels - 1):
        carried = passed_along(backward, "slab", -1)
        backward = forward + product(carried, inverse)
    return backward


def apply_once(
    vector, inverse, index, onehot, schur, constraint_basis, coarse_basis, inverse_whole, levels
):
    neumann = eliminate_chain(vector, inverse, levels)
    partial_value = jnp.take(neumann, index, axis=1)
    primal = lax.psum(partial_value, "slab")
    coarse_rhs = lax.psum(product(primal, onehot), "sub")
    multiplier = product(primal, schur)
    constrained = neumann - product(multiplier, constraint_basis)
    coarse_sol = product(coarse_rhs, inverse_whole)
    picked = product(coarse_sol, onehot.T)
    return constrained + product(picked, coarse_basis)


def on_device(
    residual,
    inverse_slab,
    diagonal,
    primal_index,
    coarse_map,
    schur_small,
    constraint_basis,
    coarse_basis,
    coarse_inverse,
):
    levels = lax.axis_size("slab")
    vector = residual[0, 0]
    inverse = inverse_slab[0, 0]
    index = primal_index[0, 0]
    coarse_count = coarse_inverse.shape[0]
    onehot = (coarse_map[0][:, None] == jnp.arange(coarse_count, dtype=jnp.int32)[None, :]).astype(
        jnp.float32
    )
    schur = schur_small[0]
    basis_one = constraint_basis[0, 0]
    basis_two = coarse_basis[0, 0]
    inverse_whole = lax.all_gather(coarse_inverse, "sub", axis=1, tiled=True)
    first_pass = apply_once(
        vector, inverse, index, onehot, schur, basis_one, basis_two, inverse_whole, levels
    )
    defect = vector - diagonal[0, 0][None, :] * first_pass
    second_pass = apply_once(
        defect, inverse, index, onehot, schur, basis_one, basis_two, inverse_whole, levels
    )
    return (first_pass + second_pass)[None, None]


def solution(mesh):
    placed = (
        P("sub", "slab", None, None),
        P("sub", "slab", None, None),
        P("sub", "slab", None),
        P("sub", "slab", None),
        P("sub", None),
        P("sub", None, None),
        P("sub", "slab", None, None),
        P("sub", "slab", None, None),
        P(None, "sub"),
    )
    return jax.shard_map(
        on_device,
        mesh=mesh,
        in_specs=placed,
        out_specs=P("sub", "slab", None, None),
        check_vma=False,
    )
```

profile of v0, /device:TPU:0, one launch (start us, length us, event | category | flops | bytes accessed | tf_op | source)
XLA Modules:
  0.0 372.0 jit_solution(13199960516831631086)
XLA Ops:
  6.5 4.9 %fusion.26 = f32[128,1024]{1,0:T(8,128)S(1)} fusion(f32[1,1,1024,1024]{3,2,1,0:T(8,128)} %param.12, f32[1,1,128,1024]{3,2,1,0:T(8,128)} %param.11), kind=kOutput, calls=%fused_computation.28 | convolution fusion | flops 1610612736 | bytes 5242880 | tf_op jit(solution)/shard_map/dot_general | solution.py:16
  11.4 2.4 collective-permute-start
  13.9 1.5 collective-permute-done
  15.4 2.4 fusion.24
  17.8 9.1 %collective-permute-start.1 = (f32[128,1024]{1,0:T(8,128)S(1)}, f32[128,1024]{1,0:T(8,128)S(1)}, u32[]{:S(2)}, u32[]{:S(2)}) collective-permute-start(f32[128,1024]{1,0:T(8,128)S(1)} %fusion.24), channel_id=1, source_target_pairs={{0,1},{1,2},{2,3},{4,5},{5,6},{6,7},{8,9},{9,10},{10,11},{12,13},{... | collective-permute-start | bytes 1572872 | tf_op jit(solution)/shard_map/ppermute | solution.py:12
  27.0 1.5 collective-permute-done.1
  28.4 2.4 fusion.22
  30.9 9.0 %collective-permute-start.2 = (f32[128,1024]{1,0:T(8,128)S(1)}, f32[128,1024]{1,0:T(8,128)S(1)}, u32[]{:S(2)}, u32[]{:S(2)}) collective-permute-start(f32[128,1024]{1,0:T(8,128)S(1)} %fusion.22), channel_id=1, source_target_pairs={{0,1},{1,2},{2,3},{4,5},{5,6},{6,7},{8,9},{9,10},{10,11},{12,13},{... | collective-permute-start | bytes 1572872 | tf_op jit(solution)/shard_map/ppermute | solution.py:12
  39.9 1.5 collective-permute-done.2
  41.4 2.4 fusion.20
  43.8 1.5 collective-permute-start.3
  45.3 8.9 %collective-permute-done.3 = f32[128,1024]{1,0:T(8,128)S(1)} collective-permute-done((f32[128,1024]{1,0:T(8,128)S(1)}, f32[128,1024]{1,0:T(8,128)S(1)}, u32[]{:S(2)}, u32[]{:S(2)}) %collective-permute-start.3) | collective-permute-done | bytes 524320 | tf_op jit(solution)/shard_map/ppermute | solution.py:12
  54.2 2.4 fusion.28
  56.6 1.3 collective-permute-start.4
  57.9 30.9 %all_gather.3 = f32[128,128]{0,1:T(8,128)S(1)} all-gather(f32[128,16]{0,1:T(8,128)S(1)} %copy-done.7), channel_id=1, replica_groups=mesh['sub'=8,'slab'=4] {'sub'}, dimensions={1}, use_global_device_ids=true | all-gather | bytes 73728 | tf_op jit(solution)/shard_map/all_gather | solution.py:67
  88.8 2.4 fusion.31
  91.3 1.4 collective-permute-start.5
  92.7 4.5 %collective-permute-done.5 = f32[128,1024]{1,0:T(8,128)S(1)} collective-permute-done((f32[128,1024]{1,0:T(8,128)S(1)}, f32[128,1024]{1,0:T(8,128)S(1)}, u32[]{:S(2)}, u32[]{:S(2)}) %collective-permute-start.5) | collective-permute-done | bytes 524320 | tf_op jit(solution)/shard_map/ppermute | solution.py:12
  97.2 2.4 fusion.34
  100.5 23.4 %psum.28 = f32[128,32]{0,1:T(8,128)S(1)} all-reduce(f32[128,32]{0,1:T(8,128)S(1)} %select_bitcast_fusion.1), channel_id=1, replica_groups=mesh['sub'=8,'slab'=4] {'slab'}, use_global_device_ids=true, to_apply=%region_0.0 | all-reduce | flops 4096 | bytes 32768 | tf_op jit(solution)/shard_map/psum | solution.py:36
  123.9 0.9 fusion.67
  125.2 70.1 %all-reduce.3.cloned.1.call-done = f32[128,128]{1,0:T(8,128)} async-done(((f32[128,128]{1,0:T(8,128)}), f32[128,128]{1,0:T(8,128)}) %all-reduce.3.cloned.1.call-update) | async-done | bytes 65552 | tf_op jit(solution)/shard_map/psum | solution.py:37
  195.3 1.1 fusion.72
  197.2 0.6 bitcast_subtract_fusion
  197.8 4.9 %fusion.12 = f32[128,1024]{1,0:T(8,128)S(1)} fusion(f32[128,1024]{1,0:T(8,128)S(1)} %get-tuple-element.6, f32[1,1,1024,1024]{3,2,1,0:T(8,128)} %param.12), kind=kOutput, calls=%fused_computation.14 | convolution fusion | flops 1610612736 | bytes 5242880 | tf_op jit(solution)/shard_map/dot_general | solution.py:16
  202.8 1.5 collective-permute-start.6
  204.3 1.3 collective-permute-done.6
  205.6 2.4 fusion.10
  208.0 8.7 %collective-permute-start.7 = (f32[128,1024]{1,0:T(8,128)S(1)}, f32[128,1024]{1,0:T(8,128)S(1)}, u32[]{:S(2)}, u32[]{:S(2)}) collective-permute-start(f32[128,1024]{1,0:T(8,128)S(1)} %fusion.10), channel_id=1, source_target_pairs={{0,1},{1,2},{2,3},{4,5},{5,6},{6,7},{8,9},{9,10},{10,11},{12,13},{... | collective-permute-start | bytes 1572872 | tf_op jit(solution)/shard_map/ppermute | solution.py:12
  216.7 1.5 collective-permute-done.7
  218.2 2.4 fusion.8
  220.6 9.0 %collective-permute-start.8 = (f32[128,1024]{1,0:T(8,128)S(1)}, f32[128,1024]{1,0:T(8,128)S(1)}, u32[]{:S(2)}, u32[]{:S(2)}) collective-permute-start(f32[128,1024]{1,0:T(8,128)S(1)} %fusion.8), channel_id=1, source_target_pairs={{0,1},{1,2},{2,3},{4,5},{5,6},{6,7},{8,9},{9,10},{10,11},{12,13},{... | collective-permute-start | bytes 1572872 | tf_op jit(solution)/shard_map/ppermute | solution.py:12
  229.6 1.5 collective-permute-done.8
  231.1 2.4 fusion.6
  233.5 1.3 collective-permute-start.9
  234.8 9.1 %collective-permute-done.9 = f32[128,1024]{1,0:T(8,128)S(1)} collective-permute-done((f32[128,1024]{1,0:T(8,128)S(1)}, f32[128,1024]{1,0:T(8,128)S(1)}, u32[]{:S(2)}, u32[]{:S(2)}) %collective-permute-start.9) | collective-permute-done | bytes 524320 | tf_op jit(solution)/shard_map/ppermute | solution.py:12
  243.9 2.4 fusion.37
  246.4 1.3 collective-permute-start.10
  247.7 9.9 %collective-permute-done.10 = f32[128,1024]{1,0:T(8,128)S(1)} collective-permute-done((f32[128,1024]{1,0:T(8,128)S(1)}, f32[128,1024]{1,0:T(8,128)S(1)}, u32[]{:S(2)}, u32[]{:S(2)}) %collective-permute-start.10) | collective-permute-done | bytes 524320 | tf_op jit(solution)/shard_map/ppermute | solution.py:12
  257.6 2.4 fusion.40
  260.0 1.5 collective-permute-start.11
  261.6 8.9 %collective-permute-done.11 = f32[128,1024]{1,0:T(8,128)S(1)} collective-permute-done((f32[128,1024]{1,0:T(8,128)S(1)}, f32[128,1024]{1,0:T(8,128)S(1)}, u32[]{:S(2)}, u32[]{:S(2)}) %collective-permute-start.11) | collective-permute-done | bytes 524320 | tf_op jit(solution)/shard_map/ppermute | solution.py:12
  270.5 2.4 fusion.43
  273.8 17.2 %psum.30 = f32[128,32]{0,1:T(8,128)S(1)} all-reduce(f32[128,32]{0,1:T(8,128)S(1)} %select_bitcast_fusion), channel_id=1, replica_groups=mesh['sub'=8,'slab'=4] {'slab'}, use_global_device_ids=true, to_apply=%region_2.4 | all-reduce | flops 4096 | bytes 32768 | tf_op jit(solution)/shard_map/psum | solution.py:36
  291.0 0.9 fusion.65
  292.2 69.2 %all-reduce.5.cloned.1.call-done = f32[128,128]{1,0:T(8,128)} async-done(((f32[128,128]{1,0:T(8,128)}), f32[128,128]{1,0:T(8,128)}) %all-reduce.5.cloned.1.call-update) | async-done | bytes 65552 | tf_op jit(solution)/shard_map/psum | solution.py:37
  361.4 1.1 fusion.73
  363.3 1.4 fusion.49
  (40 shorter events, 4.0 us)
Async XLA Ops:
  6.5 190.7 %copy-start = (f32[1,1,32,1024]{3,2,1,0:T(8,128)S(1)}, f32[1,1,32,1024]{3,2,1,0:T(8,128)}, u32[]{:S(2)}) copy-start(f32[1,1,32,1024]{3,2,1,0:T(8,128)} %param.17) | copy-start | bytes 393220
  6.5 8.8 %copy-start.3 = (f32[1,1,128,1024]{3,2,1,0:T(8,128)S(1)}, f32[1,1,128,1024]{3,2,1,0:T(8,128)}, u32[]{:S(2)}) copy-start(f32[1,1,128,1024]{3,2,1,0:T(8,128)} %param.11) | copy-start | bytes 1572868
  6.5 188.7 %all-reduce.3.cloned.1.call-start = ((), (), s32[]{:S(2)}) async-start(), calls=%async_computation | async-start | bytes 131072 | tf_op jit(solution)/shard_map/psum | solution.py:37
  6.5 8.8 %copy-start.1 = (f32[1,1,1024,1024]{3,2,1,0:T(8,128)S(1)}, f32[1,1,1024,1024]{3,2,1,0:T(8,128)}, u32[]{:S(2)}) copy-start(f32[1,1,1024,1024]{3,2,1,0:T(8,128)} %param.12) | copy-start | bytes 12582916
  11.4 3.9 %collective-permute-start = (f32[128,1024]{1,0:T(8,128)S(1)}, f32[128,1024]{1,0:T(8,128)S(1)}, u32[]{:S(2)}, u32[]{:S(2)}) collective-permute-start(f32[128,1024]{1,0:T(8,128)S(1)} %fusion.26), channel_id=1, source_target_pairs={{0,1},{1,2},{2,3},{4,5},{5,6},{6,7},{8,9},{9,10},{10,11},{12,13},{... | collective-permute-start | bytes 1572872 | tf_op jit(solution)/shard_map/ppermute | solution.py:12
  17.8 10.6 %collective-permute-start.1 = (f32[128,1024]{1,0:T(8,128)S(1)}, f32[128,1024]{1,0:T(8,128)S(1)}, u32[]{:S(2)}, u32[]{:S(2)}) collective-permute-start(f32[128,1024]{1,0:T(8,128)S(1)} %fusion.24), channel_id=1, source_target_pairs={{0,1},{1,2},{2,3},{4,5},{5,6},{6,7},{8,9},{9,10},{10,11},{12,13},{... | collective-permute-start | bytes 1572872 | tf_op jit(solution)/shard_map/ppermute | solution.py:12
  30.9 10.5 %collective-permute-start.2 = (f32[128,1024]{1,0:T(8,128)S(1)}, f32[128,1024]{1,0:T(8,128)S(1)}, u32[]{:S(2)}, u32[]{:S(2)}) collective-permute-start(f32[128,1024]{1,0:T(8,128)S(1)} %fusion.22), channel_id=1, source_target_pairs={{0,1},{1,2},{2,3},{4,5},{5,6},{6,7},{8,9},{9,10},{10,11},{12,13},{... | collective-permute-start | bytes 1572872 | tf_op jit(solution)/shard_map/ppermute | solution.py:12
  43.8 14.1 %copy-start.7 = (f32[128,16]{0,1:T(8,128)S(1)}, f32[128,16]{0,1:T(8,128)}, u32[]{:S(2)}) copy-start(f32[128,16]{0,1:T(8,128)} %param.19) | copy-start | bytes 24580
  43.8 10.4 %collective-permute-start.3 = (f32[128,1024]{1,0:T(8,128)S(1)}, f32[128,1024]{1,0:T(8,128)S(1)}, u32[]{:S(2)}, u32[]{:S(2)}) collective-permute-start(f32[128,1024]{1,0:T(8,128)S(1)} %fusion.20), channel_id=1, source_target_pairs={{1,0},{2,1},{3,2},{5,4},{6,5},{7,6},{9,8},{10,9},{11,10},{13,12},{... | collective-permute-start | bytes 1572872 | tf_op jit(solution)/shard_map/ppermute | solution.py:12
  56.6 36.1 %copy-start.9 = (s32[1,1,32]{2,1,0:T(1,128)S(1)}, s32[1,1,32]{2,1,0:T(1,128)}, u32[]{:S(2)}) copy-start(s32[1,1,32]{2,1,0:T(1,128)} %param.14) | copy-start | bytes 388
  56.6 32.2 %collective-permute-start.4 = (f32[128,1024]{1,0:T(8,128)S(1)}, f32[128,1024]{1,0:T(8,128)S(1)}, u32[]{:S(2)}, u32[]{:S(2)}) collective-permute-start(f32[128,1024]{1,0:T(8,128)S(1)} %fusion.28), channel_id=1, source_target_pairs={{1,0},{2,1},{3,2},{5,4},{6,5},{7,6},{9,8},{10,9},{11,10},{13,12},{... | collective-permute-start | bytes 1572872 | tf_op jit(solution)/shard_map/ppermute | solution.py:12
  91.2 32.7 %copy-start.6 = (s32[1,32]{1,0:T(1,128)S(1)}, s32[1,32]{1,0:T(1,128)}, u32[]{:S(2)}) copy-start(s32[1,32]{1,0:T(1,128)} %param.15) | copy-start | bytes 388
  91.2 33.6 %copy-start.5 = (f32[1,32,32]{2,1,0:T(8,128)S(1)}, f32[1,32,32]{2,1,0:T(8,128)}, u32[]{:S(2)}) copy-start(f32[1,32,32]{2,1,0:T(8,128)} %param.16) | copy-start | bytes 12292
  91.2 105.4 %copy-start.4 = (f32[1,1,32,1024]{3,2,1,0:T(8,128)S(1)}, f32[1,1,32,1024]{3,2,1,0:T(8,128)}, u32[]{:S(2)}) copy-start(f32[1,1,32,1024]{3,2,1,0:T(8,128)} %param.18) | copy-start | bytes 393220
  91.3 6.0 %collective-permute-start.5 = (f32[128,1024]{1,0:T(8,128)S(1)}, f32[128,1024]{1,0:T(8,128)S(1)}, u32[]{:S(2)}, u32[]{:S(2)}) collective-permute-start(f32[128,1024]{1,0:T(8,128)S(1)} %fusion.31), channel_id=1, source_target_pairs={{1,0},{2,1},{3,2},{5,4},{6,5},{7,6},{9,8},{10,9},{11,10},{13,12},{... | collective-permute-start | bytes 1572872 | tf_op jit(solution)/shard_map/ppermute | solution.py:12
  92.7 104.5 %copy-start.8 = (f32[1,1,1024]{2,1,0:T(1,128)S(1)}, f32[1,1,1024]{2,1,0:T(1,128)}, u32[]{:S(2)}) copy-start(f32[1,1,1024]{2,1,0:T(1,128)} %param.13) | copy-start | bytes 12292
  124.8 236.6 %all-reduce.5.cloned.1.call-start = ((), (), s32[]{:S(2)}) async-start(), calls=%async_computation.1 | async-start | bytes 131072 | tf_op jit(solution)/shard_map/psum | solution.py:37
  197.2 8.4 %copy-start.2 = (f32[1,1,1024,1024]{3,2,1,0:T(8,128)S(1)}, f32[1,1,1024,1024]{3,2,1,0:T(8,128)}, u32[]{:S(2)}) copy-start(f32[1,1,1024,1024]{3,2,1,0:T(8,128)} %param.12) | copy-start | bytes 12582916
  202.8 2.8 collective-permute-start.6
  208.0 10.2 %collective-permute-start.7 = (f32[128,1024]{1,0:T(8,128)S(1)}, f32[128,1024]{1,0:T(8,128)S(1)}, u32[]{:S(2)}, u32[]{:S(2)}) collective-permute-start(f32[128,1024]{1,0:T(8,128)S(1)} %fusion.10), channel_id=1, source_target_pairs={{0,1},{1,2},{2,3},{4,5},{5,6},{6,7},{8,9},{9,10},{10,11},{12,13},{... | collective-permute-start | bytes 1572872 | tf_op jit(solution)/shard_map/ppermute | solution.py:12
  220.6 10.5 %collective-permute-start.8 = (f32[128,1024]{1,0:T(8,128)S(1)}, f32[128,1024]{1,0:T(8,128)S(1)}, u32[]{:S(2)}, u32[]{:S(2)}) collective-permute-start(f32[128,1024]{1,0:T(8,128)S(1)} %fusion.8), channel_id=1, source_target_pairs={{0,1},{1,2},{2,3},{4,5},{5,6},{6,7},{8,9},{9,10},{10,11},{12,13},{... | collective-permute-start | bytes 1572872 | tf_op jit(solution)/shard_map/ppermute | solution.py:12
  233.5 10.4 %collective-permute-start.9 = (f32[128,1024]{1,0:T(8,128)S(1)}, f32[128,1024]{1,0:T(8,128)S(1)}, u32[]{:S(2)}, u32[]{:S(2)}) collective-permute-start(f32[128,1024]{1,0:T(8,128)S(1)} %fusion.6), channel_id=1, source_target_pairs={{1,0},{2,1},{3,2},{5,4},{6,5},{7,6},{9,8},{10,9},{11,10},{13,12},{... | collective-permute-start | bytes 1572872 | tf_op jit(solution)/shard_map/ppermute | solution.py:12
  246.4 11.2 %collective-permute-start.10 = (f32[128,1024]{1,0:T(8,128)S(1)}, f32[128,1024]{1,0:T(8,128)S(1)}, u32[]{:S(2)}, u32[]{:S(2)}) collective-permute-start(f32[128,1024]{1,0:T(8,128)S(1)} %fusion.37), channel_id=1, source_target_pairs={{1,0},{2,1},{3,2},{5,4},{6,5},{7,6},{9,8},{10,9},{11,10},{13,12},{... | collective-permute-start | bytes 1572872 | tf_op jit(solution)/shard_map/ppermute | solution.py:12
  260.0 10.5 %collective-permute-start.11 = (f32[128,1024]{1,0:T(8,128)S(1)}, f32[128,1024]{1,0:T(8,128)S(1)}, u32[]{:S(2)}, u32[]{:S(2)}) collective-permute-start(f32[128,1024]{1,0:T(8,128)S(1)} %fusion.40), channel_id=1, source_target_pairs={{1,0},{2,1},{3,2},{5,4},{6,5},{7,6},{9,8},{10,9},{11,10},{13,12},{... | collective-permute-start | bytes 1572872 | tf_op jit(solution)/shard_map/ppermute | solution.py:12
Sparse Core Ops, SparseCore 0:
  124.9 70.2 all-reduce.2
  292.0 69.3 all-reduce.4
where the time goes:
time: 380 us; the launch traced here: 372 us
  waiting for transfers between devices  189 us (50%)
  blocking collectives  71.4 us (19%)
  starting transfers between devices  48.2 us (13%)
  matrix products  47 us (12%)
  between operations  14.3 us (4%)
    psum x2, waiting for transfers between devices, apply_once(): coarse_rhs = lax.psum(product(primal, onehot), 'sub')  139 us
    ppermute x12, waiting for transfers between devices, passed_along(): return lax.ppermute(array, axis, pairs)  50.1 us
    ppermute x12, starting transfers between devices, passed_along(): return lax.ppermute(array, axis, pairs)  48.1 us
    dot_general x26, matrix products, product(): jnp.dot(left, right, precision=highest, preferred_element_type=jnp.float32)  47 us
    psum x2, blocking collectives, apply_once(): primal = lax.psum(partial_value, 'slab')  40.5 us
    all_gather x1, blocking collectives, on_device(): inverse_whole = lax.all_gather(coarse_inverse, 'sub', axis=1, tiled=True)  30.9 us
  transfers between devices with their start and end apart: 14, of which 13 were waited for; matrix products, arithmetic and copies ran while one was open for 0% of the time, Pallas kernels for 0%

commit v1 on v0

v1 whole, which is shorter than its diff:
```python
import functools

import jax
import jax.numpy as jnp
from jax import lax
from jax.experimental import pallas as pl
from jax.experimental.pallas import tpu as pltpu
from jax.sharding import PartitionSpec as P


f32 = jnp.float32
bf16 = jnp.bfloat16
highest = lax.Precision.HIGHEST
LANES = 128
BLOCKS = 2
PIECES = 4


def halves(x):
    top = x.astype(bf16)
    return top, (x - top.astype(f32)).astype(bf16)


def dot(left, right):
    return jnp.dot(left, right, preferred_element_type=f32)


def dot_rows(left, right):
    return lax.dot_general(left, right, (((1,), (1,)), ((), ())), preferred_element_type=f32)


def three(x, top_right, low_right, how=dot):
    rows = x.shape[0]
    top, low = halves(x)
    both = how(jnp.concatenate([top, low], axis=0), top_right)
    return both[:rows] + both[rows:] + how(top, low_right)


def times(x, weights, member):
    return three(x, weights[member, 0], weights[member, 1])


def times_transposed(x, weights, member):
    return three(x, weights[member, 0], weights[member, 1], dot_rows)


def spec(space):
    return pl.BlockSpec(memory_space=space)


def call(body, outs, args, work, aliases=None, scratch=(), hbm=()):
    specs = [spec(pltpu.SMEM)] + [spec(pltpu.VMEM) for _ in args[1:]]
    args = list(args)
    for place in hbm:
        specs[place] = spec(pltpu.HBM)
        args[place] = pltpu.with_memory_space_constraint(args[place], pltpu.HBM)
    return pl.pallas_call(
        body,
        out_shape=outs,
        in_specs=specs,
        out_specs=[spec(pltpu.VMEM) for _ in outs],
        input_output_aliases=aliases or {},
        scratch_shapes=list(scratch),
        cost_estimate=pl.CostEstimate(flops=int(work * 8e8), bytes_accessed=0, transcendentals=0),
        compiler_params=pltpu.CompilerParams(vmem_limit_bytes=VMEM_LIMIT),
    )(*args)


VMEM_LIMIT = 20 << 20


def struct(shape, dtype=f32):
    return jax.ShapeDtypeStruct(shape, dtype)


def pick(scal, own, oth):
    first = scal[0] == 0
    return jnp.where(first, own, oth), jnp.where(first, oth, own)


def hold(idle, before, after):
    @pl.when(idle)
    def _():
        for old, new in zip(before, after):
            new[...] = old[...]


def split_own(scal, matrix, vector, one, two, aux, own, keep, send, buffer, x, total, sems):
    member = scal[0]
    size = matrix.shape[0]
    step = size // PIECES
    rows, prim = vector.shape[0], one.shape[0]
    copies = [
        pltpu.make_async_copy(vector, x.at[pl.ds(0, rows)], sems.at[0]),
        pltpu.make_async_copy(one, x.at[pl.ds(rows, prim)], sems.at[1]),
        pltpu.make_async_copy(two, x.at[pl.ds(rows + prim, prim)], sems.at[2]),
    ]
    pieces = [
        pltpu.make_async_copy(
            matrix.at[pl.ds(i * step, step)], buffer.at[pl.ds(i * step, step)], sems.at[3 + i]
        )
        for i in range(PIECES)
    ]
    for copy in copies + pieces:
        copy.start()
    for copy in copies:
        copy.wait()
    x[rows:, :] = x[rows:, :] * aux[0:1, :]
    for i, copy in enumerate(pieces):
        cols = pl.ds(i * step, step)
        copy.wait()
        top, low = halves(buffer[cols, :])
        own[0, cols, :] = top
        own[1, cols, :] = low
        part = three(x[:, cols], own[0, cols, :], own[1, cols, :])
        if i == 0:
            total[...] = part
        else:
            total[...] += part
    half = rows // 2
    keep[:half, :] = total[pl.ds(pl.multiple_of(member * half, 8), half), :]
    send[:half, :] = total[pl.ds(pl.multiple_of((1 - member) * half, 8), half), :]
    keep[half:, :] = total[rows:, :]
    send[half:, :] = total[rows:, :]


def split_other(scal, matrix, own, weights):
    other = 1 - scal[0]
    weights[scal[0]] = own[...]
    top, low = halves(matrix[...])
    weights[other, 0] = top
    weights[other, 1] = low


def start_chain(at, scal, keep, recv, weights, f_first, f_second):
    rows = f_first.shape[0]

    @pl.when(scal[1] == 0)
    def _():
        first, second = pick(scal, keep[at : at + rows, :], recv[at : at + rows, :])
        f_first[...] = first
        f_second[...] = second + times(first, weights, 1)


def start_basis(at, scal, keep, recv, weights, f_first, f_second, part):
    rows, few = f_first.shape[0], part.shape[0]

    @pl.when(scal[1] == 0)
    def _():
        first, second = pick(scal, keep[at : at + rows, :], recv[at : at + rows, :])
        f_first[...] = first
        f_second[...] = second + times(first, weights, 1)
        part[...] = f_second[pl.ds(pl.multiple_of(scal[0] * few, 8), few), :]


def up(first, second, weights):
    second = second + times(first, weights, 1)
    return first + times(second, weights, 0), second


def top_one(at, scal, keep, recv, carried, weights, n_first, n_second):
    rows = n_first.shape[0]

    @pl.when(scal[1] == 1)
    def _():
        first, second = pick(scal, keep[at : at + rows, :], recv[at : at + rows, :])
        n_first[...], n_second[...] = up(first + times(carried[...], weights, 0), second, weights)


def top_basis(at, scal, keep, recv, carried, weights, n_first, n_second):
    few = n_first.shape[0]

    @pl.when(scal[1] == 1)
    def _():
        here = pl.ds(pl.multiple_of(at + scal[0] * few, 8), few)
        first, second = pick(scal, keep[here, :], recv[here, :])
        n_first[...], n_second[...] = up(first + times(carried[...], weights, 0), second, weights)


def top_two(scal, v_first, v_second, carried, weights, own_aux, oth_aux, n_first, n_second):
    @pl.when(scal[1] == 1)
    def _():
        d_first, d_second = pick(scal, own_aux[0:1, :], oth_aux[0:1, :])
        first = times(d_first * v_first[...] + carried[...], weights, 0)
        second = times(d_second * v_second[...] + first, weights, 1)
        n_first[...] = first + times(second, weights, 0)
        n_second[...] = second


def down(f_first, f_second, carried, weights):
    second = f_second + times(carried, weights, 1)
    return f_first + times(second, weights, 0), second


def turn(scal, f_first, f_second, carried, weights, own_aux, oth_aux, *refs):
    old, (n_first, n_second, g_first, g_second) = refs[:2], refs[2:]

    @pl.when(scal[1] == 0)
    def _():
        first, second = down(f_first[...], f_second[...], carried[...], weights)
        n_second[...] = second
        n_first[...] = first
        d_first, d_second = pick(scal, own_aux[0:1, :], oth_aux[0:1, :])
        again = times(d_first * first, weights, 0)
        g_first[...] = again
        g_second[...] = times(d_second * second + again, weights, 1)

    hold(scal[1] != 0, old, (n_first, n_second))


def back_two(scal, f_first, f_second, carried, weights, *refs):
    old, (n_first, n_second) = refs[:2], refs[2:]

    @pl.when(scal[1] == 0)
    def _():
        n_first[...], n_second[...] = down(f_first[...], f_second[...], carried[...], weights)

    hold(scal[1] != 0, old, (n_first, n_second))


def back_basis(scal, f_first, f_second, carried, weights, *refs):
    old, (n_first, n_second) = refs[:2], refs[2:]
    few = n_first.shape[0]

    @pl.when(scal[1] == 0)
    def _():
        here = pl.ds(pl.multiple_of(scal[0] * few, 8), few)
        n_first[...], n_second[...] = down(f_first[here, :], f_second[here, :], carried[...], weights)

    hold(scal[1] != 0, old, (n_first, n_second))


def adjoint_start(scal, own_spots, oth_spots, weights, y_first, y_second, sent):
    @pl.when(scal[1] == 0)
    def _():
        first, second = pick(scal, own_spots[...], oth_spots[...])
        second = second + times_transposed(first, weights, 0)
        y_first[...] = first
        y_second[...] = second
        sent[...] = times_transposed(second, weights, 1)


def adjoint_top(scal, own_spots, oth_spots, carried, weights, *refs):
    old, (y_first, y_second, z_first, z_second) = refs[:2], refs[2:]

    @pl.when(scal[1] == 1)
    def _():
        first, second = pick(scal, own_spots[...], oth_spots[...])
        first = first + carried[...]
        second = second + times_transposed(first, weights, 0)
        y_first[...] = first
        y_second[...] = second
        last = times_transposed(second, weights, 1)
        z_second[...] = last
        z_first[...] = times_transposed(first + last, weights, 0)

    hold(scal[1] != 1, old, (y_first, y_second))


def placed(u, places, width):
    prim = u.shape[0]
    zero = jnp.zeros_like(u)
    rows = [u if i in places else zero for i in range(width // prim)]
    return jnp.concatenate(rows, axis=0)


def score(x, u):
    top, low = halves(u)
    return three(x, top, low, dot_rows)


def only(x, place, prim):
    lane = lax.broadcasted_iota(jnp.int32, x.shape, 1)
    return jnp.where((lane >= place * prim) & (lane < (place + 1) * prim), x, 0.0)


def score_top(scal, keep, recv, own_aux, oth_aux, y_first, y_second, z_first, z_second, *refs):
    blocks, values = refs[:-1], refs[-1]
    prim, width = y_first.shape[0], values.shape[1]
    half = values.shape[0]

    @pl.when(scal[1] == 1)
    def _():
        first, second = pick(scal, keep[...], recv[...])
        w = score(first, placed(y_first[...] + z_second[...], (0, 2), width)) + score(
            second, placed(y_second[...], (0, 2), width)
        )
        d_first, d_second = pick(scal, own_aux[0:1, :], oth_aux[0:1, :])
        n_first = jnp.concatenate([r[...] for r in blocks[0::2]], axis=0)
        n_second = jnp.concatenate([r[...] for r in blocks[1::2]], axis=0)
        g = score(d_first * n_first, placed(z_first[...], (1,), width)) + score(
            d_second * n_second, placed(z_second[...], (1,), width)
        )
        values[...] = only(w[:half], 0, prim) + g + only(w[half:], 2, prim)


def score_turn(scal, above, carried, y_first, y_second, k_first, k_second, *refs):
    blocks, values = refs[:-1], refs[-1]
    prim, width = y_first.shape[0], values.shape[1]
    half = values.shape[0]

    @pl.when(scal[1] == 0)
    def _():
        first = jnp.concatenate([r[...] for r in blocks[0::4]] + [k_first[...]] + [r[...] for r in blocks[2::4]], axis=0)
        second = jnp.concatenate([r[...] for r in blocks[1::4]] + [k_second[...]] + [r[...] for r in blocks[3::4]], axis=0)
        w = score(first, placed(y_first[...], (0, 1, 2), width)) + score(
            second, placed(y_second[...] + carried[...], (0, 1, 2), width)
        )
        extra = k_first.shape[0]
        values[...] = (
            above[...]
            + only(w[:half], 0, prim)
            + only(w[half : half + extra], 2, prim)
            + only(w[half + extra :], 1, prim)
        )


def settle(scal, k_first, k_second, *refs):
    blocks = refs[: 4 * BLOCKS]
    keep, send, k_keep, k_send = refs[4 * BLOCKS :]
    rows = blocks[0].shape[0]
    first = scal[0] == 0
    for i in range(BLOCKS):
        a1, b1, a2, b2 = (r[...] for r in blocks[4 * i : 4 * i + 4])
        here = slice(i * rows, (i + 1) * rows)
        a, b = 2.0 * a1 - a2, 2.0 * b1 - b2
        keep[here, :] = jnp.where(first, a, b)
        send[here, :] = jnp.where(first, b, a)
    k_keep[...] = jnp.where(first, k_first[...], k_second[...])
    k_send[...] = jnp.where(first, k_second[...], k_first[...])


def finish(scal, keep, recv, q_keep, q_recv, k_keep, k_recv, one, two, out):
    rows = keep.shape[0]
    k_low, k_high = pick(scal, k_keep[...], k_recv[...])
    right = jnp.concatenate([-k_low, -k_high, one[...], two[...]], axis=0)
    top, low = halves(right)
    for n, q, which in ((keep, q_keep, scal[0]), (recv, q_recv, 1 - scal[0])):
        out[pl.ds(pl.multiple_of(which * rows, 8), rows), :] = n[...] + three(q[...], top, low)


def on_device(
    residual,
    inverse_slab,
    diagonal,
    primal_index,
    coarse_map,
    schur_small,
    constraint_basis,
    coarse_basis,
    coarse_inverse,
):
    levels = lax.axis_size("slab")
    subs = lax.axis_size("sub")
    assert levels == 4 and subs & (subs - 1) == 0
    slab = lax.axis_index("slab")
    sub = lax.axis_index("sub")
    member = slab % 2
    scal = jnp.stack([member, slab // 2]).astype(jnp.int32)

    def swap(x):
        return lax.ppermute(x, "slab", [(i, i ^ 1) for i in range(levels)])

    def rise(x):
        return lax.ppermute(x, "slab", [(0, 2), (1, 3)])

    def fall(x):
        return lax.ppermute(x, "slab", [(2, 0), (3, 1)])

    def gather(x):
        distance = 1
        while distance < subs:
            other = lax.ppermute(x, "sub", [(i, i ^ distance) for i in range(subs)])
            x = jnp.concatenate([x, other], axis=0)
            distance *= 2
        return x

    vector = residual[0, 0]
    matrix = inverse_slab[0, 0]
    one, two = constraint_basis[0, 0], coarse_basis[0, 0]
    rows, size = vector.shape
    prim = primal_index.shape[-1]
    coarse_count, share = coarse_inverse.shape
    half = rows // 2
    block = half // BLOCKS
    extra = 2 * prim
    width = -(-3 * prim // LANES) * LANES
    assert half == extra and prim <= coarse_count

    other_matrix = swap(matrix)
    spots = jnp.full((size,), -1.0, f32).at[:prim].set(primal_index[0, 0].astype(f32))
    own_aux = jnp.stack([diagonal[0, 0], spots])
    oth_aux = swap(own_aux)

    fixed = jnp.concatenate(
        [
            coarse_inverse.T,
            jnp.pad(schur_small[0], ((0, 0), (0, coarse_count - prim))),
            jnp.pad(coarse_map.astype(f32), ((0, 7), (0, coarse_count - prim))),
        ],
        axis=0,
    )
    fixed = gather(fixed).reshape(subs, share + prim + 8, coarse_count)
    inverse_rows = fixed[:, :share].reshape(coarse_count, coarse_count)
    schur = fixed[:, share : share + prim, :prim]
    maps = fixed[:, share + prim, :prim]
    order = jnp.arange(subs, dtype=jnp.int32) ^ sub
    columns = (order[:, None] * share + jnp.arange(share, dtype=jnp.int32)).reshape(-1).astype(f32)
    onehot = (maps[:, :, None] == jnp.arange(coarse_count, dtype=jnp.int32).astype(f32)).astype(f32)
    onehot_there = (maps[:, :, None] == columns).astype(f32)

    own, keep, send = call(
        split_own,
        [struct((2, size, size), bf16), struct((half + extra, size)), struct((half + extra, size))],
        [scal, matrix, vector, one, two, own_aux],
        2,
        scratch=[
            pltpu.VMEM((size, size), f32),
            pltpu.VMEM((rows + extra, size), f32),
            pltpu.VMEM((rows + extra, size), f32),
            pltpu.SemaphoreType.DMA((3 + PIECES,)),
        ],
        hbm=(1, 2, 3, 4),
    )
    recv = swap(send)
    (weights,) = call(split_other, [struct((2, 2, size, size), bf16)], [scal, other_matrix, own], 1)
    place = jnp.arange(size, dtype=jnp.int32).astype(f32)[None, :]
    own_spots = (own_aux[1, :prim, None] == place).astype(f32)
    oth_spots = (oth_aux[1, :prim, None] == place).astype(f32)

    def like(count, *heights):
        return [struct((h, size)) for h in heights for _ in range(count)]

    span = range(BLOCKS)
    f, carried = [], []
    for i in span:
        f.append(
            call(
                functools.partial(start_chain, i * block),
                like(2, block),
                [scal, keep, recv, weights],
                1,
            )
        )
        carried.append(rise(f[i][1]))
    y_first, y_second, z_sent = call(
        adjoint_start, like(3, prim), [scal, own_spots, oth_spots, weights], 2
    )
    z_carried = rise(z_sent)
    k_first, k_second, k_part = call(
        functools.partial(start_basis, half),
        like(2, extra) + like(1, prim),
        [scal, keep, recv, weights],
        1,
    )
    k_carried = rise(k_part)

    n = []
    for i in span:
        n.append(
            call(
                functools.partial(top_one, i * block),
                like(2, block),
                [scal, keep, recv, carried[i], weights],
                3,
            )
        )
        carried[i] = fall(n[i][0])
    y_first, y_second, z_first, z_second = call(
        adjoint_top,
        like(4, prim),
        [scal, own_spots, oth_spots, z_carried, weights, y_first, y_second],
        3,
        aliases={5: 0, 6: 1},
    )
    z_back = fall(z_first)
    (upper,) = call(
        score_top,
        [struct((half, width))],
        [scal, keep, recv, own_aux, oth_aux, y_first, y_second, z_first, z_second, *n[0], *n[1]],
        1,
    )
    upper = fall(upper)

    n_one, g = [], []
    for i in span:
        turned = call(
            turn,
            like(4, block),
            [scal, *f[i], carried[i], weights, own_aux, oth_aux, *n[i]],
            4,
            aliases={7: 0, 8: 1},
        )
        n_one.append(turned[:2])
        g.append(turned[2:])
        carried[i] = rise(g[i][1])
    pieces = []
    for i in span:
        pieces += [*f[i], *g[i]]
    (values,) = call(
        score_turn,
        [struct((half, width))],
        [scal, upper, z_back, y_first, y_second, k_first, k_second, *pieces],
        1,
    )
    values = gather(values).reshape(subs, half, width)

    n_two = []
    for i in span:
        n_two.append(
            call(
                top_two, like(2, block), [scal, *n_one[i], carried[i], weights, own_aux, oth_aux], 3
            )
        )
        carried[i] = fall(n_two[i][0])
    k_n = call(
        functools.partial(top_basis, half), like(2, prim), [scal, keep, recv, k_carried, weights], 3
    )
    k_carried = fall(k_n[0])
    for i in span:
        n_two[i] = call(
            back_two,
            like(2, block),
            [scal, *g[i], carried[i], weights, *n_two[i]],
            2,
            aliases={5: 0, 6: 1},
        )
    k_n = call(
        back_basis,
        like(2, prim),
        [scal, k_first, k_second, k_carried, weights, *k_n],
        2,
        aliases={5: 0, 6: 1},
    )
    pieces = []
    for i in span:
        pieces += [*n_one[i], *n_two[i]]
    m_keep, m_send, k_keep, k_send = call(settle, like(2, half, prim), [scal, *k_n, *pieces], 0.5)
    m_recv = swap(m_send)
    k_recv = swap(k_send)

    def times_high(form, left, right):
        return jnp.einsum(form, left, right, precision=highest, preferred_element_type=f32)

    p_one = values[:, :, :prim]
    p_defect = p_one - values[:, :, prim : 2 * prim]
    x_one = values[:, :prim, 2 * prim : 3 * prim]
    x_two = values[:, prim : 2 * prim, 2 * prim : 3 * prim]
    sol = times_high("rn,mn->rm", times_high("srp,spn->rn", p_one, onehot), inverse_rows)
    picked = times_high("rm,spm->srp", sol, onehot_there)
    multiplier = times_high("srp,spq->srq", p_one, schur)
    p_two = p_defect + times_high("srp,spq->srq", multiplier, x_one) - times_high(
        "srp,spq->srq", picked, x_two
    )
    sol = times_high("rn,mn->rm", times_high("srp,spn->rn", p_two, onehot), inverse_rows)
    q_one = jnp.concatenate([-multiplier[0], picked[0]], axis=1)
    q_two = jnp.concatenate(
        [
            -times_high("rp,pq->rq", p_two[0], schur[0]),
            times_high("rm,pm->rp", sol, onehot_there[0]),
        ],
        axis=1,
    )
    q = jnp.concatenate([q_one, q_one + q_two], axis=1)
    q_upper = rise(q)
    q = jnp.where(scal[1] == 0, q, q_upper)
    q_recv = swap(q)
    (out,) = call(
        finish,
        [struct((rows, size))],
        [scal, m_keep, m_recv, q, q_recv, k_keep, k_recv, one, two],
        0.5,
    )
    return out[None, None]


def solution(mesh):
    placed_as = (
        P("sub", "slab", None, None),
        P("sub", "slab", None, None),
        P("sub", "slab", None),
        P("sub", "slab", None),
        P("sub", None),
        P("sub", None, None),
        P("sub", "slab", None, None),
        P("sub", "slab", None, None),
        P(None, "sub"),
    )

    return jax.shard_map(
        on_device,
        mesh=mesh,
        in_specs=placed_as,
        out_specs=P("sub", "slab", None, None),
        check_vma=False,
    )
```

time: 380 us -> 106 us (0.28); the launches traced: 372 us -> 105 us
  waiting for transfers between devices: 189 us -> 13.5 us
  blocking collectives: 71.4 us -> 0 us
  matrix products: 47 us -> 3.22 us
  Pallas kernels: 0 us -> 35.6 us
  between operations: 14.3 us -> 0.63 us
  local copies, waits for them, and re-layouts: 1.59 us -> 8.38 us
  starting transfers between devices: 48.2 us -> 42 us
    psum x2 -> x0, waiting for transfers between devices: 139 us -> none  [apply_once(): coarse_rhs = lax.psum(product(primal, onehot), 'sub')]
    dot_general x26 -> x10, matrix products: 47 us -> 3.22 us  [times_high(): jnp.einsum(form, left, right, precision=highest, preferred_element_type=f32)]
    psum x2 -> x0, blocking collectives: 40.5 us -> none  [apply_once(): primal = lax.psum(partial_value, 'slab')]
    ppermute x12 -> x26, waiting for transfers between devices: 50.1 us -> 13.5 us  [the longest x6 9.5 us: gather(): other = lax.ppermute(x, 'sub', [(i, i ^ distance) for i in range(subs)])]
    pallas_call x0 -> x21, Pallas kernels: none -> 35.6 us  [call(): pl.pallas_call(body, out_shape=outs, in_specs=specs, out_specs=[spec(pltp...]
    all_gather x1 -> x0, blocking collectives: 30.9 us -> none  [on_device(): inverse_whole = lax.all_gather(coarse_inverse, 'sub', axis=1, tiled=True)]
    unnamed x20 -> x25, local copies, waits for them, and re-layouts: 0.06 us -> 7.92 us
    ppermute x12 -> x26, starting transfers between devices: 48.1 us -> 42 us  [the longest x7 19.1 us: rise(): return lax.ppermute(x, 'slab', [(0, 2), (1, 3)])]
  transfers between devices with their start and end apart: 14 -> 26, of which waited for: 13 -> 7; matrix products, arithmetic and copies ran while one was open for 0% -> 6% of each run, Pallas kernels for 0% -> 31%
where the time goes in v1:
time: 106 us; the launch traced here: 105 us
  starting transfers between devices  42 us (40%)
  Pallas kernels  35.6 us (34%)
  waiting for transfers between devices  13.5 us (13%)
  local copies, waits for them, and re-layouts  8.38 us (8%)
  matrix products  3.22 us (3%)
  other arithmetic  2 us (2%)
    pallas_call x21, Pallas kernels, call(): pl.pallas_call(body, out_shape=outs, in_specs=specs, out_specs=[spec(pltp...  35.6 us
    ppermute x7, starting transfers between devices, rise(): return lax.ppermute(x, 'slab', [(0, 2), (1, 3)])  19.1 us
    ppermute x6, starting transfers between devices, gather(): other = lax.ppermute(x, 'sub', [(i, i ^ distance) for i in range(subs)])  12.1 us
    ppermute x6, waiting for transfers between devices, gather(): other = lax.ppermute(x, 'sub', [(i, i ^ distance) for i in range(subs)])  9.5 us
    ppermute x7, starting transfers between devices, fall(): return lax.ppermute(x, 'slab', [(2, 0), (3, 1)])  9.04 us
    unnamed x25, local copies, waits for them, and re-layouts  7.92 us
    dot_general x10, matrix products, times_high(): jnp.einsum(form, left, right, precision=highest, preferred_element_type=f32)  3.22 us
    ppermute x7, waiting for transfers between devices, fall(): return lax.ppermute(x, 'slab', [(2, 0), (3, 1)])  2.8 us
  transfers between devices with their start and end apart: 26, of which 7 were waited for; matrix products, arithmetic and copies ran while one was open for 6% of the time, Pallas kernels for 31%

profile of v1, /device:TPU:0, one launch (start us, length us, event | category | flops | bytes accessed | tf_op | source)
XLA Modules:
  0.0 105.3 jit_solution(16403741951416092277)
XLA Ops:
  0.6 0.7 convert_bitcast_fusion
  1.2 0.7 fusion.11.aux.own_aux
  2.0 3.9 %shard_map.91 = (bf16[2,1024,1024]{2,1,0:T(8,128)(2,1)S(1)}, f32[128,1024]{1,0:T(8,128)S(1)}, f32[128,1024]{1,0:T(8,128)S(1)}) custom-call(s32[2]{0:T(128)S(1)} %pad_add_fusion.scal, f32[1024,1024]{1,0:T(8,128)} %bitcast.76, f32[128,1024]{1,0:T(8,128)} %bitcast.77, f32[32,1024]{1,0:T(8,128)} %bitcast.51, f32[32,1024]{1,0:T(8,128)} %bitcast.53, ...), custom_call_target="tpu_custom_call" | custom-call | flops 1600000000 | tf_op jit(solution)/shard_map/pallas_call | solution.py:57
  5.9 2.0 %copy-done.2 = bf16[2,1024,1024]{2,1,0:T(8,128)(2,1)} copy-done((bf16[2,1024,1024]{2,1,0:T(8,128)(2,1)}, bf16[2,1024,1024]{2,1,0:T(8,128)(2,1)S(1)}, u32[]{:S(2)}) %copy-start.2) | copy-done | bytes 4194328
  8.5 2.6 %collective-permute-start.20 = (f32[56,128]{1,0:T(8,128)S(1)}, f32[56,128]{1,0:T(8,128)S(1)}, u32[]{:S(2)}, u32[]{:S(2)}) collective-permute-start(f32[56,128]{1,0:T(8,128)S(1)} %pad_maximum_fusion.5), channel_id=1, source_target_pairs={{0,4},{4,0},{8,12},{12,8},{16,20},{20,16},{24,28},{28,24},{1,5},{5... | collective-permute-start | bytes 86024 | tf_op jit(solution)/shard_map/ppermute | solution.py:373
  11.2 1.8 %collective-permute-done.20 = f32[56,128]{1,0:T(8,128)S(1)} collective-permute-done((f32[56,128]{1,0:T(8,128)S(1)}, f32[56,128]{1,0:T(8,128)S(1)}, u32[]{:S(2)}, u32[]{:S(2)}) %collective-permute-start.20) | collective-permute-done | bytes 28704 | tf_op jit(solution)/shard_map/ppermute | solution.py:373
  13.0 2.0 %collective-permute-start.21 = (f32[112,128]{1,0:T(8,128)S(1)}, f32[112,128]{1,0:T(8,128)S(1)}, u32[]{:S(2)}, u32[]{:S(2)}) collective-permute-start(f32[112,128]{1,0:T(8,128)S(1)} %pad_maximum_fusion.3), channel_id=1, source_target_pairs={{0,8},{4,12},{8,0},{12,4},{16,24},{20,28},{24,16},{28,20},{1,9},{5... | collective-permute-start | bytes 172040 | tf_op jit(solution)/shard_map/ppermute | solution.py:373
  15.0 2.2 %collective-permute-done.21 = f32[112,128]{1,0:T(8,128)S(1)} collective-permute-done((f32[112,128]{1,0:T(8,128)S(1)}, f32[112,128]{1,0:T(8,128)S(1)}, u32[]{:S(2)}, u32[]{:S(2)}) %collective-permute-start.21) | collective-permute-done | bytes 57376 | tf_op jit(solution)/shard_map/ppermute | solution.py:373
  17.2 3.1 %collective-permute-start.22 = (f32[224,128]{1,0:T(8,128)S(1)}, f32[224,128]{1,0:T(8,128)S(1)}, u32[]{:S(2)}, u32[]{:S(2)}) collective-permute-start(f32[224,128]{1,0:T(8,128)S(1)} %get-tuple-element.109), channel_id=1, source_target_pairs={{0,16},{4,20},{8,24},{12,28},{16,0},{20,4},{24,8},{28,12},{1,17},{... | collective-permute-start | bytes 344072 | tf_op jit(solution)/shard_map/ppermute | solution.py:373
  20.4 2.8 %collective-permute-done.22 = f32[224,128]{1,0:T(8,128)S(1)} collective-permute-done((f32[224,128]{1,0:T(8,128)S(1)}, f32[224,128]{1,0:T(8,128)S(1)}, u32[]{:S(2)}, u32[]{:S(2)}) %collective-permute-start.22) | collective-permute-done | bytes 114720 | tf_op jit(solution)/shard_map/ppermute | solution.py:373
  23.2 2.2 %copy-done.3 = bf16[2,1024,1024]{2,1,0:T(8,128)(2,1)S(1)} copy-done((bf16[2,1024,1024]{2,1,0:T(8,128)(2,1)S(1)}, bf16[2,1024,1024]{2,1,0:T(8,128)(2,1)}, u32[]{:S(2)}) %copy-start.3) | copy-done | bytes 4194328
  25.4 3.2 %shard_map.92.weights = bf16[2,2,1024,1024]{3,2,1,0:T(8,128)(2,1)S(1)} custom-call(s32[2]{0:T(128)S(1)} %pad_add_fusion.scal, f32[1024,1024]{1,0:T(8,128)} %collective-permute-done.1.matrix, bf16[2,1024,1024]{2,1,0:T(8,128)(2,1)S(1)} %copy-done.3), custom_call_target="tpu_custom_call" | custom-call | flops 800000000 | tf_op jit(solution)/shard_map/pallas_call | solution.py:57
  28.6 1.4 %shard_map.101 = (f32[32,1024]{1,0:T(8,128)S(1)}, f32[32,1024]{1,0:T(8,128)S(1)}) custom-call(s32[2]{0:T(128)S(1)} %pad_add_fusion.scal, f32[128,1024]{1,0:T(8,128)S(1)} %get-tuple-element.62.keep, f32[128,1024]{1,0:T(8,128)S(1)} %collective-permute-done.recv, bf16[2,2,1024,1024]{3,2,1,0:T(8,128)(2,1)S(1)} %shard_map.92.weights), custom_call_target="tpu_custom_call" | custom-call | flops 800000000 | tf_op jit(solution)/shard_map/pallas_call | solution.py:57
  30.0 4.1 %collective-permute-start.9 = (f32[32,1024]{1,0:T(8,128)S(1)}, f32[32,1024]{1,0:T(8,128)S(1)}, u32[]{:S(2)}, u32[]{:S(2)}) collective-permute-start(f32[32,1024]{1,0:T(8,128)S(1)} %get-tuple-element.85.f_second.refs_5_), channel_id=1, source_target_pairs={{0,2},{1,3},{4,6},{5,7},{8,10},{9,11},{12,14},{13,15},{16,18},{17,... | collective-permute-start | bytes 393224 | tf_op jit(solution)/shard_map/ppermute | solution.py:365
  34.0 1.4 %shard_map.96 = (f32[32,1024]{1,0:T(8,128)S(1)}, f32[32,1024]{1,0:T(8,128)S(1)}) custom-call(s32[2]{0:T(128)S(1)} %pad_add_fusion.scal, f32[128,1024]{1,0:T(8,128)S(1)} %get-tuple-element.62.keep, f32[128,1024]{1,0:T(8,128)S(1)} %collective-permute-done.recv, bf16[2,2,1024,1024]{3,2,1,0:T(8,128)(2,1)S(1)} %shard_map.92.weights), custom_call_target="tpu_custom_call" | custom-call | flops 800000000 | tf_op jit(solution)/shard_map/pallas_call | solution.py:57
  35.4 1.3 %collective-permute-start.4 = (f32[32,1024]{1,0:T(8,128)S(1)}, f32[32,1024]{1,0:T(8,128)S(1)}, u32[]{:S(2)}, u32[]{:S(2)}) collective-permute-start(f32[32,1024]{1,0:T(8,128)S(1)} %get-tuple-element.73.f_second.refs_1_), channel_id=1, source_target_pairs={{0,2},{1,3},{4,6},{5,7},{8,10},{9,11},{12,14},{13,15},{16,18},{17,... | collective-permute-start | bytes 393224 | tf_op jit(solution)/shard_map/ppermute | solution.py:365
  36.7 3.1 %shard_map.107 = (f32[32,1024]{1,0:T(8,128)S(1)}, f32[32,1024]{1,0:T(8,128)S(1)}, f32[32,1024]{1,0:T(8,128)S(1)}) custom-call(s32[2]{0:T(128)S(1)} %pad_add_fusion.scal, f32[32,1024]{1,0:T(8,128)S(1)} %get-tuple-element.119.own_spots, f32[32,1024]{1,0:T(8,128)S(1)} %get-tuple-element.118.oth_spots, bf16[2,2,1024,1024]{3,2,1,0:T(8,128)(2,1)S(1)} %shard_map.92.weights), custom_call_target="tpu_custom_call" | custom-call | flops 1600000000 | tf_op jit(solution)/shard_map/pallas_call | solution.py:57
  39.8 1.3 %collective-permute-start.14 = (f32[32,1024]{1,0:T(8,128)S(1)}, f32[32,1024]{1,0:T(8,128)S(1)}, u32[]{:S(2)}, u32[]{:S(2)}) collective-permute-start(f32[32,1024]{1,0:T(8,128)S(1)} %get-tuple-element.98), channel_id=1, source_target_pairs={{0,2},{1,3},{4,6},{5,7},{8,10},{9,11},{12,14},{13,15},{16,18},{17,... | collective-permute-start | bytes 393224 | tf_op jit(solution)/shard_map/ppermute | solution.py:365
  41.1 1.3 %shard_map.93 = (f32[64,1024]{1,0:T(8,128)S(1)}, f32[64,1024]{1,0:T(8,128)S(1)}, f32[32,1024]{1,0:T(8,128)S(1)}) custom-call(s32[2]{0:T(128)S(1)} %pad_add_fusion.scal, f32[128,1024]{1,0:T(8,128)S(1)} %get-tuple-element.62.keep, f32[128,1024]{1,0:T(8,128)S(1)} %collective-permute-done.recv, bf16[2,2,1024,1024]{3,2,1,0:T(8,128)(2,1)S(1)} %shard_map.92.weights), custom_call_target="tpu_custom_call" | custom-call | flops 800000000 | tf_op jit(solution)/shard_map/pallas_call | solution.py:57
  42.5 1.3 %collective-permute-start.2 = (f32[32,1024]{1,0:T(8,128)S(1)}, f32[32,1024]{1,0:T(8,128)S(1)}, u32[]{:S(2)}, u32[]{:S(2)}) collective-permute-start(f32[32,1024]{1,0:T(8,128)S(1)} %get-tuple-element.67), channel_id=1, source_target_pairs={{0,2},{1,3},{4,6},{5,7},{8,10},{9,11},{12,14},{13,15},{16,18},{17,... | collective-permute-start | bytes 393224 | tf_op jit(solution)/shard_map/ppermute | solution.py:365
  44.3 1.3 %collective-permute-start.10 = (f32[32,1024]{1,0:T(8,128)S(1)}, f32[32,1024]{1,0:T(8,128)S(1)}, u32[]{:S(2)}, u32[]{:S(2)}) collective-permute-start(f32[32,1024]{1,0:T(8,128)S(1)} %get-tuple-element.86.refs_0_.refs_2_), channel_id=1, source_target_pairs={{2,0},{3,1},{6,4},{7,5},{10,8},{11,9},{14,12},{15,13},{18,16},{19,... | collective-permute-start | bytes 393224 | tf_op jit(solution)/shard_map/ppermute | solution.py:368
  46.2 1.3 %collective-permute-start.5 = (f32[32,1024]{1,0:T(8,128)S(1)}, f32[32,1024]{1,0:T(8,128)S(1)}, u32[]{:S(2)}, u32[]{:S(2)}) collective-permute-start(f32[32,1024]{1,0:T(8,128)S(1)} %get-tuple-element.74.refs_0_), channel_id=1, source_target_pairs={{2,0},{3,1},{6,4},{7,5},{10,8},{11,9},{14,12},{15,13},{18,16},{19,... | collective-permute-start | bytes 393224 | tf_op jit(solution)/shard_map/ppermute | solution.py:368
  47.5 0.8 shard_map.108
  48.3 1.3 %collective-permute-start.16 = (f32[32,1024]{1,0:T(8,128)S(1)}, f32[32,1024]{1,0:T(8,128)S(1)}, u32[]{:S(2)}, u32[]{:S(2)}) collective-permute-start(f32[32,1024]{1,0:T(8,128)S(1)} %get-tuple-element.103.z_first), channel_id=1, source_target_pairs={{2,0},{3,1},{6,4},{7,5},{10,8},{11,9},{14,12},{15,13},{18,16},{19,... | collective-permute-start | bytes 393224 | tf_op jit(solution)/shard_map/ppermute | solution.py:368
  50.2 1.3 %collective-permute-start.15 = (f32[64,128]{1,0:T(8,128)S(1)}, f32[64,128]{1,0:T(8,128)S(1)}, u32[]{:S(2)}, u32[]{:S(2)}) collective-permute-start(f32[64,128]{1,0:T(8,128)S(1)} %shard_map.109), channel_id=1, source_target_pairs={{2,0},{3,1},{6,4},{7,5},{10,8},{11,9},{14,12},{15,13},{18,16},{19,... | collective-permute-start | bytes 98312 | tf_op jit(solution)/shard_map/ppermute | solution.py:368
  52.0 1.3 %collective-permute-start.3 = (f32[32,1024]{1,0:T(8,128)S(1)}, f32[32,1024]{1,0:T(8,128)S(1)}, u32[]{:S(2)}, u32[]{:S(2)}) collective-permute-start(f32[32,1024]{1,0:T(8,128)S(1)} %get-tuple-element.68.refs_0_), channel_id=1, source_target_pairs={{2,0},{3,1},{6,4},{7,5},{10,8},{11,9},{14,12},{15,13},{18,16},{19,... | collective-permute-start | bytes 393224 | tf_op jit(solution)/shard_map/ppermute | solution.py:368
  53.3 3.6 %shard_map.103 = (f32[32,1024]{1,0:T(8,128)S(1)}, f32[32,1024]{1,0:T(8,128)S(1)}, f32[32,1024]{1,0:T(8,128)S(1)}, f32[32,1024]{1,0:T(8,128)S(1)}) custom-call(s32[2]{0:T(128)S(1)} %pad_add_fusion.scal, f32[32,1024]{1,0:T(8,128)S(1)} %get-tuple-element.84.f_first.refs_4_, ...), custom_call_target="tpu_custom_call", output_to_operand_aliasing={{0}: (7, {}), {1}: (8, {})} | custom-call | flops 3200000000 | tf_op jit(solution)/shard_map/pallas_call | solution.py:57
  56.9 3.6 %shard_map.98 = (f32[32,1024]{1,0:T(8,128)S(1)}, f32[32,1024]{1,0:T(8,128)S(1)}, f32[32,1024]{1,0:T(8,128)S(1)}, f32[32,1024]{1,0:T(8,128)S(1)}) custom-call(s32[2]{0:T(128)S(1)} %pad_add_fusion.scal, f32[32,1024]{1,0:T(8,128)S(1)} %get-tuple-element.72.f_first.refs_0_, ...), custom_call_target="tpu_custom_call", output_to_operand_aliasing={{0}: (7, {}), {1}: (8, {})} | custom-call | flops 3200000000 | tf_op jit(solution)/shard_map/pallas_call | solution.py:57
  60.5 2.8 %collective-permute-done.15.above = f32[64,128]{1,0:T(8,128)S(1)} collective-permute-done((f32[64,128]{1,0:T(8,128)S(1)}, f32[64,128]{1,0:T(8,128)S(1)}, u32[]{:S(2)}, u32[]{:S(2)}) %collective-permute-start.15) | collective-permute-done | bytes 32800 | tf_op jit(solution)/shard_map/ppermute | solution.py:368
  63.3 1.3 %shard_map.110 = f32[64,128]{1,0:T(8,128)S(1)} custom-call(s32[2]{0:T(128)S(1)} %pad_add_fusion.scal, f32[64,128]{1,0:T(8,128)S(1)} %collective-permute-done.15.above, f32[32,1024]{1,0:T(8,128)S(1)} %collective-permute-done.16.carried, f32[32,1024]{1,0:T(8,128)S(1)} %get-tuple-element.101.y_first, f32[32,1024]{1,0:T(8,128)S(1)} %get-tuple-element.102.y_second, ...), custom_call_target="tpu_custom_call" | custom-call | flops 800000000 | tf_op jit(solution)/shard_map/pallas_call | solution.py:57
  64.6 1.5 %collective-permute-start.17 = (f32[64,128]{1,0:T(8,128)S(1)}, f32[64,128]{1,0:T(8,128)S(1)}, u32[]{:S(2)}, u32[]{:S(2)}) collective-permute-start(f32[64,128]{1,0:T(8,128)S(1)} %shard_map.110), channel_id=1, source_target_pairs={{0,4},{4,0},{8,12},{12,8},{16,20},{20,16},{24,28},{28,24},{1,5},{5... | collective-permute-start | bytes 98312 | tf_op jit(solution)/shard_map/ppermute | solution.py:373
  66.3 4.3 %collective-permute-start.11 = (f32[32,1024]{1,0:T(8,128)S(1)}, f32[32,1024]{1,0:T(8,128)S(1)}, u32[]{:S(2)}, u32[]{:S(2)}) collective-permute-start(f32[32,1024]{1,0:T(8,128)S(1)} %get-tuple-element.91.f_second.refs_7_), channel_id=1, source_target_pairs={{0,2},{1,3},{4,6},{5,7},{8,10},{9,11},{12,14},{13,15},{16,18},{17,... | collective-permute-start | bytes 393224 | tf_op jit(solution)/shard_map/ppermute | solution.py:365
  70.6 1.3 %collective-permute-start.7 = (f32[32,1024]{1,0:T(8,128)S(1)}, f32[32,1024]{1,0:T(8,128)S(1)}, u32[]{:S(2)}, u32[]{:S(2)}) collective-permute-start(f32[32,1024]{1,0:T(8,128)S(1)} %get-tuple-element.79.f_second.refs_3_), channel_id=1, source_target_pairs={{0,2},{1,3},{4,6},{5,7},{8,10},{9,11},{12,14},{13,15},{16,18},{17,... | collective-permute-start | bytes 393224 | tf_op jit(solution)/shard_map/ppermute | solution.py:365
  71.9 0.7 collective-permute-start.18
  72.6 2.1 %shard_map.95 = (f32[32,1024]{1,0:T(8,128)S(1)}, f32[32,1024]{1,0:T(8,128)S(1)}) custom-call(s32[2]{0:T(128)S(1)} %pad_add_fusion.scal, f32[64,1024]{1,0:T(8,128)S(1)} %get-tuple-element.65.f_first.k_first, f32[64,1024]{1,0:T(8,128)S(1)} %get-tuple-element.66.f_second.k_second, ...), custom_call_target="tpu_custom_call", output_to_operand_aliasing={{0}: (5, {}), {1}: (6, {})} | custom-call | flops 1600000000 | tf_op jit(solution)/shard_map/pallas_call | solution.py:57
  74.7 1.5 %collective-permute-done.18 = f32[128,128]{1,0:T(8,128)S(1)} collective-permute-done((f32[128,128]{1,0:T(8,128)S(1)}, f32[128,128]{1,0:T(8,128)S(1)}, u32[]{:S(2)}, u32[]{:S(2)}) %collective-permute-start.18) | collective-permute-done | bytes 65568 | tf_op jit(solution)/shard_map/ppermute | solution.py:373
  76.3 2.1 %collective-permute-start.19 = (f32[256,128]{1,0:T(8,128)S(1)}, f32[256,128]{1,0:T(8,128)S(1)}, u32[]{:S(2)}, u32[]{:S(2)}) collective-permute-start(f32[256,128]{1,0:T(8,128)S(1)} %pad_maximum_fusion.1), channel_id=1, source_target_pairs={{0,16},{4,20},{8,24},{12,28},{16,0},{20,4},{24,8},{28,12},{1,17},{... | collective-permute-start | bytes 393224 | tf_op jit(solution)/shard_map/ppermute | solution.py:373
  78.4 0.8 shard_map.104
  79.1 1.3 %collective-permute-start.12 = (f32[32,1024]{1,0:T(8,128)S(1)}, f32[32,1024]{1,0:T(8,128)S(1)}, u32[]{:S(2)}, u32[]{:S(2)}) collective-permute-start(f32[32,1024]{1,0:T(8,128)S(1)} %get-tuple-element.92.refs_0_), channel_id=1, source_target_pairs={{2,0},{3,1},{6,4},{7,5},{10,8},{11,9},{14,12},{15,13},{18,16},{19,... | collective-permute-start | bytes 393224 | tf_op jit(solution)/shard_map/ppermute | solution.py:368
  81.0 1.3 %collective-permute-start.8 = (f32[32,1024]{1,0:T(8,128)S(1)}, f32[32,1024]{1,0:T(8,128)S(1)}, u32[]{:S(2)}, u32[]{:S(2)}) collective-permute-start(f32[32,1024]{1,0:T(8,128)S(1)} %get-tuple-element.80.refs_0_), channel_id=1, source_target_pairs={{2,0},{3,1},{6,4},{7,5},{10,8},{11,9},{14,12},{15,13},{18,16},{19,... | collective-permute-start | bytes 393224 | tf_op jit(solution)/shard_map/ppermute | solution.py:368
  82.3 1.3 %collective-permute-done.19 = f32[256,128]{1,0:T(8,128)S(1)} collective-permute-done((f32[256,128]{1,0:T(8,128)S(1)}, f32[256,128]{1,0:T(8,128)S(1)}, u32[]{:S(2)}, u32[]{:S(2)}) %collective-permute-start.19) | collective-permute-done | bytes 131104 | tf_op jit(solution)/shard_map/ppermute | solution.py:373
  87.8 5.6 %collective-permute-start.23 = (f32[64,128]{1,0:T(8,128)S(1)}, f32[64,128]{1,0:T(8,128)S(1)}, u32[]{:S(2)}, u32[]{:S(2)}) collective-permute-start(f32[64,128]{1,0:T(8,128)S(1)} %pad_maximum_fusion.4), channel_id=1, source_target_pairs={{0,2},{1,3},{4,6},{5,7},{8,10},{9,11},{12,14},{13,15},{16,18},{17,... | collective-permute-start | bytes 98312 | tf_op jit(solution)/shard_map/ppermute | solution.py:365
  93.4 3.4 %copy-done.1 = bf16[2,2,1024,1024]{3,2,1,0:T(8,128)(2,1)S(1)} copy-done((bf16[2,2,1024,1024]{3,2,1,0:T(8,128)(2,1)S(1)}, bf16[2,2,1024,1024]{3,2,1,0:T(8,128)(2,1)}, u32[]{:S(2)}) %copy-start.1) | copy-done | bytes 8388632
  96.8 2.1 %shard_map.105 = (f32[32,1024]{1,0:T(8,128)S(1)}, f32[32,1024]{1,0:T(8,128)S(1)}) custom-call(s32[2]{0:T(128)S(1)} %pad_add_fusion.scal, f32[32,1024]{1,0:T(8,128)S(1)} %get-tuple-element.90.f_first.refs_6_, f32[32,1024]{1,0:T(8,128)S(1)} %get-tuple-element.91.f_second.refs_7_, ...), custom_call_target="tpu_custom_call", output_to_operand_aliasing={{0}: (5, {}), {1}: (6, {})} | custom-call | flops 1600000000 | tf_op jit(solution)/shard_map/pallas_call | solution.py:57
  98.9 2.1 %shard_map.100 = (f32[32,1024]{1,0:T(8,128)S(1)}, f32[32,1024]{1,0:T(8,128)S(1)}) custom-call(s32[2]{0:T(128)S(1)} %pad_add_fusion.scal, f32[32,1024]{1,0:T(8,128)S(1)} %get-tuple-element.78.f_first.refs_2_, f32[32,1024]{1,0:T(8,128)S(1)} %get-tuple-element.79.f_second.refs_3_, ...), custom_call_target="tpu_custom_call", output_to_operand_aliasing={{0}: (5, {}), {1}: (6, {})} | custom-call | flops 1600000000 | tf_op jit(solution)/shard_map/pallas_call | solution.py:57
  101.0 0.6 shard_map.106
  102.5 1.1 %collective-permute-done.24.q_recv = f32[64,128]{1,0:T(8,128)S(1)} collective-permute-done((f32[64,128]{1,0:T(8,128)S(1)}, f32[64,128]{1,0:T(8,128)S(1)}, u32[]{:S(2)}, u32[]{:S(2)}) %collective-permute-start.24) | collective-permute-done | bytes 32800 | tf_op jit(solution)/shard_map/ppermute | solution.py:362
  103.6 1.7 %shard_map.111 = f32[128,1024]{1,0:T(8,128)} custom-call(s32[2]{0:T(128)S(1)} %pad_add_fusion.scal, f32[64,1024]{1,0:T(8,128)S(1)} %get-tuple-element.96.keep, f32[64,1024]{1,0:T(8,128)S(1)} %collective-permute-done.13.recv, f32[64,128]{1,0:T(8,128)S(1)} %broadcast_select_fusion.q_keep, f32[64,128]{1,0:T(8,128)S(1)} %collective-permute-done.24.q_recv, ...), custom_call_target="tpu_custom_call" | custom-call | flops 400000000 | tf_op jit(solution)/shard_map/pallas_call | solution.py:57
  (89 shorter events, 9.3 us)
Async XLA Ops:
  0.0 8.4 %copy-start.8 = (s32[1,32]{1,0:T(1,128)S(1)}, s32[1,32]{1,0:T(1,128)}, u32[]{:S(2)}) copy-start(s32[1,32]{1,0:T(1,128)} %param.15) | copy-start | bytes 388
  0.0 8.4 %copy-start.6 = (f32[128,16]{0,1:T(8,128)S(1)}, f32[128,16]{0,1:T(8,128)}, u32[]{:S(2)}) copy-start(f32[128,16]{0,1:T(8,128)} %param.19) | copy-start | bytes 24580
  0.0 8.4 %copy-start.7 = (f32[1,32,32]{2,1,0:T(8,128)S(1)}, f32[1,32,32]{2,1,0:T(8,128)}, u32[]{:S(2)}) copy-start(f32[1,32,32]{2,1,0:T(8,128)} %param.16) | copy-start | bytes 12292
  0.0 23.2 %collective-permute-start.1 = (f32[1024,1024]{1,0:T(8,128)}, f32[1024,1024]{1,0:T(8,128)}, u32[]{:S(2)}, u32[]{:S(2)}) collective-permute-start(f32[1024,1024]{1,0:T(8,128)} %bitcast.75), channel_id=1, source_target_pairs={{0,1},{1,0},{2,3},{3,2},{4,5},{5,4},{6,7},{7,6},{8,9},{9,8},{10,11... | collective-permute-start | bytes 12582920 | tf_op jit(solution)/shard_map/ppermute | solution.py:362
  1.9 9.3 %collective-permute-start.6 = (f32[2,1024]{1,0:T(2,128)S(1)}, f32[2,1024]{1,0:T(2,128)S(1)}, u32[]{:S(2)}, u32[]{:S(2)}) collective-permute-start(f32[2,1024]{1,0:T(2,128)S(1)} %fusion.11.aux.own_aux), channel_id=1, source_target_pairs={{0,1},{1,0},{2,3},{3,2},{4,5},{5,4},{6,7},{7,6},{8,9},{9,8},{10,11... | collective-permute-start | bytes 24584 | tf_op jit(solution)/shard_map/ppermute | solution.py:362
  5.9 2.0 %copy-start.2 = (bf16[2,1024,1024]{2,1,0:T(8,128)(2,1)}, bf16[2,1024,1024]{2,1,0:T(8,128)(2,1)S(1)}, u32[]{:S(2)}) copy-start(bf16[2,1024,1024]{2,1,0:T(8,128)(2,1)S(1)} %get-tuple-element.64.own) | copy-start | bytes 12582916
  7.9 20.7 %collective-permute-start = (f32[128,1024]{1,0:T(8,128)S(1)}, f32[128,1024]{1,0:T(8,128)S(1)}, u32[]{:S(2)}, u32[]{:S(2)}) collective-permute-start(f32[128,1024]{1,0:T(8,128)S(1)} %get-tuple-element.63), channel_id=1, source_target_pairs={{0,1},{1,0},{2,3},{3,2},{4,5},{5,4},{6,7},{7,6},{8,9},{9,8},{10,11... | collective-permute-start | bytes 1572872 | tf_op jit(solution)/shard_map/ppermute | solution.py:362
  8.5 4.5 %collective-permute-start.20 = (f32[56,128]{1,0:T(8,128)S(1)}, f32[56,128]{1,0:T(8,128)S(1)}, u32[]{:S(2)}, u32[]{:S(2)}) collective-permute-start(f32[56,128]{1,0:T(8,128)S(1)} %pad_maximum_fusion.5), channel_id=1, source_target_pairs={{0,4},{4,0},{8,12},{12,8},{16,20},{20,16},{24,28},{28,24},{1,5},{5... | collective-permute-start | bytes 86024 | tf_op jit(solution)/shard_map/ppermute | solution.py:373
  13.0 4.2 %collective-permute-start.21 = (f32[112,128]{1,0:T(8,128)S(1)}, f32[112,128]{1,0:T(8,128)S(1)}, u32[]{:S(2)}, u32[]{:S(2)}) collective-permute-start(f32[112,128]{1,0:T(8,128)S(1)} %pad_maximum_fusion.3), channel_id=1, source_target_pairs={{0,8},{4,12},{8,0},{12,4},{16,24},{20,28},{24,16},{28,20},{1,9},{5... | collective-permute-start | bytes 172040 | tf_op jit(solution)/shard_map/ppermute | solution.py:373
  17.2 6.0 %collective-permute-start.22 = (f32[224,128]{1,0:T(8,128)S(1)}, f32[224,128]{1,0:T(8,128)S(1)}, u32[]{:S(2)}, u32[]{:S(2)}) collective-permute-start(f32[224,128]{1,0:T(8,128)S(1)} %get-tuple-element.109), channel_id=1, source_target_pairs={{0,16},{4,20},{8,24},{12,28},{16,0},{20,4},{24,8},{28,12},{1,17},{... | collective-permute-start | bytes 344072 | tf_op jit(solution)/shard_map/ppermute | solution.py:373
  23.2 2.2 %copy-start.3 = (bf16[2,1024,1024]{2,1,0:T(8,128)(2,1)S(1)}, bf16[2,1024,1024]{2,1,0:T(8,128)(2,1)}, u32[]{:S(2)}) copy-start(bf16[2,1024,1024]{2,1,0:T(8,128)(2,1)} %copy-done.2) | copy-start | bytes 12582916
  28.6 51.9 %copy-start = (bf16[2,2,1024,1024]{3,2,1,0:T(8,128)(2,1)}, bf16[2,2,1024,1024]{3,2,1,0:T(8,128)(2,1)S(1)}, u32[]{:S(2)}) copy-start(bf16[2,2,1024,1024]{3,2,1,0:T(8,128)(2,1)S(1)} %shard_map.92.weights) | copy-start | bytes 25165828
  30.0 13.8 %collective-permute-start.9 = (f32[32,1024]{1,0:T(8,128)S(1)}, f32[32,1024]{1,0:T(8,128)S(1)}, u32[]{:S(2)}, u32[]{:S(2)}) collective-permute-start(f32[32,1024]{1,0:T(8,128)S(1)} %get-tuple-element.85.f_second.refs_5_), channel_id=1, source_target_pairs={{0,2},{1,3},{4,6},{5,7},{8,10},{9,11},{12,14},{13,15},{16,18},{17,... | collective-permute-start | bytes 393224 | tf_op jit(solution)/shard_map/ppermute | solution.py:365
  35.4 10.3 %collective-permute-start.4 = (f32[32,1024]{1,0:T(8,128)S(1)}, f32[32,1024]{1,0:T(8,128)S(1)}, u32[]{:S(2)}, u32[]{:S(2)}) collective-permute-start(f32[32,1024]{1,0:T(8,128)S(1)} %get-tuple-element.73.f_second.refs_1_), channel_id=1, source_target_pairs={{0,2},{1,3},{4,6},{5,7},{8,10},{9,11},{12,14},{13,15},{16,18},{17,... | collective-permute-start | bytes 393224 | tf_op jit(solution)/shard_map/ppermute | solution.py:365
  39.8 7.7 %collective-permute-start.14 = (f32[32,1024]{1,0:T(8,128)S(1)}, f32[32,1024]{1,0:T(8,128)S(1)}, u32[]{:S(2)}, u32[]{:S(2)}) collective-permute-start(f32[32,1024]{1,0:T(8,128)S(1)} %get-tuple-element.98), channel_id=1, source_target_pairs={{0,2},{1,3},{4,6},{5,7},{8,10},{9,11},{12,14},{13,15},{16,18},{17,... | collective-permute-start | bytes 393224 | tf_op jit(solution)/shard_map/ppermute | solution.py:365
  42.5 9.0 %collective-permute-start.2 = (f32[32,1024]{1,0:T(8,128)S(1)}, f32[32,1024]{1,0:T(8,128)S(1)}, u32[]{:S(2)}, u32[]{:S(2)}) collective-permute-start(f32[32,1024]{1,0:T(8,128)S(1)} %get-tuple-element.67), channel_id=1, source_target_pairs={{0,2},{1,3},{4,6},{5,7},{8,10},{9,11},{12,14},{13,15},{16,18},{17,... | collective-permute-start | bytes 393224 | tf_op jit(solution)/shard_map/ppermute | solution.py:365
  44.3 9.0 %collective-permute-start.10 = (f32[32,1024]{1,0:T(8,128)S(1)}, f32[32,1024]{1,0:T(8,128)S(1)}, u32[]{:S(2)}, u32[]{:S(2)}) collective-permute-start(f32[32,1024]{1,0:T(8,128)S(1)} %get-tuple-element.86.refs_0_.refs_2_), channel_id=1, source_target_pairs={{2,0},{3,1},{6,4},{7,5},{10,8},{11,9},{14,12},{15,13},{18,16},{19,... | collective-permute-start | bytes 393224 | tf_op jit(solution)/shard_map/ppermute | solution.py:368
  46.2 10.7 %collective-permute-start.5 = (f32[32,1024]{1,0:T(8,128)S(1)}, f32[32,1024]{1,0:T(8,128)S(1)}, u32[]{:S(2)}, u32[]{:S(2)}) collective-permute-start(f32[32,1024]{1,0:T(8,128)S(1)} %get-tuple-element.74.refs_0_), channel_id=1, source_target_pairs={{2,0},{3,1},{6,4},{7,5},{10,8},{11,9},{14,12},{15,13},{18,16},{19,... | collective-permute-start | bytes 393224 | tf_op jit(solution)/shard_map/ppermute | solution.py:368
  48.3 15.0 %collective-permute-start.16 = (f32[32,1024]{1,0:T(8,128)S(1)}, f32[32,1024]{1,0:T(8,128)S(1)}, u32[]{:S(2)}, u32[]{:S(2)}) collective-permute-start(f32[32,1024]{1,0:T(8,128)S(1)} %get-tuple-element.103.z_first), channel_id=1, source_target_pairs={{2,0},{3,1},{6,4},{7,5},{10,8},{11,9},{14,12},{15,13},{18,16},{19,... | collective-permute-start | bytes 393224 | tf_op jit(solution)/shard_map/ppermute | solution.py:368
  50.2 13.1 %collective-permute-start.15 = (f32[64,128]{1,0:T(8,128)S(1)}, f32[64,128]{1,0:T(8,128)S(1)}, u32[]{:S(2)}, u32[]{:S(2)}) collective-permute-start(f32[64,128]{1,0:T(8,128)S(1)} %shard_map.109), channel_id=1, source_target_pairs={{2,0},{3,1},{6,4},{7,5},{10,8},{11,9},{14,12},{15,13},{18,16},{19,... | collective-permute-start | bytes 98312 | tf_op jit(solution)/shard_map/ppermute | solution.py:368
  52.0 20.6 %collective-permute-start.3 = (f32[32,1024]{1,0:T(8,128)S(1)}, f32[32,1024]{1,0:T(8,128)S(1)}, u32[]{:S(2)}, u32[]{:S(2)}) collective-permute-start(f32[32,1024]{1,0:T(8,128)S(1)} %get-tuple-element.68.refs_0_), channel_id=1, source_target_pairs={{2,0},{3,1},{6,4},{7,5},{10,8},{11,9},{14,12},{15,13},{18,16},{19,... | collective-permute-start | bytes 393224 | tf_op jit(solution)/shard_map/ppermute | solution.py:368
  64.6 7.3 %collective-permute-start.17 = (f32[64,128]{1,0:T(8,128)S(1)}, f32[64,128]{1,0:T(8,128)S(1)}, u32[]{:S(2)}, u32[]{:S(2)}) collective-permute-start(f32[64,128]{1,0:T(8,128)S(1)} %shard_map.110), channel_id=1, source_target_pairs={{0,4},{4,0},{8,12},{12,8},{16,20},{20,16},{24,28},{28,24},{1,5},{5... | collective-permute-start | bytes 98312 | tf_op jit(solution)/shard_map/ppermute | solution.py:373
  66.3 12.1 %collective-permute-start.11 = (f32[32,1024]{1,0:T(8,128)S(1)}, f32[32,1024]{1,0:T(8,128)S(1)}, u32[]{:S(2)}, u32[]{:S(2)}) collective-permute-start(f32[32,1024]{1,0:T(8,128)S(1)} %get-tuple-element.91.f_second.refs_7_), channel_id=1, source_target_pairs={{0,2},{1,3},{4,6},{5,7},{8,10},{9,11},{12,14},{13,15},{16,18},{17,... | collective-permute-start | bytes 393224 | tf_op jit(solution)/shard_map/ppermute | solution.py:365
  70.6 9.9 %collective-permute-start.7 = (f32[32,1024]{1,0:T(8,128)S(1)}, f32[32,1024]{1,0:T(8,128)S(1)}, u32[]{:S(2)}, u32[]{:S(2)}) collective-permute-start(f32[32,1024]{1,0:T(8,128)S(1)} %get-tuple-element.79.f_second.refs_3_), channel_id=1, source_target_pairs={{0,2},{1,3},{4,6},{5,7},{8,10},{9,11},{12,14},{13,15},{16,18},{17,... | collective-permute-start | bytes 393224 | tf_op jit(solution)/shard_map/ppermute | solution.py:365
  71.9 4.3 %collective-permute-start.18 = (f32[128,128]{1,0:T(8,128)S(1)}, f32[128,128]{1,0:T(8,128)S(1)}, u32[]{:S(2)}, u32[]{:S(2)}) collective-permute-start(f32[128,128]{1,0:T(8,128)S(1)} %pad_maximum_fusion.2), channel_id=1, source_target_pairs={{0,8},{4,12},{8,0},{12,4},{16,24},{20,28},{24,16},{28,20},{1,9},{5... | collective-permute-start | bytes 196616 | tf_op jit(solution)/shard_map/ppermute | solution.py:373
  76.3 7.3 %collective-permute-start.19 = (f32[256,128]{1,0:T(8,128)S(1)}, f32[256,128]{1,0:T(8,128)S(1)}, u32[]{:S(2)}, u32[]{:S(2)}) collective-permute-start(f32[256,128]{1,0:T(8,128)S(1)} %pad_maximum_fusion.1), channel_id=1, source_target_pairs={{0,16},{4,20},{8,24},{12,28},{16,0},{20,4},{24,8},{28,12},{1,17},{... | collective-permute-start | bytes 393224 | tf_op jit(solution)/shard_map/ppermute | solution.py:373
  79.1 14.2 %collective-permute-start.12 = (f32[32,1024]{1,0:T(8,128)S(1)}, f32[32,1024]{1,0:T(8,128)S(1)}, u32[]{:S(2)}, u32[]{:S(2)}) collective-permute-start(f32[32,1024]{1,0:T(8,128)S(1)} %get-tuple-element.92.refs_0_), channel_id=1, source_target_pairs={{2,0},{3,1},{6,4},{7,5},{10,8},{11,9},{14,12},{15,13},{18,16},{19,... | collective-permute-start | bytes 393224 | tf_op jit(solution)/shard_map/ppermute | solution.py:368
  81.0 17.9 %collective-permute-start.8 = (f32[32,1024]{1,0:T(8,128)S(1)}, f32[32,1024]{1,0:T(8,128)S(1)}, u32[]{:S(2)}, u32[]{:S(2)}) collective-permute-start(f32[32,1024]{1,0:T(8,128)S(1)} %get-tuple-element.80.refs_0_), channel_id=1, source_target_pairs={{2,0},{3,1},{6,4},{7,5},{10,8},{11,9},{14,12},{15,13},{18,16},{19,... | collective-permute-start | bytes 393224 | tf_op jit(solution)/shard_map/ppermute | solution.py:368
  87.8 14.4 %collective-permute-start.23 = (f32[64,128]{1,0:T(8,128)S(1)}, f32[64,128]{1,0:T(8,128)S(1)}, u32[]{:S(2)}, u32[]{:S(2)}) collective-permute-start(f32[64,128]{1,0:T(8,128)S(1)} %pad_maximum_fusion.4), channel_id=1, source_target_pairs={{0,2},{1,3},{4,6},{5,7},{8,10},{9,11},{12,14},{13,15},{16,18},{17,... | collective-permute-start | bytes 98312 | tf_op jit(solution)/shard_map/ppermute | solution.py:365
  93.4 3.4 %copy-start.1 = (bf16[2,2,1024,1024]{3,2,1,0:T(8,128)(2,1)S(1)}, bf16[2,2,1024,1024]{3,2,1,0:T(8,128)(2,1)}, u32[]{:S(2)}) copy-start(bf16[2,2,1024,1024]{3,2,1,0:T(8,128)(2,1)} %copy-done) | copy-start | bytes 25165828
  98.9 4.7 %copy-start.4 = (f32[1,1,32,1024]{3,2,1,0:T(8,128)S(1)}, f32[1,1,32,1024]{3,2,1,0:T(8,128)}, u32[]{:S(2)}) copy-start(f32[1,1,32,1024]{3,2,1,0:T(8,128)} %param.17) | copy-start | bytes 393220
  98.9 4.7 %copy-start.5 = (f32[1,1,32,1024]{3,2,1,0:T(8,128)S(1)}, f32[1,1,32,1024]{3,2,1,0:T(8,128)}, u32[]{:S(2)}) copy-start(f32[1,1,32,1024]{3,2,1,0:T(8,128)} %param.18) | copy-start | bytes 393220
  101.6 1.9 %collective-permute-start.13 = (f32[64,1024]{1,0:T(8,128)S(1)}, f32[64,1024]{1,0:T(8,128)S(1)}, u32[]{:S(2)}, u32[]{:S(2)}) collective-permute-start(f32[64,1024]{1,0:T(8,128)S(1)} %get-tuple-element.97), channel_id=1, source_target_pairs={{0,1},{1,0},{2,3},{3,2},{4,5},{5,4},{6,7},{7,6},{8,9},{9,8},{10,11... | collective-permute-start | bytes 786440 | tf_op jit(solution)/shard_map/ppermute | solution.py:362
  101.7 1.9 %collective-permute-start.25 = (f32[32,1024]{1,0:T(8,128)S(1)}, f32[32,1024]{1,0:T(8,128)S(1)}, u32[]{:S(2)}, u32[]{:S(2)}) collective-permute-start(f32[32,1024]{1,0:T(8,128)S(1)} %get-tuple-element.106), channel_id=1, source_target_pairs={{0,1},{1,0},{2,3},{3,2},{4,5},{5,4},{6,7},{7,6},{8,9},{9,8},{10,11... | collective-permute-start | bytes 393224 | tf_op jit(solution)/shard_map/ppermute | solution.py:362
  102.3 1.3 %collective-permute-start.24 = (f32[64,128]{1,0:T(8,128)S(1)}, f32[64,128]{1,0:T(8,128)S(1)}, u32[]{:S(2)}, u32[]{:S(2)}) collective-permute-start(f32[64,128]{1,0:T(8,128)S(1)} %broadcast_select_fusion.q_keep), channel_id=1, source_target_pairs={{0,1},{1,0},{2,3},{3,2},{4,5},{5,4},{6,7},{7,6},{8,9},{9,8},{10,11... | collective-permute-start | bytes 98312 | tf_op jit(solution)/shard_map/ppermute | solution.py:362

commit v2 on v1

v2 whole, which is shorter than its diff:
```python
import functools

import jax
import jax.numpy as jnp
from jax import lax
from jax.experimental import pallas as pl
from jax.experimental.pallas import tpu as pltpu
from jax.sharding import PartitionSpec as P


f32 = jnp.float32
bf16 = jnp.bfloat16
highest = lax.Precision.HIGHEST
LANES = 128
BLOCKS = 2
PIECES = 4


def halves(x):
    top = x.astype(bf16)
    return top, (x - top.astype(f32)).astype(bf16)


def dot(left, right):
    return jnp.dot(left, right, preferred_element_type=f32)


def dot_rows(left, right):
    return lax.dot_general(left, right, (((1,), (1,)), ((), ())), preferred_element_type=f32)


def three(x, top_right, low_right, how=dot):
    rows = x.shape[0]
    top, low = halves(x)
    both = how(jnp.concatenate([top, low], axis=0), top_right)
    return both[:rows] + both[rows:] + how(top, low_right)


def times(x, weights, member):
    step = weights[0].shape[2]
    top, low = halves(x)
    both = jnp.concatenate([top, low], axis=0)
    rows = x.shape[0]
    first, second = 0.0, 0.0
    for i, piece in enumerate(weights):
        cols = slice(i * step, (i + 1) * step)
        first = first + dot(both[:, cols], piece[member, 0])
        second = second + dot(top[:, cols], piece[member, 1])
    return first[:rows] + first[rows:] + second


def times_transposed(x, weights, member):
    return jnp.concatenate(
        [three(x, piece[member, 0], piece[member, 1], dot_rows) for piece in weights], axis=1
    )


def member():
    return lax.axis_index("slab") & 1


def pair():
    return lax.axis_index("slab") >> 1


def spec(space):
    return pl.BlockSpec(memory_space=space)


def call(body, outs, args, work, aliases=None, scratch=(), hbm=()):
    specs = [spec(pltpu.VMEM) for _ in args]
    args = list(args)
    for place in hbm:
        specs[place] = spec(pltpu.HBM)
        args[place] = pltpu.with_memory_space_constraint(args[place], pltpu.HBM)
    return pl.pallas_call(
        body,
        out_shape=outs,
        in_specs=specs,
        out_specs=[spec(pltpu.VMEM) for _ in outs],
        input_output_aliases=aliases or {},
        scratch_shapes=list(scratch),
        cost_estimate=pl.CostEstimate(flops=int(work * 8e8), bytes_accessed=0, transcendentals=0),
        compiler_params=pltpu.CompilerParams(vmem_limit_bytes=VMEM_LIMIT),
    )(*args)


VMEM_LIMIT = 16 << 20


def struct(shape, dtype=f32):
    return jax.ShapeDtypeStruct(shape, dtype)


def pick(own, oth):
    first = member() == 0
    return jnp.where(first, own, oth), jnp.where(first, oth, own)


def hold(idle, before, after):
    @pl.when(idle)
    def _():
        for old, new in zip(before, after):
            new[...] = old[...]


def load(matrix, *refs):
    pieces, sems = refs[:PIECES], refs[PIECES]
    step = pieces[0].shape[0]
    copies = [
        pltpu.make_async_copy(matrix.at[pl.ds(i * step, step)], piece, sems.at[i])
        for i, piece in enumerate(pieces)
    ]
    for copy in copies:
        copy.start()
    for copy in copies:
        copy.wait()


def first_products(*refs):
    vector, one, two, diagonal, index = refs[:5]
    pieces = refs[5 : 5 + PIECES]
    keep, send, x, total, sems = refs[5 + PIECES :]
    rows, prim = vector.shape[0], one.shape[0]
    extra = 2 * prim
    copies = [
        pltpu.make_async_copy(vector, x.at[pl.ds(0, rows)], sems.at[0]),
        pltpu.make_async_copy(one, x.at[pl.ds(rows, prim)], sems.at[1]),
        pltpu.make_async_copy(two, x.at[pl.ds(rows + prim, prim)], sems.at[2]),
    ]
    for copy in copies:
        copy.start()
    for copy in copies:
        copy.wait()
    x[rows:, :] = x[rows:, :] * diagonal[...]
    step = pieces[0].shape[0]
    for i, piece in enumerate(pieces):
        top, low = halves(piece[...])
        part = three(x[:, i * step : (i + 1) * step], top, low)
        if i == 0:
            total[...] = part
        else:
            total[...] += part
    half = rows // 2
    here, there = member(), 1 - member()
    for out, which in ((keep, here), (send, there)):
        out[:half, :] = total[pl.ds(pl.multiple_of(which * half, 8), half), :]
        out[half : half + extra, :] = total[rows:, :]
        out[half + extra :, :] = jnp.zeros_like(out[half + extra :, :])
        out[half + extra : half + extra + 1, :] = diagonal[...]
        out[half + extra + 1 : half + extra + 2, :prim] = index[...].astype(f32)


def split(own, oth, weights):
    here = member()
    for which, piece in ((here, own), (1 - here, oth)):
        top, low = halves(piece[...])
        weights[which, 0] = top
        weights[which, 1] = low


def diagonals(keep, recv):
    place = keep.shape[0] - 8
    return pick(keep[place : place + 1, :], recv[place : place + 1, :])


def start_chain(keep, recv, *refs):
    weights, (f_first, f_second) = refs[:PIECES], refs[PIECES:]
    rows = f_first.shape[0]

    @pl.when(pair() == 0)
    def _():
        first, second = pick(keep[:rows, :], recv[:rows, :])
        f_first[...] = first
        f_second[...] = second + times(first, weights, 1)


def start_last(keep, recv, *refs):
    weights, (f_first, f_second, k_first, k_second) = refs[:PIECES], refs[PIECES:]
    rows, extra = f_first.shape[0], k_first.shape[0]
    stop = keep.shape[0] - 8

    @pl.when(pair() == 0)
    def _():
        at = stop - extra - rows
        first, second = pick(keep[at:stop, :], recv[at:stop, :])
        second = second + times(first, weights, 1)
        f_first[...] = first[:rows]
        f_second[...] = second[:rows]
        k_first[...] = first[rows:]
        k_second[...] = second[rows:]


def top_one(at, keep, recv, carried, *refs):
    weights, (n_first, n_second) = refs[:PIECES], refs[PIECES:]
    rows = n_first.shape[0]

    @pl.when(pair() == 1)
    def _():
        first, second = pick(keep[at : at + rows, :], recv[at : at + rows, :])
        first = first + times(carried[...], weights, 0)
        second = second + times(first, weights, 1)
        n_first[...] = first + times(second, weights, 0)
        n_second[...] = second


def top_two(with_basis, keep, recv, v_first, v_second, carried, *refs):
    riding, weights, (n_first, n_second) = refs[0], refs[1 : 1 + PIECES], refs[1 + PIECES :]
    rows = v_first.shape[0]
    few = riding.shape[0] // 2
    extra = 2 * few
    at = keep.shape[0] - 8 - extra

    @pl.when(pair() == 1)
    def _():
        d_first, d_second = diagonals(keep, recv)
        x = d_first * v_first[...] + carried[...]
        if with_basis:
            here = pl.ds(pl.multiple_of(at + member() * few, 8), few)
            k_first, k_second = pick(keep[here, :], recv[here, :])
            first = times(jnp.concatenate([x, riding[few:, :]], axis=0), weights, 0)
            k_first = first[rows:] + k_first
            y = d_second * v_second[...] + first[:rows]
            second = times(jnp.concatenate([y, k_first], axis=0), weights, 1)
            first = jnp.concatenate([first[:rows], k_first], axis=0)
            second = jnp.concatenate([second[:rows], second[rows:] + k_second], axis=0)
        else:
            first = times(x, weights, 0)
            second = times(d_second * v_second[...] + first, weights, 1)
        n_first[...] = first + times(second, weights, 0)
        n_second[...] = second


def down(f_first, f_second, carried, weights):
    second = f_second + times(carried, weights, 1)
    return f_first + times(second, weights, 0), second


def turn(keep, recv, f_first, f_second, carried, *refs):
    weights, old = refs[:PIECES], refs[PIECES : PIECES + 2]
    n_first, n_second, g_first, g_second = refs[PIECES + 2 :]

    @pl.when(pair() == 0)
    def _():
        first, second = down(f_first[...], f_second[...], carried[...], weights)
        n_second[...] = second
        n_first[...] = first
        d_first, d_second = diagonals(keep, recv)
        again = times(d_first * first, weights, 0)
        g_first[...] = again
        g_second[...] = times(d_second * second + again, weights, 1)

    hold(pair() != 0, old, (n_first, n_second))


def back(with_basis, f_first, f_second, k_first, k_second, carried, *refs):
    weights, old, (n_first, n_second) = refs[:PIECES], refs[PIECES : PIECES + 2], refs[PIECES + 2 :]
    few = k_first.shape[0] // 2

    @pl.when(pair() == 0)
    def _():
        first, second = f_first[...], f_second[...]
        if with_basis:
            here = pl.ds(pl.multiple_of(member() * few, 8), few)
            first = jnp.concatenate([first, k_first[here, :]], axis=0)
            second = jnp.concatenate([second, k_second[here, :]], axis=0)
        n_first[...], n_second[...] = down(first, second, carried[...], weights)

    hold(pair() != 0, old, (n_first, n_second))


def adjoint_start(own_spots, oth_spots, k_second, *refs):
    weights, (y_first, y_second, sent) = refs[:PIECES], refs[PIECES:]
    prim = y_first.shape[0]

    @pl.when(pair() == 0)
    def _():
        first, second = pick(own_spots[...], oth_spots[...])
        second = second + times_transposed(first, weights, 0)
        y_first[...] = first
        y_second[...] = second
        sent[:prim, :] = times_transposed(second, weights, 1)
        sent[prim:, :] = k_second[pl.ds(pl.multiple_of(member() * prim, 8), prim), :]


def placed(u, places, width):
    prim = u.shape[0]
    zero = jnp.zeros_like(u)
    rows = [u if i in places else zero for i in range(width // prim)]
    return jnp.concatenate(rows, axis=0)


def score(x, u):
    top, low = halves(u)
    return three(x, top, low, dot_rows)


def only(x, place, prim):
    lane = lax.broadcasted_iota(jnp.int32, x.shape, 1)
    return jnp.where((lane >= place * prim) & (lane < (place + 1) * prim), x, 0.0)


def pack(values, out, at):
    rows, width = values.shape
    per = out.shape[1] // width
    for j in range(rows // 8):
        row = at + (j // per) * 8
        out[row : row + 8, (j % per) * width : (j % per + 1) * width] = values[8 * j : 8 * j + 8, :]


def unpack(packed, at, rows, width):
    per = packed.shape[1] // width
    return jnp.concatenate(
        [
            packed[
                at + (j // per) * 8 : at + (j // per) * 8 + 8,
                (j % per) * width : (j % per + 1) * width,
            ]
            for j in range(rows // 8)
        ],
        axis=0,
    )


def adjoint_top(width, keep, recv, own_spots, oth_spots, carried, *refs):
    weights, refs = refs[:PIECES], refs[PIECES:]
    blocks, old, (y_first, y_second, sent) = refs[: 2 * BLOCKS], refs[2 * BLOCKS : -3], refs[-3:]
    prim = y_first.shape[0]

    @pl.when(pair() == 1)
    def _():
        first, second = pick(own_spots[...], oth_spots[...])
        first = first + carried[:prim, :]
        second = second + times_transposed(first, weights, 0)
        z_second = times_transposed(second, weights, 1)
        first = first + z_second
        z_first = times_transposed(first, weights, 0)
        sent[:prim, :] = z_first
        w_first, w_second = pick(keep[...], recv[...])
        stop = w_first.shape[0] - 8
        w = score(w_first[:stop], placed(first, (0, 2), width)) + score(
            w_second[:stop], placed(second, (0, 2), width)
        )
        d_first, d_second = diagonals(keep, recv)
        n_first = jnp.concatenate([r[...] for r in blocks[0::2]], axis=0)
        n_second = jnp.concatenate([r[...] for r in blocks[1::2]], axis=0)
        g = score(d_first * n_first, placed(z_first, (1,), width)) + score(
            d_second * n_second, placed(z_second, (1,), width)
        )
        half = n_first.shape[0]
        pack(only(w[:half], 0, prim) + g + only(w[half:], 2, prim), sent, prim)

    hold(pair() != 1, old, (y_first, y_second))


def score_turn(carried, y_first, y_second, k_first, k_second, *refs):
    blocks, values = refs[:-1], refs[-1]
    prim = y_first.shape[0]
    half, width = values.shape

    @pl.when(pair() == 0)
    def _():
        first = jnp.concatenate(
            [r[...] for r in blocks[0::4]] + [k_first[...]] + [r[...] for r in blocks[2::4]], axis=0
        )
        second = jnp.concatenate(
            [r[...] for r in blocks[1::4]] + [k_second[...]] + [r[...] for r in blocks[3::4]], axis=0
        )
        w = score(first, placed(y_first[...], (0, 1, 2), width)) + score(
            second, placed(y_second[...] + carried[:prim, :], (0, 1, 2), width)
        )
        extra = k_first.shape[0]
        values[...] = (
            unpack(carried, prim, half, width)
            + only(w[:half], 0, prim)
            + only(w[half : half + extra], 2, prim)
            + only(w[half + extra :], 1, prim)
        )


def settle(*refs):
    blocks, (keep, send) = refs[: 4 * BLOCKS], refs[4 * BLOCKS :]
    rows = blocks[0].shape[0]
    for i in range(BLOCKS):
        a1, b1, a2, b2 = blocks[4 * i : 4 * i + 4]
        here = slice(i * rows, (i + 1) * rows)
        keep[here, :], send[here, :] = pick(
            2.0 * a1[...] - a2[:rows, :], 2.0 * b1[...] - b2[:rows, :]
        )
    keep[BLOCKS * rows :, :], send[BLOCKS * rows :, :] = pick(blocks[2][rows:, :], blocks[3][rows:, :])


def finish(keep, recv, q_keep, q_recv, one, two, out):
    prim = one.shape[0]
    rows = keep.shape[0] - prim
    k_low, k_high = pick(keep[rows:, :], recv[rows:, :])
    right = jnp.concatenate([-k_low, -k_high, one[...], two[...]], axis=0)
    top, low = halves(right)
    here = member()
    for n, q, which in ((keep, q_keep, here), (recv, q_recv, 1 - here)):
        out[pl.ds(pl.multiple_of(which * rows, 8), rows), :] = n[:rows, :] + three(q[...], top, low)


def on_device(
    residual,
    inverse_slab,
    diagonal,
    primal_index,
    coarse_map,
    schur_small,
    constraint_basis,
    coarse_basis,
    coarse_inverse,
):
    levels = lax.axis_size("slab")
    subs = lax.axis_size("sub")
    assert levels == 4 and subs & (subs - 1) == 0
    sub = lax.axis_index("sub")

    def swap(x):
        return lax.ppermute(x, "slab", [(i, i ^ 1) for i in range(levels)])

    def rise(x):
        return lax.ppermute(x, "slab", [(0, 2), (1, 3)])

    def fall(x):
        return lax.ppermute(x, "slab", [(2, 0), (3, 1)])

    def gather(x):
        distance = 1
        while distance < subs:
            pairs = [
                (i * levels + k, (i ^ distance) * levels + k) for i in range(subs) for k in range(2)
            ]
            other = lax.ppermute(x, ("sub", "slab"), pairs)
            x = jnp.concatenate([x, other], axis=0)
            distance *= 2
        return x

    vector = residual[0, 0]
    matrix = inverse_slab[0, 0]
    one, two = constraint_basis[0, 0], coarse_basis[0, 0]
    rows, size = vector.shape
    prim = primal_index.shape[-1]
    coarse_count, share = coarse_inverse.shape
    half = rows // 2
    block = half // BLOCKS
    extra = 2 * prim
    width = -(-3 * prim // LANES) * LANES
    packed = -(-half * width // (8 * size)) * 8
    step = size // PIECES
    assert half == extra and prim <= coarse_count and size % width == 0

    def like(count, *heights):
        return [struct((h, size)) for h in heights for _ in range(count)]

    own = call(load, like(PIECES, step), [matrix], 1, scratch=[pltpu.SemaphoreType.DMA((PIECES,))], hbm=(0,))
    oth = [swap(piece) for piece in own]

    fixed = jnp.concatenate(
        [
            coarse_inverse.T,
            jnp.pad(schur_small[0], ((0, 0), (0, coarse_count - prim))),
            jnp.pad(coarse_map.astype(f32), ((0, 7), (0, coarse_count - prim))),
        ],
        axis=0,
    )
    fixed = gather(fixed).reshape(subs, share + prim + 8, coarse_count)
    inverse_rows = fixed[:, :share].reshape(coarse_count, coarse_count)
    schur = fixed[:, share : share + prim, :prim]
    maps = fixed[:, share + prim, :prim]
    order = jnp.arange(subs, dtype=jnp.int32) ^ sub
    columns = (order[:, None] * share + jnp.arange(share, dtype=jnp.int32)).reshape(-1).astype(f32)
    onehot = (maps[:, :, None] == jnp.arange(coarse_count, dtype=jnp.int32).astype(f32)).astype(f32)
    onehot_there = (maps[:, :, None] == columns).astype(f32)

    keep, send = call(
        first_products,
        like(2, half + extra + 8),
        [vector, one, two, diagonal[0], primal_index[0], *own],
        2,
        scratch=[
            pltpu.VMEM((rows + extra, size), f32),
            pltpu.VMEM((rows + extra, size), f32),
            pltpu.SemaphoreType.DMA((3,)),
        ],
        hbm=(0, 1, 2),
    )
    recv = swap(send)
    weights = [
        call(split, [struct((2, 2, step, size), bf16)], [own[i], oth[i]], 0.3)[0]
        for i in range(PIECES)
    ]
    place = jnp.arange(size, dtype=jnp.int32)
    own_spots = (primal_index[0, 0][:, None] == place).astype(f32)
    oth_spots = (recv[half + extra + 1, :prim][:, None] == place.astype(f32)).astype(f32)

    span = range(BLOCKS)
    f, carried = [], []
    for i in span[:-1]:
        f.append(call(start_chain, like(2, block), [keep, recv, *weights], 1))
        carried.append(rise(f[i][1]))
    *f_last, k_first, k_second = call(start_last, like(2, block, extra), [keep, recv, *weights], 1)
    f.append(f_last)
    carried.append(rise(f_last[1]))
    y_first, y_second, sent = call(
        adjoint_start,
        like(2, prim) + like(1, 2 * prim),
        [own_spots, oth_spots, k_second, *weights],
        2,
    )
    riding = rise(sent)

    n = []
    for i in span:
        n.append(
            call(
                functools.partial(top_one, i * block),
                like(2, block),
                [keep, recv, carried[i], *weights],
                3,
            )
        )
        carried[i] = fall(n[i][0])
    y_first, y_second, sent = call(
        functools.partial(adjoint_top, width),
        like(2, prim) + like(1, prim + packed),
        [keep, recv, own_spots, oth_spots, riding, *weights, *n[0], *n[1], y_first, y_second],
        4,
        aliases={5 + PIECES + 2 * BLOCKS: 0, 6 + PIECES + 2 * BLOCKS: 1},
    )
    z_back = fall(sent)

    n_one, g = [], []
    for i in span:
        turned = call(
            turn,
            like(4, block),
            [keep, recv, *f[i], carried[i], *weights, *n[i]],
            4,
            aliases={5 + PIECES: 0, 6 + PIECES: 1},
        )
        n_one.append(turned[:2])
        g.append(turned[2:])
        carried[i] = rise(g[i][1])
    pieces = []
    for i in span:
        pieces += [*f[i], *g[i]]
    (values,) = call(
        score_turn,
        [struct((half, width))],
        [z_back, y_first, y_second, k_first, k_second, *pieces],
        1,
    )
    values = gather(values).reshape(subs, half, width)

    n_two = []
    for i in span:
        n_two.append(
            call(
                functools.partial(top_two, i == 0),
                like(2, block + prim if i == 0 else block),
                [keep, recv, *n_one[i], carried[i], riding, *weights],
                3,
            )
        )
        carried[i] = fall(n_two[i][0])
    for i in span:
        n_two[i] = call(
            functools.partial(back, i == 0),
            like(2, block + prim if i == 0 else block),
            [*g[i], k_first, k_second, carried[i], *weights, *n_two[i]],
            2,
            aliases={5 + PIECES: 0, 6 + PIECES: 1},
        )
    pieces = []
    for i in span:
        pieces += [*n_one[i], *n_two[i]]
    m_keep, m_send = call(settle, like(2, half + prim), pieces, 0.5)
    m_recv = swap(m_send)

    def times_high(form, left, right):
        return jnp.einsum(form, left, right, precision=highest, preferred_element_type=f32)

    p_one = values[:, :, :prim]
    p_defect = p_one - values[:, :, prim : 2 * prim]
    x_one = values[:, :prim, 2 * prim : 3 * prim]
    x_two = values[:, prim : 2 * prim, 2 * prim : 3 * prim]
    sol = times_high("rn,mn->rm", times_high("srp,spn->rn", p_one, onehot), inverse_rows)
    picked = times_high("rm,spm->srp", sol, onehot_there)
    multiplier = times_high("srp,spq->srq", p_one, schur)
    p_two = p_defect + times_high("srp,spq->srq", multiplier, x_one) - times_high(
        "srp,spq->srq", picked, x_two
    )
    sol = times_high("rn,mn->rm", times_high("srp,spn->rn", p_two, onehot), inverse_rows)
    q_one = jnp.concatenate([-multiplier[0], picked[0]], axis=1)
    q_two = jnp.concatenate(
        [
            -times_high("rp,pq->rq", p_two[0], schur[0]),
            times_high("rm,pm->rp", sol, onehot_there[0]),
        ],
        axis=1,
    )
    q = jnp.concatenate([q_one, q_one + q_two], axis=1)
    q_upper = rise(q)
    q = jnp.where(pair() == 0, q, q_upper)
    q_recv = swap(q)
    (out,) = call(finish, [struct((rows, size))], [m_keep, m_recv, q, q_recv, one, two], 0.5)
    return out[None, None]


def solution(mesh):
    placed_as = (
        P("sub", "slab", None, None),
        P("sub", "slab", None, None),
        P("sub", "slab", None),
        P("sub", "slab", None),
        P("sub", None),
        P("sub", None, None),
        P("sub", "slab", None, None),
        P("sub", "slab", None, None),
        P(None, "sub"),
    )

    return jax.shard_map(
        on_device,
        mesh=mesh,
        in_specs=placed_as,
        out_specs=P("sub", "slab", None, None),
        check_vma=False,
    )
```

time: 106 us -> 131 us (1.24)
  local copies, waits for them, and re-layouts: 8.38 us -> 22.6 us
  waiting for transfers between devices: 13.5 us -> 20.8 us
  matrix products: 3.22 us -> 9.63 us
  Pallas kernels: 35.6 us -> 31.7 us
    ppermute x6, starting transfers between devices: 12.1 us -> 21.7 us  [gather(): other = lax.ppermute(x, ('sub', 'slab'), pairs)]
    unnamed x25 -> x87, local copies, waits for them, and re-layouts: 7.92 us -> 17.5 us
    ppermute x7 -> x6, starting transfers between devices: 19.1 us -> 12.3 us  [rise(): return lax.ppermute(x, 'slab', [(0, 2), (1, 3)])]
    dot_general x10, matrix products: 3.22 us -> 9.63 us  [times_high(): jnp.einsum(form, left, right, precision=highest, preferred_element_type=f32)]
    ppermute x7 -> x6, waiting for transfers between devices: 0.02 us -> 5.4 us  [rise(): return lax.ppermute(x, 'slab', [(0, 2), (1, 3)])]
    ppermute x6, waiting for transfers between devices: 9.5 us -> 14.2 us  [gather(): other = lax.ppermute(x, ('sub', 'slab'), pairs)]
    pallas_call x21, Pallas kernels: 35.6 us -> 31.7 us  [call(): pl.pallas_call(body, out_shape=outs, in_specs=specs, out_specs=[spec(pltp...]
    ppermute x7 -> x5, waiting for transfers between devices: 2.8 us -> 0.03 us  [fall(): return lax.ppermute(x, 'slab', [(2, 0), (3, 1)])]
  transfers between devices with their start and end apart: 26 -> 24, of which waited for: 7 -> 8; matrix products, arithmetic and copies ran while one was open for 6% -> 18% of each run, Pallas kernels for 31% -> 17%
where the time goes in v2:
time: 131 us; the launch traced here: 129 us
  starting transfers between devices  41.7 us (32%)
  Pallas kernels  31.7 us (24%)
  local copies, waits for them, and re-layouts  22.6 us (17%)
  waiting for transfers between devices  20.8 us (16%)
  matrix products  9.63 us (7%)
  other arithmetic  2 us (2%)
    pallas_call x21, Pallas kernels, call(): pl.pallas_call(body, out_shape=outs, in_specs=specs, out_specs=[spec(pltp...  31.7 us
    ppermute x6, starting transfers between devices, gather(): other = lax.ppermute(x, ('sub', 'slab'), pairs)  21.7 us
    unnamed x87, local copies, waits for them, and re-layouts  17.5 us
    ppermute x6, waiting for transfers between devices, gather(): other = lax.ppermute(x, ('sub', 'slab'), pairs)  14.2 us
    ppermute x6, starting transfers between devices, rise(): return lax.ppermute(x, 'slab', [(0, 2), (1, 3)])  12.3 us
    dot_general x10, matrix products, times_high(): jnp.einsum(form, left, right, precision=highest, preferred_element_type=f32)  9.63 us
    ppermute x5, starting transfers between devices, fall(): return lax.ppermute(x, 'slab', [(2, 0), (3, 1)])  6.46 us
    ppermute x6, waiting for transfers between devices, rise(): return lax.ppermute(x, 'slab', [(0, 2), (1, 3)])  5.4 us
  transfers between devices with their start and end apart: 24, of which 8 were waited for; matrix products, arithmetic and copies ran while one was open for 18% of the time, Pallas kernels for 17%

profile of v2, /device:TPU:0, one launch (start us, length us, event | category | flops | bytes accessed | tf_op | source)
XLA Modules:
  0.0 129.4 jit_solution(11898793143404604159)
XLA Ops:
  0.0 3.9 %shard_map.91 = (f32[256,1024]{1,0:T(8,128)}, f32[256,1024]{1,0:T(8,128)S(1)}, f32[256,1024]{1,0:T(8,128)}, f32[256,1024]{1,0:T(8,128)}) custom-call(f32[1024,1024]{1,0:T(8,128)} %bitcast.59), custom_call_target="tpu_custom_call" | custom-call | flops 800000000 | tf_op jit(solution)/shard_map/pallas_call | solution.py:76
  6.9 4.8 %collective-permute-start.19 = (f32[56,128]{1,0:T(8,128)S(1)}, f32[56,128]{1,0:T(8,128)S(1)}, u32[]{:S(2)}, u32[]{:S(2)}) collective-permute-start(f32[56,128]{1,0:T(8,128)S(1)} %pad_maximum_fusion.5), channel_id=1, source_target_pairs={{0,4},{1,5},{4,0},{5,1},{8,12},{9,13},{12,8},{13,9},{16,20},{17,21... | collective-permute-start | bytes 86024 | tf_op jit(solution)/shard_map/ppermute | solution.py:435
  11.8 4.5 %shard_map.92 = (f32[136,1024]{1,0:T(8,128)S(1)}, f32[136,1024]{1,0:T(8,128)S(1)}) custom-call(f32[128,1024]{1,0:T(8,128)} %bitcast.74, f32[32,1024]{1,0:T(8,128)} %bitcast.47, f32[32,1024]{1,0:T(8,128)} %bitcast.49, f32[1,1024]{1,0:T(1,128)S(1)} %bitcast.53, s32[1,32]{1,0:T(1,128)S(1)} %bitcast.51, f32[256,1024]{1,0:T(8,128)} %get-tuple-element.45.refs_5_.own, ...), custom_call_target="tpu_custom_call" | custom-call | flops 1600000000 | tf_op jit(solution)/shard_map/pallas_call | solution.py:76
  16.3 3.5 %collective-permute-start.20 = (f32[112,128]{1,0:T(8,128)S(1)}, f32[112,128]{1,0:T(8,128)S(1)}, u32[]{:S(2)}, u32[]{:S(2)}) collective-permute-start(f32[112,128]{1,0:T(8,128)S(1)} %pad_maximum_fusion.3), channel_id=1, source_target_pairs={{0,8},{1,9},{4,12},{5,13},{8,0},{9,1},{12,4},{13,5},{16,24},{17,25... | collective-permute-start | bytes 172040 | tf_op jit(solution)/shard_map/ppermute | solution.py:435
  20.5 2.0 %collective-permute-done.20 = f32[112,128]{1,0:T(8,128)S(1)} collective-permute-done((f32[112,128]{1,0:T(8,128)S(1)}, f32[112,128]{1,0:T(8,128)S(1)}, u32[]{:S(2)}, u32[]{:S(2)}) %collective-permute-start.20) | collective-permute-done | bytes 57376 | tf_op jit(solution)/shard_map/ppermute | solution.py:435
  23.1 4.5 %collective-permute-start.21 = (f32[224,128]{1,0:T(8,128)}, f32[224,128]{1,0:T(8,128)}, u32[]{:S(2)}, u32[]{:S(2)}) collective-permute-start(f32[224,128]{1,0:T(8,128)} %get-tuple-element.87), channel_id=1, source_target_pairs={{0,16},{1,17},{4,20},{5,21},{8,24},{9,25},{12,28},{13,29},{16,0},{... | collective-permute-start | bytes 344072 | tf_op jit(solution)/shard_map/ppermute | solution.py:435
  27.7 4.7 %collective-permute-done.21 = f32[224,128]{1,0:T(8,128)} collective-permute-done((f32[224,128]{1,0:T(8,128)}, f32[224,128]{1,0:T(8,128)}, u32[]{:S(2)}, u32[]{:S(2)}) %collective-permute-start.21) | collective-permute-done | bytes 114720 | tf_op jit(solution)/shard_map/ppermute | solution.py:435
  36.7 1.2 copy-done.7
  37.9 1.2 copy-done.9
  39.4 1.8 %shard_map.95.refs_2_.refs_3_ = bf16[2,2,256,1024]{3,2,1,0:T(8,128)(2,1)S(1)} custom-call(f32[256,1024]{1,0:T(8,128)} %get-tuple-element.47.refs_7_.own, f32[256,1024]{1,0:T(8,128)} %collective-permute-done.3.oth), custom_call_target="tpu_custom_call" | custom-call | flops 240000000 | tf_op jit(solution)/shard_map/pallas_call | solution.py:76
  41.3 2.6 %shard_map.96.refs_3_.refs_4_ = bf16[2,2,256,1024]{3,2,1,0:T(8,128)(2,1)S(1)} custom-call(f32[256,1024]{1,0:T(8,128)} %get-tuple-element.48.refs_8_.own, f32[256,1024]{1,0:T(8,128)} %collective-permute-done.4.oth), custom_call_target="tpu_custom_call" | custom-call | flops 240000000 | tf_op jit(solution)/shard_map/pallas_call | solution.py:76
  43.9 2.6 %shard_map.93.refs_0_.refs_1_ = bf16[2,2,256,1024]{3,2,1,0:T(8,128)(2,1)S(1)} custom-call(f32[256,1024]{1,0:T(8,128)} %get-tuple-element.45.refs_5_.own, f32[256,1024]{1,0:T(8,128)} %collective-permute-done.1.oth), custom_call_target="tpu_custom_call" | custom-call | flops 240000000 | tf_op jit(solution)/shard_map/pallas_call | solution.py:76
  47.4 1.3 %collective-permute-start.10 = (f32[32,1024]{1,0:T(8,128)S(1)}, f32[32,1024]{1,0:T(8,128)S(1)}, u32[]{:S(2)}, u32[]{:S(2)}) collective-permute-start(f32[32,1024]{1,0:T(8,128)S(1)} %get-tuple-element.67.f_second.refs_5_), channel_id=1, source_target_pairs={{0,2},{1,3},{4,6},{5,7},{8,10},{9,11},{12,14},{13,15},{16,18},{17,... | collective-permute-start | bytes 393224 | tf_op jit(solution)/shard_map/ppermute | solution.py:424
  49.5 1.3 %collective-permute-start.5 = (f32[32,1024]{1,0:T(8,128)S(1)}, f32[32,1024]{1,0:T(8,128)S(1)}, u32[]{:S(2)}, u32[]{:S(2)}) collective-permute-start(f32[32,1024]{1,0:T(8,128)S(1)} %get-tuple-element.52.f_second.refs_1_), channel_id=1, source_target_pairs={{0,2},{1,3},{4,6},{5,7},{8,10},{9,11},{12,14},{13,15},{16,18},{17,... | collective-permute-start | bytes 393224 | tf_op jit(solution)/shard_map/ppermute | solution.py:424
  50.8 2.6 %shard_map.101 = (f32[32,1024]{1,0:T(8,128)S(1)}, f32[32,1024]{1,0:T(8,128)S(1)}, f32[64,1024]{1,0:T(8,128)S(1)}) custom-call(f32[32,1024]{1,0:T(8,128)S(1)} %fusion.6.own_spots, f32[32,1024]{1,0:T(8,128)S(1)} %compare_convert_fusion.oth_spots, f32[64,1024]{1,0:T(8,128)S(1)} %get-tuple-element.60.k_second, ...), custom_call_target="tpu_custom_call" | custom-call | flops 1600000000 | tf_op jit(solution)/shard_map/pallas_call | solution.py:76
  53.4 1.3 %collective-permute-start.8 = (f32[64,1024]{1,0:T(8,128)S(1)}, f32[64,1024]{1,0:T(8,128)S(1)}, u32[]{:S(2)}, u32[]{:S(2)}) collective-permute-start(f32[64,1024]{1,0:T(8,128)S(1)} %get-tuple-element.61), channel_id=1, source_target_pairs={{0,2},{1,3},{4,6},{5,7},{8,10},{9,11},{12,14},{13,15},{16,18},{17,... | collective-permute-start | bytes 786440 | tf_op jit(solution)/shard_map/ppermute | solution.py:424
  54.8 1.3 collective-permute-start.11
  56.1 1.3 collective-permute-start.6
  57.4 3.8 %collective-permute-done.8.refs_0_.carried = f32[64,1024]{1,0:T(8,128)S(1)} collective-permute-done((f32[64,1024]{1,0:T(8,128)S(1)}, f32[64,1024]{1,0:T(8,128)S(1)}, u32[]{:S(2)}, u32[]{:S(2)}) %collective-permute-start.8) | collective-permute-done | bytes 262176 | tf_op jit(solution)/shard_map/ppermute | solution.py:424
  61.3 1.3 collective-permute-start.15
  62.6 3.1 %shard_map.105 = (f32[32,1024]{1,0:T(8,128)S(1)}, f32[32,1024]{1,0:T(8,128)S(1)}, f32[32,1024]{1,0:T(8,128)S(1)}, f32[32,1024]{1,0:T(8,128)S(1)}) custom-call(f32[136,1024]{1,0:T(8,128)S(1)} %get-tuple-element.49.keep, f32[136,1024]{1,0:T(8,128)S(1)} %collective-permute-done.recv, ...), custom_call_target="tpu_custom_call", output_to_operand_aliasing={{0}: (9, {}), {1}: (10, {})} | custom-call | flops 3200000000 | tf_op jit(solution)/shard_map/pallas_call | solution.py:76
  65.7 5.8 %collective-permute-start.12 = (f32[32,1024]{1,0:T(8,128)S(1)}, f32[32,1024]{1,0:T(8,128)S(1)}, u32[]{:S(2)}, u32[]{:S(2)}) collective-permute-start(f32[32,1024]{1,0:T(8,128)S(1)} %get-tuple-element.73.f_second.refs_7_), channel_id=1, source_target_pairs={{0,2},{1,3},{4,6},{5,7},{8,10},{9,11},{12,14},{13,15},{16,18},{17,... | collective-permute-start | bytes 393224 | tf_op jit(solution)/shard_map/ppermute | solution.py:424
  71.5 3.1 %shard_map.99 = (f32[32,1024]{1,0:T(8,128)S(1)}, f32[32,1024]{1,0:T(8,128)S(1)}, f32[32,1024]{1,0:T(8,128)S(1)}, f32[32,1024]{1,0:T(8,128)S(1)}) custom-call(f32[136,1024]{1,0:T(8,128)S(1)} %get-tuple-element.49.keep, f32[136,1024]{1,0:T(8,128)S(1)} %collective-permute-done.recv, ...), custom_call_target="tpu_custom_call", output_to_operand_aliasing={{0}: (9, {}), {1}: (10, {})} | custom-call | flops 3200000000 | tf_op jit(solution)/shard_map/pallas_call | solution.py:76
  74.6 1.3 %collective-permute-start.7 = (f32[32,1024]{1,0:T(8,128)S(1)}, f32[32,1024]{1,0:T(8,128)S(1)}, u32[]{:S(2)}, u32[]{:S(2)}) collective-permute-start(f32[32,1024]{1,0:T(8,128)S(1)} %get-tuple-element.58.f_second.refs_3_), channel_id=1, source_target_pairs={{0,2},{1,3},{4,6},{5,7},{8,10},{9,11},{12,14},{13,15},{16,18},{17,... | collective-permute-start | bytes 393224 | tf_op jit(solution)/shard_map/ppermute | solution.py:424
  76.7 2.4 %collective-permute-start.16 = (f32[64,128]{1,0:T(8,128)S(1)}, f32[64,128]{1,0:T(8,128)S(1)}, u32[]{:S(2)}, u32[]{:S(2)}) collective-permute-start(f32[64,128]{1,0:T(8,128)S(1)} %shard_map.110), channel_id=1, source_target_pairs={{0,4},{1,5},{4,0},{5,1},{8,12},{9,13},{12,8},{13,9},{16,20},{17,21... | collective-permute-start | bytes 98312 | tf_op jit(solution)/shard_map/ppermute | solution.py:435
  79.2 1.3 collective-permute-start.13
  80.5 2.0 %collective-permute-done.16 = f32[64,128]{1,0:T(8,128)S(1)} collective-permute-done((f32[64,128]{1,0:T(8,128)S(1)}, f32[64,128]{1,0:T(8,128)S(1)}, u32[]{:S(2)}, u32[]{:S(2)}) %collective-permute-start.16) | collective-permute-done | bytes 32800 | tf_op jit(solution)/shard_map/ppermute | solution.py:435
  82.5 2.6 %collective-permute-start.17 = (f32[128,128]{1,0:T(8,128)S(1)}, f32[128,128]{1,0:T(8,128)S(1)}, u32[]{:S(2)}, u32[]{:S(2)}) collective-permute-start(f32[128,128]{1,0:T(8,128)S(1)} %pad_maximum_fusion.2), channel_id=1, source_target_pairs={{0,8},{1,9},{4,12},{5,13},{8,0},{9,1},{12,4},{13,5},{16,24},{17,25... | collective-permute-start | bytes 196616 | tf_op jit(solution)/shard_map/ppermute | solution.py:435
  85.2 1.3 collective-permute-start.9
  86.5 2.2 %collective-permute-done.17 = f32[128,128]{1,0:T(8,128)S(1)} collective-permute-done((f32[128,128]{1,0:T(8,128)S(1)}, f32[128,128]{1,0:T(8,128)S(1)}, u32[]{:S(2)}, u32[]{:S(2)}) %collective-permute-start.17) | collective-permute-done | bytes 65568 | tf_op jit(solution)/shard_map/ppermute | solution.py:435
  88.7 3.9 %collective-permute-start.18 = (f32[256,128]{1,0:T(8,128)S(1)}, f32[256,128]{1,0:T(8,128)S(1)}, u32[]{:S(2)}, u32[]{:S(2)}) collective-permute-start(f32[256,128]{1,0:T(8,128)S(1)} %pad_maximum_fusion.1), channel_id=1, source_target_pairs={{0,16},{1,17},{4,20},{5,21},{8,24},{9,25},{12,28},{13,29},{16,0},{... | collective-permute-start | bytes 393224 | tf_op jit(solution)/shard_map/ppermute | solution.py:435
  92.7 1.8 %shard_map.107 = (f32[32,1024]{1,0:T(8,128)S(1)}, f32[32,1024]{1,0:T(8,128)S(1)}) custom-call(f32[32,1024]{1,0:T(8,128)S(1)} %get-tuple-element.72.f_first.refs_6_, f32[32,1024]{1,0:T(8,128)S(1)} %get-tuple-element.73.f_second.refs_7_, f32[64,1024]{1,0:T(8,128)S(1)} %get-tuple-element.59.k_first, ...), custom_call_target="tpu_custom_call", output_to_operand_aliasing={{0}: (9, {}), {1}: (10, {})} | custom-call | flops 1600000000 | tf_op jit(solution)/shard_map/pallas_call | solution.py:76
  94.5 3.3 %collective-permute-done.18 = f32[256,128]{1,0:T(8,128)S(1)} collective-permute-done((f32[256,128]{1,0:T(8,128)S(1)}, f32[256,128]{1,0:T(8,128)S(1)}, u32[]{:S(2)}, u32[]{:S(2)}) %collective-permute-start.18) | collective-permute-done | bytes 131104 | tf_op jit(solution)/shard_map/ppermute | solution.py:435
  97.9 1.2 fusion.4
  100.1 1.7 %copy.47 = f32[8,64,32]{1,2,0:T(8,128)} copy(f32[8,64,32]{2,1,0:T(8,128)} %get-tuple-element.86) | data formatting | bytes 131072
  101.8 1.7 %copy.50 = f32[8,64,32]{1,2,0:T(8,128)} copy(f32[8,64,32]{2,1,0:T(8,128)} %get-tuple-element.85) | data formatting | bytes 131072
  103.5 1.3 convolution_bitcast_fusion.2
  105.3 1.6 %convolution_add_fusion = f32[8,64,32]{1,2,0:T(8,128)S(1)} fusion(f32[8,64,32]{1,2,0:T(8,128)} %fusion.4, f32[8,64,128]{2,1,0:T(8,128)} %bitcast.57, f32[8,64,32]{1,2,0:T(8,128)} %copy.47, f32[8,64,32]{1,2,0:T(8,128)} %copy.50), kind=kOutput, calls=%fused_computation.1 | convolution fusion | flops 6324224 | bytes 589824 | tf_op jit(solution)/shard_map/srp,spq->srq/dot_general | solution.py:583
  106.9 1.4 %convolution_subtract_fusion = f32[8,64,32]{1,2,0:T(8,128)S(1)} fusion(f32[8,64,32]{1,2,0:T(8,128)S(1)} %convolution_add_fusion, f32[8,32,64]{2,1,0:T(8,128)S(1)} %fusion.14, f32[8,64,128]{2,1,0:T(8,128)} %bitcast.58), kind=kOutput, calls=%fused_computation | convolution fusion | flops 6307840 | bytes 327680 | tf_op jit(solution)/shard_map/srp,spq->srq/dot_general | solution.py:583
  110.2 1.7 %copy.40 = f32[8,32,64]{1,2,0:T(8,128)} copy(f32[8,32,64]{2,1,0:T(8,128)} %copy-done.33) | data formatting | bytes 131072 | tf_op jit(solution)/shard_map/rm,spm->srp/dot_general | solution.py:583
  113.7 1.6 %copy-done.1 = bf16[2,2,256,1024]{3,2,1,0:T(8,128)(2,1)S(1)} copy-done((bf16[2,2,256,1024]{3,2,1,0:T(8,128)(2,1)S(1)}, bf16[2,2,256,1024]{3,2,1,0:T(8,128)(2,1)}, u32[]{:S(2)}) %copy-start.1) | copy-done | bytes 2097176
  115.3 1.6 %copy-done.3 = bf16[2,2,256,1024]{3,2,1,0:T(8,128)(2,1)S(1)} copy-done((bf16[2,2,256,1024]{3,2,1,0:T(8,128)(2,1)S(1)}, bf16[2,2,256,1024]{3,2,1,0:T(8,128)(2,1)}, u32[]{:S(2)}) %copy-start.3) | copy-done | bytes 2097176
  116.9 1.6 %copy-done.5 = bf16[2,2,256,1024]{3,2,1,0:T(8,128)(2,1)S(1)} copy-done((bf16[2,2,256,1024]{3,2,1,0:T(8,128)(2,1)S(1)}, bf16[2,2,256,1024]{3,2,1,0:T(8,128)(2,1)}, u32[]{:S(2)}) %copy-start.5) | copy-done | bytes 2097176
  120.3 1.6 %shard_map.103 = (f32[64,1024]{1,0:T(8,128)S(1)}, f32[64,1024]{1,0:T(8,128)S(1)}) custom-call(f32[32,1024]{1,0:T(8,128)S(1)} %copy-done.13, f32[32,1024]{1,0:T(8,128)S(1)} %copy-done.15, f32[64,1024]{1,0:T(8,128)S(1)} %get-tuple-element.59.k_first, f32[64,1024]{1,0:T(8,128)S(1)} %get-tuple-element.60.k_second, ...), custom_call_target="tpu_custom_call", output_to_operand_aliasing={{0}: (9, {}), {1}: (10, {})} | custom-call | flops 1600000000 | tf_op jit(solution)/shard_map/pallas_call | solution.py:76
  123.9 1.3 collective-permute-start.22
  125.3 1.6 %collective-permute-done.22 = f32[64,128]{1,0:T(8,128)S(1)} collective-permute-done((f32[64,128]{1,0:T(8,128)S(1)}, f32[64,128]{1,0:T(8,128)S(1)}, u32[]{:S(2)}, u32[]{:S(2)}) %collective-permute-start.22) | collective-permute-done | bytes 32800 | tf_op jit(solution)/shard_map/ppermute | solution.py:424
  127.0 1.2 collective-permute-done.23.q_recv
  128.2 1.2 shard_map.111
  (146 shorter events, 20.8 us)
Async XLA Ops:
  0.0 5.1 %copy-start.37 = (f32[128,16]{0,1:T(8,128)S(1)}, f32[128,16]{0,1:T(8,128)}, u32[]{:S(2)}) copy-start(f32[128,16]{0,1:T(8,128)} %param.17) | copy-start | bytes 24580
  0.0 5.7 %copy-start.39 = (s32[1,32]{1,0:T(1,128)S(1)}, s32[1,32]{1,0:T(1,128)}, u32[]{:S(2)}) copy-start(s32[1,32]{1,0:T(1,128)} %param.13) | copy-start | bytes 388
  0.0 5.7 %copy-start.38 = (f32[1,32,32]{2,1,0:T(8,128)S(1)}, f32[1,32,32]{2,1,0:T(8,128)}, u32[]{:S(2)}) copy-start(f32[1,32,32]{2,1,0:T(8,128)} %param.14) | copy-start | bytes 12292
  0.0 11.8 %copy-start.30 = (s32[1,1,32]{2,1,0:T(1,128)S(1)}, s32[1,1,32]{2,1,0:T(1,128)}, u32[]{:S(2)}) copy-start(s32[1,1,32]{2,1,0:T(1,128)} %param.12) | copy-start | bytes 388
  0.0 11.8 %copy-start.31 = (f32[1,1,1024]{2,1,0:T(1,128)S(1)}, f32[1,1,1024]{2,1,0:T(1,128)}, u32[]{:S(2)}) copy-start(f32[1,1,1024]{2,1,0:T(1,128)} %param.11) | copy-start | bytes 12292
  4.0 12.4 %copy-start.6 = (f32[256,1024]{1,0:T(8,128)}, f32[256,1024]{1,0:T(8,128)S(1)}, u32[]{:S(2)}) copy-start(f32[256,1024]{1,0:T(8,128)S(1)} %get-tuple-element.46.refs_6_.own) | copy-start | bytes 3145732
  4.0 31.7 %collective-permute-start.2 = (f32[256,1024]{1,0:T(8,128)S(1)}, f32[256,1024]{1,0:T(8,128)S(1)}, u32[]{:S(2)}, u32[]{:S(2)}) collective-permute-start(f32[256,1024]{1,0:T(8,128)S(1)} %get-tuple-element.46.refs_6_.own), channel_id=1, source_target_pairs={{0,1},{1,0},{2,3},{3,2},{4,5},{5,4},{6,7},{7,6},{8,9},{9,8},{10,11... | collective-permute-start | bytes 3145736 | tf_op jit(solution)/shard_map/ppermute | solution.py:421
  4.5 34.9 %collective-permute-start.3 = (f32[256,1024]{1,0:T(8,128)}, f32[256,1024]{1,0:T(8,128)}, u32[]{:S(2)}, u32[]{:S(2)}) collective-permute-start(f32[256,1024]{1,0:T(8,128)} %get-tuple-element.47.refs_7_.own), channel_id=1, source_target_pairs={{0,1},{1,0},{2,3},{3,2},{4,5},{5,4},{6,7},{7,6},{8,9},{9,8},{10,11... | collective-permute-start | bytes 3145736 | tf_op jit(solution)/shard_map/ppermute | solution.py:421
  4.6 36.7 %collective-permute-start.4 = (f32[256,1024]{1,0:T(8,128)}, f32[256,1024]{1,0:T(8,128)}, u32[]{:S(2)}, u32[]{:S(2)}) collective-permute-start(f32[256,1024]{1,0:T(8,128)} %get-tuple-element.48.refs_8_.own), channel_id=1, source_target_pairs={{0,1},{1,0},{2,3},{3,2},{4,5},{5,4},{6,7},{7,6},{8,9},{9,8},{10,11... | collective-permute-start | bytes 3145736 | tf_op jit(solution)/shard_map/ppermute | solution.py:421
  5.0 38.9 %collective-permute-start.1 = (f32[256,1024]{1,0:T(8,128)}, f32[256,1024]{1,0:T(8,128)}, u32[]{:S(2)}, u32[]{:S(2)}) collective-permute-start(f32[256,1024]{1,0:T(8,128)} %get-tuple-element.45.refs_5_.own), channel_id=1, source_target_pairs={{0,1},{1,0},{2,3},{3,2},{4,5},{5,4},{6,7},{7,6},{8,9},{9,8},{10,11... | collective-permute-start | bytes 3145736 | tf_op jit(solution)/shard_map/ppermute | solution.py:421
  6.9 9.4 %collective-permute-start.19 = (f32[56,128]{1,0:T(8,128)S(1)}, f32[56,128]{1,0:T(8,128)S(1)}, u32[]{:S(2)}, u32[]{:S(2)}) collective-permute-start(f32[56,128]{1,0:T(8,128)S(1)} %pad_maximum_fusion.5), channel_id=1, source_target_pairs={{0,4},{1,5},{4,0},{5,1},{8,12},{9,13},{12,8},{13,9},{16,20},{17,21... | collective-permute-start | bytes 86024 | tf_op jit(solution)/shard_map/ppermute | solution.py:435
  16.3 6.1 %collective-permute-start.20 = (f32[112,128]{1,0:T(8,128)S(1)}, f32[112,128]{1,0:T(8,128)S(1)}, u32[]{:S(2)}, u32[]{:S(2)}) collective-permute-start(f32[112,128]{1,0:T(8,128)S(1)} %pad_maximum_fusion.3), channel_id=1, source_target_pairs={{0,8},{1,9},{4,12},{5,13},{8,0},{9,1},{12,4},{13,5},{16,24},{17,25... | collective-permute-start | bytes 172040 | tf_op jit(solution)/shard_map/ppermute | solution.py:435
  23.1 9.3 %collective-permute-start.21 = (f32[224,128]{1,0:T(8,128)}, f32[224,128]{1,0:T(8,128)}, u32[]{:S(2)}, u32[]{:S(2)}) collective-permute-start(f32[224,128]{1,0:T(8,128)} %get-tuple-element.87), channel_id=1, source_target_pairs={{0,16},{1,17},{4,20},{5,21},{8,24},{9,25},{12,28},{13,29},{16,0},{... | collective-permute-start | bytes 344072 | tf_op jit(solution)/shard_map/ppermute | solution.py:435
  32.3 3.2 %collective-permute-start = (f32[136,1024]{1,0:T(8,128)S(1)}, f32[136,1024]{1,0:T(8,128)S(1)}, u32[]{:S(2)}, u32[]{:S(2)}) collective-permute-start(f32[136,1024]{1,0:T(8,128)S(1)} %get-tuple-element.50), channel_id=1, source_target_pairs={{0,1},{1,0},{2,3},{3,2},{4,5},{5,4},{6,7},{7,6},{8,9},{9,8},{10,11... | collective-permute-start | bytes 1671176 | tf_op jit(solution)/shard_map/ppermute | solution.py:421
  41.3 51.4 %copy-start = (bf16[2,2,256,1024]{3,2,1,0:T(8,128)(2,1)}, bf16[2,2,256,1024]{3,2,1,0:T(8,128)(2,1)S(1)}, u32[]{:S(2)}) copy-start(bf16[2,2,256,1024]{3,2,1,0:T(8,128)(2,1)S(1)} %shard_map.95.refs_2_.refs_3_) | copy-start | bytes 6291460
  43.9 48.8 %copy-start.2 = (bf16[2,2,256,1024]{3,2,1,0:T(8,128)(2,1)}, bf16[2,2,256,1024]{3,2,1,0:T(8,128)(2,1)S(1)}, u32[]{:S(2)}) copy-start(bf16[2,2,256,1024]{3,2,1,0:T(8,128)(2,1)S(1)} %shard_map.96.refs_3_.refs_4_) | copy-start | bytes 6291460
  46.5 46.2 %copy-start.4 = (bf16[2,2,256,1024]{3,2,1,0:T(8,128)(2,1)}, bf16[2,2,256,1024]{3,2,1,0:T(8,128)(2,1)S(1)}, u32[]{:S(2)}) copy-start(bf16[2,2,256,1024]{3,2,1,0:T(8,128)(2,1)S(1)} %shard_map.93.refs_0_.refs_1_) | copy-start | bytes 6291460
  47.4 7.4 %collective-permute-start.10 = (f32[32,1024]{1,0:T(8,128)S(1)}, f32[32,1024]{1,0:T(8,128)S(1)}, u32[]{:S(2)}, u32[]{:S(2)}) collective-permute-start(f32[32,1024]{1,0:T(8,128)S(1)} %get-tuple-element.67.f_second.refs_5_), channel_id=1, source_target_pairs={{0,2},{1,3},{4,6},{5,7},{8,10},{9,11},{12,14},{13,15},{16,18},{17,... | collective-permute-start | bytes 393224 | tf_op jit(solution)/shard_map/ppermute | solution.py:424
  49.5 6.6 %collective-permute-start.5 = (f32[32,1024]{1,0:T(8,128)S(1)}, f32[32,1024]{1,0:T(8,128)S(1)}, u32[]{:S(2)}, u32[]{:S(2)}) collective-permute-start(f32[32,1024]{1,0:T(8,128)S(1)} %get-tuple-element.52.f_second.refs_1_), channel_id=1, source_target_pairs={{0,2},{1,3},{4,6},{5,7},{8,10},{9,11},{12,14},{13,15},{16,18},{17,... | collective-permute-start | bytes 393224 | tf_op jit(solution)/shard_map/ppermute | solution.py:424
  53.4 7.8 %collective-permute-start.8 = (f32[64,1024]{1,0:T(8,128)S(1)}, f32[64,1024]{1,0:T(8,128)S(1)}, u32[]{:S(2)}, u32[]{:S(2)}) collective-permute-start(f32[64,1024]{1,0:T(8,128)S(1)} %get-tuple-element.61), channel_id=1, source_target_pairs={{0,2},{1,3},{4,6},{5,7},{8,10},{9,11},{12,14},{13,15},{16,18},{17,... | collective-permute-start | bytes 786440 | tf_op jit(solution)/shard_map/ppermute | solution.py:424
  54.8 7.8 %collective-permute-start.11 = (f32[32,1024]{1,0:T(8,128)S(1)}, f32[32,1024]{1,0:T(8,128)S(1)}, u32[]{:S(2)}, u32[]{:S(2)}) collective-permute-start(f32[32,1024]{1,0:T(8,128)S(1)} %get-tuple-element.68.refs_4_.refs_6_), channel_id=1, source_target_pairs={{2,0},{3,1},{6,4},{7,5},{10,8},{11,9},{14,12},{15,13},{18,16},{19,... | collective-permute-start | bytes 393224 | tf_op jit(solution)/shard_map/ppermute | solution.py:427
  56.1 15.3 %collective-permute-start.6 = (f32[32,1024]{1,0:T(8,128)S(1)}, f32[32,1024]{1,0:T(8,128)S(1)}, u32[]{:S(2)}, u32[]{:S(2)}) collective-permute-start(f32[32,1024]{1,0:T(8,128)S(1)} %get-tuple-element.53.refs_4_), channel_id=1, source_target_pairs={{2,0},{3,1},{6,4},{7,5},{10,8},{11,9},{14,12},{15,13},{18,16},{19,... | collective-permute-start | bytes 393224 | tf_op jit(solution)/shard_map/ppermute | solution.py:427
  61.3 14.6 %collective-permute-start.15 = (f32[40,1024]{1,0:T(8,128)S(1)}, f32[40,1024]{1,0:T(8,128)S(1)}, u32[]{:S(2)}, u32[]{:S(2)}) collective-permute-start(f32[40,1024]{1,0:T(8,128)S(1)} %get-tuple-element.82), channel_id=1, source_target_pairs={{2,0},{3,1},{6,4},{7,5},{10,8},{11,9},{14,12},{15,13},{18,16},{19,... | collective-permute-start | bytes 491528 | tf_op jit(solution)/shard_map/ppermute | solution.py:427
  65.7 13.5 %copy-start.24 = (f32[32,1024]{1,0:T(8,128)}, f32[32,1024]{1,0:T(8,128)S(1)}, u32[]{:S(2)}) copy-start(f32[32,1024]{1,0:T(8,128)S(1)} %get-tuple-element.70.v_first.refs_4_) | copy-start | bytes 393220
  65.7 13.5 %copy-start.26 = (f32[32,1024]{1,0:T(8,128)}, f32[32,1024]{1,0:T(8,128)S(1)}, u32[]{:S(2)}) copy-start(f32[32,1024]{1,0:T(8,128)S(1)} %get-tuple-element.71.v_second.refs_5_) | copy-start | bytes 393220
  65.7 13.4 %collective-permute-start.12 = (f32[32,1024]{1,0:T(8,128)S(1)}, f32[32,1024]{1,0:T(8,128)S(1)}, u32[]{:S(2)}, u32[]{:S(2)}) collective-permute-start(f32[32,1024]{1,0:T(8,128)S(1)} %get-tuple-element.73.f_second.refs_7_), channel_id=1, source_target_pairs={{0,2},{1,3},{4,6},{5,7},{8,10},{9,11},{12,14},{13,15},{16,18},{17,... | collective-permute-start | bytes 393224 | tf_op jit(solution)/shard_map/ppermute | solution.py:424
  74.6 4.6 %copy-start.12 = (f32[32,1024]{1,0:T(8,128)}, f32[32,1024]{1,0:T(8,128)S(1)}, u32[]{:S(2)}) copy-start(f32[32,1024]{1,0:T(8,128)S(1)} %get-tuple-element.57.f_first.refs_2_) | copy-start | bytes 393220
  74.6 4.6 %copy-start.14 = (f32[32,1024]{1,0:T(8,128)}, f32[32,1024]{1,0:T(8,128)S(1)}, u32[]{:S(2)}) copy-start(f32[32,1024]{1,0:T(8,128)S(1)} %get-tuple-element.58.f_second.refs_3_) | copy-start | bytes 393220
  74.6 10.5 %copy-start.16 = (f32[32,1024]{1,0:T(8,128)}, f32[32,1024]{1,0:T(8,128)S(1)}, u32[]{:S(2)}) copy-start(f32[32,1024]{1,0:T(8,128)S(1)} %get-tuple-element.55.v_first.refs_0_) | copy-start | bytes 393220
  74.6 10.5 %copy-start.18 = (f32[32,1024]{1,0:T(8,128)}, f32[32,1024]{1,0:T(8,128)S(1)}, u32[]{:S(2)}) copy-start(f32[32,1024]{1,0:T(8,128)S(1)} %get-tuple-element.56.v_second.refs_1_) | copy-start | bytes 393220
  74.6 10.5 %collective-permute-start.7 = (f32[32,1024]{1,0:T(8,128)S(1)}, f32[32,1024]{1,0:T(8,128)S(1)}, u32[]{:S(2)}, u32[]{:S(2)}) collective-permute-start(f32[32,1024]{1,0:T(8,128)S(1)} %get-tuple-element.58.f_second.refs_3_), channel_id=1, source_target_pairs={{0,2},{1,3},{4,6},{5,7},{8,10},{9,11},{12,14},{13,15},{16,18},{17,... | collective-permute-start | bytes 393224 | tf_op jit(solution)/shard_map/ppermute | solution.py:424
  76.7 5.8 %collective-permute-start.16 = (f32[64,128]{1,0:T(8,128)S(1)}, f32[64,128]{1,0:T(8,128)S(1)}, u32[]{:S(2)}, u32[]{:S(2)}) collective-permute-start(f32[64,128]{1,0:T(8,128)S(1)} %shard_map.110), channel_id=1, source_target_pairs={{0,4},{1,5},{4,0},{5,1},{8,12},{9,13},{12,8},{13,9},{16,20},{17,21... | collective-permute-start | bytes 98312 | tf_op jit(solution)/shard_map/ppermute | solution.py:435
  79.2 13.4 %collective-permute-start.13 = (f32[32,1024]{1,0:T(8,128)S(1)}, f32[32,1024]{1,0:T(8,128)S(1)}, u32[]{:S(2)}, u32[]{:S(2)}) collective-permute-start(f32[32,1024]{1,0:T(8,128)S(1)} %get-tuple-element.74.refs_4_), channel_id=1, source_target_pairs={{2,0},{3,1},{6,4},{7,5},{10,8},{11,9},{14,12},{15,13},{18,16},{19,... | collective-permute-start | bytes 393224 | tf_op jit(solution)/shard_map/ppermute | solution.py:427
  82.5 6.1 %collective-permute-start.17 = (f32[128,128]{1,0:T(8,128)S(1)}, f32[128,128]{1,0:T(8,128)S(1)}, u32[]{:S(2)}, u32[]{:S(2)}) collective-permute-start(f32[128,128]{1,0:T(8,128)S(1)} %pad_maximum_fusion.2), channel_id=1, source_target_pairs={{0,8},{1,9},{4,12},{5,13},{8,0},{9,1},{12,4},{13,5},{16,24},{17,25... | collective-permute-start | bytes 196616 | tf_op jit(solution)/shard_map/ppermute | solution.py:435
  85.2 9.4 %copy-start.10 = (f32[64,1024]{1,0:T(8,128)}, f32[64,1024]{1,0:T(8,128)S(1)}, u32[]{:S(2)}) copy-start(f32[64,1024]{1,0:T(8,128)S(1)} %get-tuple-element.63.refs_5_) | copy-start | bytes 786436
  85.2 28.5 %collective-permute-start.9 = (f32[64,1024]{1,0:T(8,128)S(1)}, f32[64,1024]{1,0:T(8,128)S(1)}, u32[]{:S(2)}, u32[]{:S(2)}) collective-permute-start(f32[64,1024]{1,0:T(8,128)S(1)} %get-tuple-element.62.refs_4_), channel_id=1, source_target_pairs={{2,0},{3,1},{6,4},{7,5},{10,8},{11,9},{14,12},{15,13},{18,16},{19,... | collective-permute-start | bytes 786440 | tf_op jit(solution)/shard_map/ppermute | solution.py:427
  88.7 9.2 %collective-permute-start.18 = (f32[256,128]{1,0:T(8,128)S(1)}, f32[256,128]{1,0:T(8,128)S(1)}, u32[]{:S(2)}, u32[]{:S(2)}) collective-permute-start(f32[256,128]{1,0:T(8,128)S(1)} %pad_maximum_fusion.1), channel_id=1, source_target_pairs={{0,16},{1,17},{4,20},{5,21},{8,24},{9,25},{12,28},{13,29},{16,0},{... | collective-permute-start | bytes 393224 | tf_op jit(solution)/shard_map/ppermute | solution.py:435
  92.7 5.2 %copy-start.35 = (f32[448,128]{1,0:T(8,128)S(1)}, f32[448,128]{1,0:T(8,128)}, u32[]{:S(2)}) copy-start(f32[448,128]{1,0:T(8,128)} %copy-done.34) | copy-start | bytes 688132
  94.5 3.4 %copy-start.20 = (f32[32,1024]{1,0:T(8,128)}, f32[32,1024]{1,0:T(8,128)S(1)}, u32[]{:S(2)}) copy-start(f32[32,1024]{1,0:T(8,128)S(1)} %get-tuple-element.76.refs_6_) | copy-start | bytes 393220
  94.5 4.6 %copy-start.22 = (f32[32,1024]{1,0:T(8,128)}, f32[32,1024]{1,0:T(8,128)S(1)}, u32[]{:S(2)}) copy-start(f32[32,1024]{1,0:T(8,128)S(1)} %get-tuple-element.77.refs_7_) | copy-start | bytes 393220
  99.1 12.8 %slice-start = ((f32[8,64,32]{1,2,0:T(8,128)}), f32[1,64,32]{1,2,0:T(8,128)S(1)}, s32[]{:S(2)}) async-start(f32[8,64,32]{1,2,0:T(8,128)} %fusion.4), calls=%async_computation | async-start | bytes 32768 | tf_op jit(solution)/shard_map/slice | solution.py:596
  99.1 14.5 %copy-start.11 = (f32[64,1024]{1,0:T(8,128)S(1)}, f32[64,1024]{1,0:T(8,128)}, u32[]{:S(2)}) copy-start(f32[64,1024]{1,0:T(8,128)} %copy-done.10) | copy-start | bytes 786436
  120.3 2.7 %copy-start.36 = (f32[1,64,32]{2,1,0:T(8,128)S(1)}, f32[1,64,32]{2,1,0:T(8,128)}, u32[]{:S(2)}) copy-start(f32[1,64,32]{2,1,0:T(8,128)} %copy.49) | copy-start | bytes 24580
  121.9 6.3 %copy-start.28 = (f32[1,1,32,1024]{3,2,1,0:T(8,128)S(1)}, f32[1,1,32,1024]{3,2,1,0:T(8,128)}, u32[]{:S(2)}) copy-start(f32[1,1,32,1024]{3,2,1,0:T(8,128)} %param.15) | copy-start | bytes 393220
  121.9 6.3 %copy-start.29 = (f32[1,1,32,1024]{3,2,1,0:T(8,128)S(1)}, f32[1,1,32,1024]{3,2,1,0:T(8,128)}, u32[]{:S(2)}) copy-start(f32[1,1,32,1024]{3,2,1,0:T(8,128)} %param.16) | copy-start | bytes 393220
  122.1 6.1 %collective-permute-start.14 = (f32[96,1024]{1,0:T(8,128)S(1)}, f32[96,1024]{1,0:T(8,128)S(1)}, u32[]{:S(2)}, u32[]{:S(2)}) collective-permute-start(f32[96,1024]{1,0:T(8,128)S(1)} %get-tuple-element.79), channel_id=1, source_target_pairs={{0,1},{1,0},{2,3},{3,2},{4,5},{5,4},{6,7},{7,6},{8,9},{9,8},{10,11... | collective-permute-start | bytes 1179656 | tf_op jit(solution)/shard_map/ppermute | solution.py:421
  123.9 2.9 %collective-permute-start.22 = (f32[64,128]{1,0:T(8,128)S(1)}, f32[64,128]{1,0:T(8,128)S(1)}, u32[]{:S(2)}, u32[]{:S(2)}) collective-permute-start(f32[64,128]{1,0:T(8,128)S(1)} %pad_maximum_fusion.4), channel_id=1, source_target_pairs={{0,2},{1,3},{4,6},{5,7},{8,10},{9,11},{12,14},{13,15},{16,18},{17,... | collective-permute-start | bytes 98312 | tf_op jit(solution)/shard_map/ppermute | solution.py:424
  126.9 1.3 collective-permute-start.23
  (17 other events, 24.5 us)

commit v3 on v2

--- a/solution.py
+++ b/solution.py
@@ -10,10 +10,10 @@
 
 f32 = jnp.float32
 bf16 = jnp.bfloat16
-highest = lax.Precision.HIGHEST
 LANES = 128
 BLOCKS = 2
 PIECES = 4
+PARTS = 1
 
 
 def halves(x):
@@ -67,7 +67,7 @@
     return pl.BlockSpec(memory_space=space)
 
 
-def call(body, outs, args, work, aliases=None, scratch=(), hbm=()):
+def call(body, outs, args, work, aliases=None, scratch=(), hbm=(), limit=None):
     specs = [spec(pltpu.VMEM) for _ in args]
     args = list(args)
     for place in hbm:
@@ -81,7 +81,7 @@
         input_output_aliases=aliases or {},
         scratch_shapes=list(scratch),
         cost_estimate=pl.CostEstimate(flops=int(work * 8e8), bytes_accessed=0, transcendentals=0),
-        compiler_params=pltpu.CompilerParams(vmem_limit_bytes=VMEM_LIMIT),
+        compiler_params=pltpu.CompilerParams(vmem_limit_bytes=limit or VMEM_LIMIT),
     )(*args)
 
 
@@ -104,23 +104,24 @@
             new[...] = old[...]
 
 
-def load(matrix, *refs):
-    pieces, sems = refs[:PIECES], refs[PIECES]
-    step = pieces[0].shape[0]
-    copies = [
-        pltpu.make_async_copy(matrix.at[pl.ds(i * step, step)], piece, sems.at[i])
-        for i, piece in enumerate(pieces)
-    ]
-    for copy in copies:
-        copy.start()
-    for copy in copies:
-        copy.wait()
-
-
-def first_products(*refs):
-    vector, one, two, diagonal, index = refs[:5]
-    pieces = refs[5 : 5 + PIECES]
-    keep, send, x, total, sems = refs[5 + PIECES :]
+def fix(inverse, schur, maps, out):
+    share, prim = inverse.shape[1], schur.shape[0]
+    unit = lax.broadcasted_iota(jnp.int32, (share, share), 0) == lax.broadcasted_iota(
+        jnp.int32, (share, share), 1
+    )
+    unit = unit.astype(f32).astype(bf16)
+    top, low = halves(inverse[...])
+    rest = (inverse[...] - top.astype(f32) - low.astype(f32)).astype(bf16)
+    out[:share, :] = dot_rows(unit, top) + dot_rows(unit, low) + dot_rows(unit, rest)
+    out[share : share + prim, :] = jnp.zeros_like(out[share : share + prim, :])
+    out[share : share + prim, :prim] = schur[...]
+    out[share + prim :, :] = jnp.full_like(out[share + prim :, :], -1.0)
+    out[share + prim : share + prim + 1, :prim] = maps[...].astype(f32)
+
+
+def first_products(matrix, vector, one, two, diagonal, index, own, keep, send, buffer, x, total, sems):
+    size = matrix.shape[0]
+    step = size // PIECES
     rows, prim = vector.shape[0], one.shape[0]
     extra = 2 * prim
     copies = [
@@ -128,15 +129,24 @@
         pltpu.make_async_copy(one, x.at[pl.ds(rows, prim)], sems.at[1]),
         pltpu.make_async_copy(two, x.at[pl.ds(rows + prim, prim)], sems.at[2]),
     ]
-    for copy in copies:
+    pieces = [
+        pltpu.make_async_copy(
+            matrix.at[pl.ds(i * step, step)], buffer.at[pl.ds(i * step, step)], sems.at[3 + i]
+        )
+        for i in range(PIECES)
+    ]
+    for copy in copies + pieces:
         copy.start()
     for copy in copies:
         copy.wait()
     x[rows:, :] = x[rows:, :] * diagonal[...]
-    step = pieces[0].shape[0]
-    for i, piece in enumerate(pieces):
-        top, low = halves(piece[...])
-        part = three(x[:, i * step : (i + 1) * step], top, low)
+    for i, copy in enumerate(pieces):
+        cols = pl.ds(i * step, step)
+        copy.wait()
+        top, low = halves(buffer[cols, :])
+        own[0, cols, :] = top
+        own[1, cols, :] = low
+        part = three(x[:, cols], own[0, cols, :], own[1, cols, :])
         if i == 0:
             total[...] = part
         else:
@@ -151,12 +161,24 @@
         out[half + extra + 1 : half + extra + 2, :prim] = index[...].astype(f32)
 
 
-def split(own, oth, weights):
+def split(matrix, own, weights, buffer, sems):
+    step = matrix.shape[0] // PIECES
+    pieces = [
+        pltpu.make_async_copy(
+            matrix.at[pl.ds(i * step, step)], buffer.at[pl.ds(i * step, step)], sems.at[i]
+        )
+        for i in range(PIECES)
+    ]
+    for copy in pieces:
+        copy.start()
     here = member()
-    for which, piece in ((here, own), (1 - here, oth)):
-        top, low = halves(piece[...])
-        weights[which, 0] = top
-        weights[which, 1] = low
+    weights[here] = own[...]
+    for i, copy in enumerate(pieces):
+        cols = pl.ds(i * step, step)
+        copy.wait()
+        top, low = halves(buffer[cols, :])
+        weights[1 - here, 0, cols, :] = top
+        weights[1 - here, 1, cols, :] = low
 
 
 def diagonals(keep, recv):
@@ -165,7 +187,7 @@
 
 
 def start_chain(keep, recv, *refs):
-    weights, (f_first, f_second) = refs[:PIECES], refs[PIECES:]
+    weights, (f_first, f_second) = refs[:PARTS], refs[PARTS:]
     rows = f_first.shape[0]
 
     @pl.when(pair() == 0)
@@ -176,7 +198,7 @@
 
 
 def start_last(keep, recv, *refs):
-    weights, (f_first, f_second, k_first, k_second) = refs[:PIECES], refs[PIECES:]
+    weights, (f_first, f_second, k_first, k_second) = refs[:PARTS], refs[PARTS:]
     rows, extra = f_first.shape[0], k_first.shape[0]
     stop = keep.shape[0] - 8
 
@@ -192,7 +214,7 @@
 
 
 def top_one(at, keep, recv, carried, *refs):
-    weights, (n_first, n_second) = refs[:PIECES], refs[PIECES:]
+    weights, (n_first, n_second) = refs[:PARTS], refs[PARTS:]
     rows = n_first.shape[0]
 
     @pl.when(pair() == 1)
@@ -205,7 +227,7 @@
 
 
 def top_two(with_basis, keep, recv, v_first, v_second, carried, *refs):
-    riding, weights, (n_first, n_second) = refs[0], refs[1 : 1 + PIECES], refs[1 + PIECES :]
+    riding, weights, (n_first, n_second) = refs[0], refs[1 : 1 + PARTS], refs[1 + PARTS :]
     rows = v_first.shape[0]
     few = riding.shape[0] // 2
     extra = 2 * few
@@ -237,8 +259,8 @@
 
 
 def turn(keep, recv, f_first, f_second, carried, *refs):
-    weights, old = refs[:PIECES], refs[PIECES : PIECES + 2]
-    n_first, n_second, g_first, g_second = refs[PIECES + 2 :]
+    weights, old = refs[:PARTS], refs[PARTS : PARTS + 2]
+    n_first, n_second, g_first, g_second = refs[PARTS + 2 :]
 
     @pl.when(pair() == 0)
     def _():
@@ -254,7 +276,7 @@
 
 
 def back(with_basis, f_first, f_second, k_first, k_second, carried, *refs):
-    weights, old, (n_first, n_second) = refs[:PIECES], refs[PIECES : PIECES + 2], refs[PIECES + 2 :]
+    weights, old, (n_first, n_second) = refs[:PARTS], refs[PARTS : PARTS + 2], refs[PARTS + 2 :]
     few = k_first.shape[0] // 2
 
     @pl.when(pair() == 0)
@@ -270,7 +292,7 @@
 
 
 def adjoint_start(own_spots, oth_spots, k_second, *refs):
-    weights, (y_first, y_second, sent) = refs[:PIECES], refs[PIECES:]
+    weights, (y_first, y_second, sent) = refs[:PARTS], refs[PARTS:]
     prim = y_first.shape[0]
 
     @pl.when(pair() == 0)
@@ -323,7 +345,7 @@
 
 
 def adjoint_top(width, keep, recv, own_spots, oth_spots, carried, *refs):
-    weights, refs = refs[:PIECES], refs[PIECES:]
+    weights, refs = refs[:PARTS], refs[PARTS:]
     blocks, old, (y_first, y_second, sent) = refs[: 2 * BLOCKS], refs[2 * BLOCKS : -3], refs[-3:]
     prim = y_first.shape[0]
 
@@ -388,6 +410,88 @@
             2.0 * a1[...] - a2[:rows, :], 2.0 * b1[...] - b2[:rows, :]
         )
     keep[BLOCKS * rows :, :], send[BLOCKS * rows :, :] = pick(blocks[2][rows:, :], blocks[3][rows:, :])
+
+
+def wide(x, rows):
+    return jnp.concatenate([x, jnp.zeros((rows - x.shape[0], x.shape[1]), f32)], axis=0)
+
+
+def solve(subs, prim, values, fixed, q):
+    half, width = q.shape
+    count = fixed.shape[1]
+    height = fixed.shape[0] // subs
+    share = height - prim - 8
+    me = lax.axis_index("sub")
+    unknown = lax.broadcasted_iota(jnp.int32, (count, width), 0)
+    there = ((unknown // share) ^ me) * share + unknown % share
+    unknown, there = unknown.astype(f32), there.astype(f32)
+    lane = lax.broadcasted_iota(jnp.int32, (half, width), 1)
+
+    def at(ref, j, size, start=0, stop=None):
+        stop = size if stop is None else stop
+        base = j * size + start
+        if not isinstance(base, int):
+            base = pl.multiple_of(base, 8)
+        return ref[pl.ds(base, stop - start), :]
+
+    def loop(body, begin):
+        if subs <= 8:
+            for j in range(subs):
+                begin = body(j, begin)
+            return begin
+        return lax.fori_loop(0, subs, body, begin)
+
+    def times_rows(left, right):
+        top, low = halves(right)
+        return three(left, top, low, dot_rows)
+
+    def times_plain(left, right):
+        top, low = halves(right)
+        return three(left, top, low)
+
+    def map_of(j):
+        return at(fixed, j, height, share + prim, height)[0:1, :width]
+
+    def spot(row, ids):
+        return (ids == row).astype(f32)
+
+    def add_first(j, total):
+        return total + times_rows(at(values, j, half), spot(map_of(j), unknown))
+
+    inverse = jnp.concatenate([at(fixed, j, height, 0, share) for j in range(subs)], axis=0)
+    zero = jnp.zeros((half, count), f32)
+    found = times_rows(loop(add_first, zero), inverse)
+
+    def parts(j):
+        v = at(values, j, half)
+        row = map_of(j)
+        schur = at(fixed, j, height, share, share + prim)[:, :width]
+        multiplier = times_plain(v, wide(schur, width))
+        picked = times_plain(found, spot(row, there))
+        change = times_plain(multiplier, wide(v[:prim], width)) - times_plain(
+            picked, wide(v[prim : 2 * prim], width)
+        )
+        return row, schur, multiplier, picked, jnp.where(lane < 2 * prim, v, change)
+
+    def add_second(j, total):
+        row, _, _, _, p = parts(j)
+        signs = (
+            spot(row, unknown)
+            - spot(pltpu.roll(row, prim, 1), unknown)
+            + spot(pltpu.roll(row, 2 * prim, 1), unknown)
+        )
+        return total + times_rows(p, signs)
+
+    found_two = times_rows(loop(add_second, zero), inverse)
+    row, schur, multiplier, picked, p = parts(0)
+    multiplier_two = times_plain(p, wide(jnp.concatenate([schur, -schur, schur], axis=0), width))
+    picked_two = times_plain(found_two, spot(row, there))
+    q[...] = (
+        pltpu.roll(picked, prim, 1)
+        - multiplier
+        - pltpu.roll(multiplier + multiplier_two, 2 * prim, 1)
+        + pltpu.roll(picked + picked_two, 3 * prim, 1)
+    )
 
 
 def finish(keep, recv, q_keep, q_recv, one, two, out):
@@ -415,7 +519,6 @@
     levels = lax.axis_size("slab")
     subs = lax.axis_size("sub")
     assert levels == 4 and subs & (subs - 1) == 0
-    sub = lax.axis_index("sub")
 
     def swap(x):
         return lax.ppermute(x, "slab", [(i, i ^ 1) for i in range(levels)])
@@ -448,49 +551,43 @@
     extra = 2 * prim
     width = -(-3 * prim // LANES) * LANES
     packed = -(-half * width // (8 * size)) * 8
-    step = size // PIECES
-    assert half == extra and prim <= coarse_count and size % width == 0
+    assert half == extra and prim <= coarse_count and size % width == 0 and 4 * prim <= width
 
     def like(count, *heights):
         return [struct((h, size)) for h in heights for _ in range(count)]
 
-    own = call(load, like(PIECES, step), [matrix], 1, scratch=[pltpu.SemaphoreType.DMA((PIECES,))], hbm=(0,))
-    oth = [swap(piece) for piece in own]
-
-    fixed = jnp.concatenate(
-        [
-            coarse_inverse.T,
-            jnp.pad(schur_small[0], ((0, 0), (0, coarse_count - prim))),
-            jnp.pad(coarse_map.astype(f32), ((0, 7), (0, coarse_count - prim))),
-        ],
-        axis=0,
-    )
-    fixed = gather(fixed).reshape(subs, share + prim + 8, coarse_count)
-    inverse_rows = fixed[:, :share].reshape(coarse_count, coarse_count)
-    schur = fixed[:, share : share + prim, :prim]
-    maps = fixed[:, share + prim, :prim]
-    order = jnp.arange(subs, dtype=jnp.int32) ^ sub
-    columns = (order[:, None] * share + jnp.arange(share, dtype=jnp.int32)).reshape(-1).astype(f32)
-    onehot = (maps[:, :, None] == jnp.arange(coarse_count, dtype=jnp.int32).astype(f32)).astype(f32)
-    onehot_there = (maps[:, :, None] == columns).astype(f32)
-
-    keep, send = call(
+    other_matrix = swap(matrix)
+
+    (fixed,) = call(
+        fix,
+        [struct((share + prim + 8, coarse_count))],
+        [coarse_inverse, schur_small[0], coarse_map],
+        0.1,
+    )
+    fixed = gather(fixed)
+
+    own, keep, send = call(
         first_products,
-        like(2, half + extra + 8),
-        [vector, one, two, diagonal[0], primal_index[0], *own],
+        [struct((2, size, size), bf16)] + like(2, half + extra + 8),
+        [matrix, vector, one, two, diagonal[0], primal_index[0]],
         2,
         scratch=[
+            pltpu.VMEM((size, size), f32),
             pltpu.VMEM((rows + extra, size), f32),
             pltpu.VMEM((rows + extra, size), f32),
-            pltpu.SemaphoreType.DMA((3,)),
+            pltpu.SemaphoreType.DMA((3 + PIECES,)),
         ],
-        hbm=(0, 1, 2),
+        hbm=(0, 1, 2, 3),
     )
     recv = swap(send)
-    weights = [
-        call(split, [struct((2, 2, step, size), bf16)], [own[i], oth[i]], 0.3)[0]
-        for i in range(PIECES)
-    ]
+    weights = call(
+        split,
+        [struct((2, 2, size, size), bf16)],
+        [other_matrix, own],
+        1,
+        scratch=[pltpu.VMEM((size, size), f32), pltpu.SemaphoreType.DMA((PIECES,))],
+        hbm=(0,),
+    )
     place = jnp.arange(size, dtype=jnp.int32)
     own_spots = (primal_index[0, 0][:, None] == place).astype(f32)
     oth_spots = (recv[half + extra + 1, :prim][:, None] == place.astype(f32)).astype(f32)
@@ -522,15 +619,6 @@
             )
         )
         carried[i] = fall(n[i][0])
-    y_first, y_second, sent = call(
-        functools.partial(adjoint_top, width),
-        like(2, prim) + like(1, prim + packed),
-        [keep, recv, own_spots, oth_spots, riding, *weights, *n[0], *n[1], y_first, y_second],
-        4,
-        aliases={5 + PIECES + 2 * BLOCKS: 0, 6 + PIECES + 2 * BLOCKS: 1},
-    )
-    z_back = fall(sent)
-
     n_one, g = [], []
     for i in span:
         turned = call(
@@ -538,11 +626,21 @@
             like(4, block),
             [keep, recv, *f[i], carried[i], *weights, *n[i]],
             4,
-            aliases={5 + PIECES: 0, 6 + PIECES: 1},
+            aliases={5 + PARTS: 0, 6 + PARTS: 1},
         )
         n_one.append(turned[:2])
         g.append(turned[2:])
         carried[i] = rise(g[i][1])
+        if i == 0:
+            passed = [x for j in span for x in (n_one[0] if j == 0 else n[j])]
+            y_first, y_second, sent = call(
+                functools.partial(adjoint_top, width),
+                like(2, prim) + like(1, prim + packed),
+                [keep, recv, own_spots, oth_spots, riding, *weights, *passed, y_first, y_second],
+                4,
+                aliases={5 + PARTS + 2 * BLOCKS: 0, 6 + PARTS + 2 * BLOCKS: 1},
+            )
+            z_back = fall(sent)
     pieces = []
     for i in span:
         pieces += [*f[i], *g[i]]
@@ -552,7 +650,7 @@
         [z_back, y_first, y_second, k_first, k_second, *pieces],
         1,
     )
-    values = gather(values).reshape(subs, half, width)
+    values = gather(values)
 
     n_two = []
     for i in span:
@@ -571,7 +669,7 @@
             like(2, block + prim if i == 0 else block),
             [*g[i], k_first, k_second, carried[i], *weights, *n_two[i]],
             2,
-            aliases={5 + PIECES: 0, 6 + PIECES: 1},
+            aliases={5 + PARTS: 0, 6 + PARTS: 1},
         )
     pieces = []
     for i in span:
@@ -579,29 +677,13 @@
     m_keep, m_send = call(settle, like(2, half + prim), pieces, 0.5)
     m_recv = swap(m_send)
 
-    def times_high(form, left, right):
-        return jnp.einsum(form, left, right, precision=highest, preferred_element_type=f32)
-
-    p_one = values[:, :, :prim]
-    p_defect = p_one - values[:, :, prim : 2 * prim]
-    x_one = values[:, :prim, 2 * prim : 3 * prim]
-    x_two = values[:, prim : 2 * prim, 2 * prim : 3 * prim]
-    sol = times_high("rn,mn->rm", times_high("srp,spn->rn", p_one, onehot), inverse_rows)
-    picked = times_high("rm,spm->srp", sol, onehot_there)
-    multiplier = times_high("srp,spq->srq", p_one, schur)
-    p_two = p_defect + times_high("srp,spq->srq", multiplier, x_one) - times_high(
-        "srp,spq->srq", picked, x_two
-    )
-    sol = times_high("rn,mn->rm", times_high("srp,spn->rn", p_two, onehot), inverse_rows)
-    q_one = jnp.concatenate([-multiplier[0], picked[0]], axis=1)
-    q_two = jnp.concatenate(
-        [
-            -times_high("rp,pq->rq", p_two[0], schur[0]),
-            times_high("rm,pm->rp", sol, onehot_there[0]),
-        ],
-        axis=1,
-    )
-    q = jnp.concatenate([q_one, q_one + q_two], axis=1)
+    (q,) = call(
+        functools.partial(solve, subs, prim),
+        [struct((half, width))],
+        [values, fixed],
+        0.5,
+        limit=VMEM_LIMIT + 8 * (values.size + fixed.size),
+    )
     q_upper = rise(q)
     q = jnp.where(pair() == 0, q, q_upper)
     q_recv = swap(q)

time: 131 us -> 88.5 us (0.68)
  local copies, waits for them, and re-layouts: 22.6 us -> 5.67 us
  matrix products: 9.63 us -> 0 us
  Pallas kernels: 31.7 us -> 25 us
  starting transfers between devices: 41.7 us -> 38.5 us
  waiting for transfers between devices: 20.8 us -> 18.2 us
  other arithmetic: 2 us -> 0.23 us
    unnamed x87 -> x21, local copies, waits for them, and re-layouts: 17.5 us -> 5.66 us
    dot_general x10 -> x0, matrix products: 9.63 us -> none  [times_high(): jnp.einsum(form, left, right, precision=highest, preferred_element_type=f32)]
    ppermute x5, waiting for transfers between devices: 0.03 us -> 6.89 us  [fall(): return lax.ppermute(x, 'slab', [(2, 0), (3, 1)])]
    pallas_call x21 -> x19, Pallas kernels: 31.7 us -> 25 us  [call(): pl.pallas_call(body, out_shape=outs, in_specs=specs, out_specs=[spec(pltp...]
    ppermute x6, waiting for transfers between devices: 14.2 us -> 8.47 us  [gather(): other = lax.ppermute(x, ('sub', 'slab'), pairs)]
    ppermute x6, starting transfers between devices: 12.3 us -> 8.09 us  [rise(): return lax.ppermute(x, 'slab', [(0, 2), (1, 3)])]
    ppermute x6, waiting for transfers between devices: 5.4 us -> 1.59 us  [rise(): return lax.ppermute(x, 'slab', [(0, 2), (1, 3)])]
    slice x5 -> x0, local copies, waits for them, and re-layouts: 1.76 us -> none  [the longest x1 0.91 us: on_device(): p_defect = p_one - values[:, :, prim:2 * prim]]
  transfers between devices with their start and end apart: 24 -> 21, of which waited for: 8 -> 9; matrix products, arithmetic and copies ran while one was open for 18% -> 0% of each run, Pallas kernels for 17% -> 27%
where the time goes in v3:
time: 88.5 us; the launch traced here: 88 us
  starting transfers between devices  38.5 us (44%)
  Pallas kernels  25 us (28%)
  waiting for transfers between devices  18.2 us (21%)
  local copies, waits for them, and re-layouts  5.67 us (6%)
    pallas_call x19, Pallas kernels, call(): pl.pallas_call(body, out_shape=outs, in_specs=specs, out_specs=[spec(pltp...  25 us
    ppermute x6, starting transfers between devices, gather(): other = lax.ppermute(x, ('sub', 'slab'), pairs)  23.3 us
    ppermute x6, waiting for transfers between devices, gather(): other = lax.ppermute(x, ('sub', 'slab'), pairs)  8.47 us
    ppermute x6, starting transfers between devices, rise(): return lax.ppermute(x, 'slab', [(0, 2), (1, 3)])  8.09 us
    ppermute x5, waiting for transfers between devices, fall(): return lax.ppermute(x, 'slab', [(2, 0), (3, 1)])  6.89 us
    ppermute x5, starting transfers between devices, fall(): return lax.ppermute(x, 'slab', [(2, 0), (3, 1)])  6.46 us
    unnamed x21, local copies, waits for them, and re-layouts  5.66 us
  transfers between devices with their start and end apart: 21, of which 9 were waited for; matrix products, arithmetic and copies ran while one was open for 0% of the time, Pallas kernels for 27%

profile of v3, /device:TPU:0, one launch (start us, length us, event | category | flops | bytes accessed | tf_op | source)
XLA Modules:
  0.0 88.0 jit_solution(6318389314292979322)
XLA Ops:
  0.0 0.6 collective-permute-start.1
  0.6 0.7 copy-done.4
  1.2 0.7 copy-done.7
  1.9 3.4 %shard_map.91 = (bf16[2,1024,1024]{2,1,0:T(8,128)(2,1)S(1)}, f32[136,1024]{1,0:T(8,128)S(1)}, f32[136,1024]{1,0:T(8,128)S(1)}) custom-call(f32[1024,1024]{1,0:T(8,128)} %bitcast.20, f32[128,1024]{1,0:T(8,128)} %bitcast.21, f32[32,1024]{1,0:T(8,128)} %bitcast.11, f32[32,1024]{1,0:T(8,128)} %bitcast.13, f32[1,1024]{1,0:T(1,128)S(1)} %bitcast.18, ...), custom_call_target="tpu_custom_call" | custom-call | flops 1600000000 | tf_op jit(solution)/shard_map/pallas_call | solution.py:76
  5.3 2.0 %copy-done = bf16[2,1024,1024]{2,1,0:T(8,128)(2,1)} copy-done((bf16[2,1024,1024]{2,1,0:T(8,128)(2,1)}, bf16[2,1024,1024]{2,1,0:T(8,128)(2,1)S(1)}, u32[]{:S(2)}) %copy-start) | copy-done | bytes 4194328
  7.3 0.1 copy.20.inverse
  7.5 0.1 shard_map.107
  7.6 4.9 %collective-permute-start.16 = (f32[56,128]{1,0:T(8,128)S(1)}, f32[56,128]{1,0:T(8,128)S(1)}, u32[]{:S(2)}, u32[]{:S(2)}) collective-permute-start(f32[56,128]{1,0:T(8,128)S(1)} %shard_map.107), channel_id=1, source_target_pairs={{0,4},{1,5},{4,0},{5,1},{8,12},{9,13},{12,8},{13,9},{16,20},{17,21... | collective-permute-start | bytes 86024 | tf_op jit(solution)/shard_map/ppermute | solution.py:538
  12.5 0.1 fusion.own_spots
  12.6 1.7 %collective-permute-done.16 = f32[56,128]{1,0:T(8,128)S(1)} collective-permute-done((f32[56,128]{1,0:T(8,128)S(1)}, f32[56,128]{1,0:T(8,128)S(1)}, u32[]{:S(2)}, u32[]{:S(2)}) %collective-permute-start.16) | collective-permute-done | bytes 28704 | tf_op jit(solution)/shard_map/ppermute | solution.py:538
  14.4 4.0 %collective-permute-start.17 = (f32[112,128]{1,0:T(8,128)S(1)}, f32[112,128]{1,0:T(8,128)S(1)}, u32[]{:S(2)}, u32[]{:S(2)}) collective-permute-start(f32[112,128]{1,0:T(8,128)S(1)} %pad_maximum_fusion.5), channel_id=1, source_target_pairs={{0,8},{1,9},{4,12},{5,13},{8,0},{9,1},{12,4},{13,5},{16,24},{17,25... | collective-permute-start | bytes 172040 | tf_op jit(solution)/shard_map/ppermute | solution.py:538
  18.4 2.1 %collective-permute-done.17 = f32[112,128]{1,0:T(8,128)S(1)} collective-permute-done((f32[112,128]{1,0:T(8,128)S(1)}, f32[112,128]{1,0:T(8,128)S(1)}, u32[]{:S(2)}, u32[]{:S(2)}) %collective-permute-start.17) | collective-permute-done | bytes 57376 | tf_op jit(solution)/shard_map/ppermute | solution.py:538
  20.5 4.9 %collective-permute-start.18 = (f32[224,128]{1,0:T(8,128)S(1)}, f32[224,128]{1,0:T(8,128)S(1)}, u32[]{:S(2)}, u32[]{:S(2)}) collective-permute-start(f32[224,128]{1,0:T(8,128)S(1)} %pad_maximum_fusion.3), channel_id=1, source_target_pairs={{0,16},{1,17},{4,20},{5,21},{8,24},{9,25},{12,28},{13,29},{16,0},{... | collective-permute-start | bytes 344072 | tf_op jit(solution)/shard_map/ppermute | solution.py:538
  25.6 2.2 %copy-done.1 = bf16[2,1024,1024]{2,1,0:T(8,128)(2,1)S(1)} copy-done((bf16[2,1024,1024]{2,1,0:T(8,128)(2,1)S(1)}, bf16[2,1024,1024]{2,1,0:T(8,128)(2,1)}, u32[]{:S(2)}) %copy-start.1) | copy-done | bytes 4194328
  27.8 2.3 %shard_map.92.refs_0_.refs_1_ = bf16[2,2,1024,1024]{3,2,1,0:T(8,128)(2,1)S(1)} custom-call(f32[1024,1024]{1,0:T(8,128)} %collective-permute-done.1.matrix, bf16[2,1024,1024]{2,1,0:T(8,128)(2,1)S(1)} %copy-done.1), custom_call_target="tpu_custom_call" | custom-call | flops 800000000 | tf_op jit(solution)/shard_map/pallas_call | solution.py:76
  30.1 0.8 shard_map.93
  31.0 1.3 %collective-permute-start.2 = (f32[32,1024]{1,0:T(8,128)S(1)}, f32[32,1024]{1,0:T(8,128)S(1)}, u32[]{:S(2)}, u32[]{:S(2)}) collective-permute-start(f32[32,1024]{1,0:T(8,128)S(1)} %get-tuple-element.46.f_second.refs_1_), channel_id=1, source_target_pairs={{0,2},{1,3},{4,6},{5,7},{8,10},{9,11},{12,14},{13,15},{16,18},{17,... | collective-permute-start | bytes 393224 | tf_op jit(solution)/shard_map/ppermute | solution.py:527
  32.3 0.9 %shard_map.96 = (f32[32,1024]{1,0:T(8,128)S(1)}, f32[32,1024]{1,0:T(8,128)S(1)}, f32[64,1024]{1,0:T(8,128)S(1)}, f32[64,1024]{1,0:T(8,128)S(1)}) custom-call(f32[136,1024]{1,0:T(8,128)S(1)} %get-tuple-element.42.keep, f32[136,1024]{1,0:T(8,128)S(1)} %collective-permute-done.recv, bf16[2,2,1024,1024]{3,2,1,0:T(8,128)(2,1)S(1)} %shard_map.92.refs_0_.refs_1_), custom_call_target="tpu_custom_call" | custom-call | flops 800000000 | tf_op jit(solution)/shard_map/pallas_call | solution.py:76
  33.2 1.3 %collective-permute-start.7 = (f32[32,1024]{1,0:T(8,128)S(1)}, f32[32,1024]{1,0:T(8,128)S(1)}, u32[]{:S(2)}, u32[]{:S(2)}) collective-permute-start(f32[32,1024]{1,0:T(8,128)S(1)} %get-tuple-element.61.f_second.refs_5_), channel_id=1, source_target_pairs={{0,2},{1,3},{4,6},{5,7},{8,10},{9,11},{12,14},{13,15},{16,18},{17,... | collective-permute-start | bytes 393224 | tf_op jit(solution)/shard_map/ppermute | solution.py:527
  34.5 2.6 %shard_map.97 = (f32[32,1024]{1,0:T(8,128)S(1)}, f32[32,1024]{1,0:T(8,128)S(1)}, f32[64,1024]{1,0:T(8,128)S(1)}) custom-call(f32[32,1024]{1,0:T(8,128)S(1)} %fusion.own_spots, f32[32,1024]{1,0:T(8,128)S(1)} %compare_convert_fusion.oth_spots, f32[64,1024]{1,0:T(8,128)S(1)} %get-tuple-element.54.k_second, bf16[2,2,1024,1024]{3,2,1,0:T(8,128)(2,1)S(1)} %shard_map.92.refs_0_.refs_1_), custom_call_target="tpu_custom_call" | custom-call | flops 1600000000 | tf_op jit(solution)/shard_map/pallas_call | solution.py:76
  37.1 1.3 %collective-permute-start.5 = (f32[64,1024]{1,0:T(8,128)S(1)}, f32[64,1024]{1,0:T(8,128)S(1)}, u32[]{:S(2)}, u32[]{:S(2)}) collective-permute-start(f32[64,1024]{1,0:T(8,128)S(1)} %get-tuple-element.55), channel_id=1, source_target_pairs={{0,2},{1,3},{4,6},{5,7},{8,10},{9,11},{12,14},{13,15},{16,18},{17,... | collective-permute-start | bytes 786440 | tf_op jit(solution)/shard_map/ppermute | solution.py:527
  38.4 1.3 %collective-permute-start.3 = (f32[32,1024]{1,0:T(8,128)S(1)}, f32[32,1024]{1,0:T(8,128)S(1)}, u32[]{:S(2)}, u32[]{:S(2)}) collective-permute-start(f32[32,1024]{1,0:T(8,128)S(1)} %get-tuple-element.47.refs_1_), channel_id=1, source_target_pairs={{2,0},{3,1},{6,4},{7,5},{10,8},{11,9},{14,12},{15,13},{18,16},{19,... | collective-permute-start | bytes 393224 | tf_op jit(solution)/shard_map/ppermute | solution.py:530
  39.7 1.3 %collective-permute-start.8 = (f32[32,1024]{1,0:T(8,128)S(1)}, f32[32,1024]{1,0:T(8,128)S(1)}, u32[]{:S(2)}, u32[]{:S(2)}) collective-permute-start(f32[32,1024]{1,0:T(8,128)S(1)} %get-tuple-element.62.refs_1_.refs_3_), channel_id=1, source_target_pairs={{2,0},{3,1},{6,4},{7,5},{10,8},{11,9},{14,12},{15,13},{18,16},{19,... | collective-permute-start | bytes 393224 | tf_op jit(solution)/shard_map/ppermute | solution.py:530
  41.0 5.5 %collective-permute-done.3.carried = f32[32,1024]{1,0:T(8,128)S(1)} collective-permute-done((f32[32,1024]{1,0:T(8,128)S(1)}, f32[32,1024]{1,0:T(8,128)S(1)}, u32[]{:S(2)}, u32[]{:S(2)}) %collective-permute-start.3) | collective-permute-done | bytes 131104 | tf_op jit(solution)/shard_map/ppermute | solution.py:530
  46.6 3.0 %shard_map.95 = (f32[32,1024]{1,0:T(8,128)S(1)}, f32[32,1024]{1,0:T(8,128)S(1)}, f32[32,1024]{1,0:T(8,128)S(1)}, f32[32,1024]{1,0:T(8,128)S(1)}) custom-call(f32[136,1024]{1,0:T(8,128)S(1)} %get-tuple-element.42.keep, f32[136,1024]{1,0:T(8,128)S(1)} %collective-permute-done.recv, ...), custom_call_target="tpu_custom_call", output_to_operand_aliasing={{0}: (6, {}), {1}: (7, {})} | custom-call | flops 3200000000 | tf_op jit(solution)/shard_map/pallas_call | solution.py:76
  49.6 0.2 shard_map.105
  49.9 1.3 %collective-permute-start.12 = (f32[40,1024]{1,0:T(8,128)S(1)}, f32[40,1024]{1,0:T(8,128)S(1)}, u32[]{:S(2)}, u32[]{:S(2)}) collective-permute-start(f32[40,1024]{1,0:T(8,128)S(1)} %get-tuple-element.76), channel_id=1, source_target_pairs={{2,0},{3,1},{6,4},{7,5},{10,8},{11,9},{14,12},{15,13},{18,16},{19,... | collective-permute-start | bytes 491528 | tf_op jit(solution)/shard_map/ppermute | solution.py:530
  51.2 3.0 %shard_map.101 = (f32[32,1024]{1,0:T(8,128)S(1)}, f32[32,1024]{1,0:T(8,128)S(1)}, f32[32,1024]{1,0:T(8,128)S(1)}, f32[32,1024]{1,0:T(8,128)S(1)}) custom-call(f32[136,1024]{1,0:T(8,128)S(1)} %get-tuple-element.42.keep, f32[136,1024]{1,0:T(8,128)S(1)} %collective-permute-done.recv, ...), custom_call_target="tpu_custom_call", output_to_operand_aliasing={{0}: (6, {}), {1}: (7, {})} | custom-call | flops 3200000000 | tf_op jit(solution)/shard_map/pallas_call | solution.py:76
  54.2 1.6 %collective-permute-start.9 = (f32[32,1024]{1,0:T(8,128)S(1)}, f32[32,1024]{1,0:T(8,128)S(1)}, u32[]{:S(2)}, u32[]{:S(2)}) collective-permute-start(f32[32,1024]{1,0:T(8,128)S(1)} %get-tuple-element.67.f_second.refs_7_), channel_id=1, source_target_pairs={{0,2},{1,3},{4,6},{5,7},{8,10},{9,11},{12,14},{13,15},{16,18},{17,... | collective-permute-start | bytes 393224 | tf_op jit(solution)/shard_map/ppermute | solution.py:527
  55.8 1.3 %collective-permute-start.4 = (f32[32,1024]{1,0:T(8,128)S(1)}, f32[32,1024]{1,0:T(8,128)S(1)}, u32[]{:S(2)}, u32[]{:S(2)}) collective-permute-start(f32[32,1024]{1,0:T(8,128)S(1)} %get-tuple-element.52.f_second.refs_3_), channel_id=1, source_target_pairs={{0,2},{1,3},{4,6},{5,7},{8,10},{9,11},{12,14},{13,15},{16,18},{17,... | collective-permute-start | bytes 393224 | tf_op jit(solution)/shard_map/ppermute | solution.py:527
  57.1 0.8 shard_map.106
  57.9 3.4 %collective-permute-start.13 = (f32[64,128]{1,0:T(8,128)S(1)}, f32[64,128]{1,0:T(8,128)S(1)}, u32[]{:S(2)}, u32[]{:S(2)}) collective-permute-start(f32[64,128]{1,0:T(8,128)S(1)} %shard_map.106), channel_id=1, source_target_pairs={{0,4},{1,5},{4,0},{5,1},{8,12},{9,13},{12,8},{13,9},{16,20},{17,21... | collective-permute-start | bytes 98312 | tf_op jit(solution)/shard_map/ppermute | solution.py:538
  61.4 1.3 %collective-permute-start.10 = (f32[32,1024]{1,0:T(8,128)S(1)}, f32[32,1024]{1,0:T(8,128)S(1)}, u32[]{:S(2)}, u32[]{:S(2)}) collective-permute-start(f32[32,1024]{1,0:T(8,128)S(1)} %get-tuple-element.68.refs_1_), channel_id=1, source_target_pairs={{2,0},{3,1},{6,4},{7,5},{10,8},{11,9},{14,12},{15,13},{18,16},{19,... | collective-permute-start | bytes 393224 | tf_op jit(solution)/shard_map/ppermute | solution.py:530
  62.7 1.0 %collective-permute-done.13 = f32[64,128]{1,0:T(8,128)S(1)} collective-permute-done((f32[64,128]{1,0:T(8,128)S(1)}, f32[64,128]{1,0:T(8,128)S(1)}, u32[]{:S(2)}, u32[]{:S(2)}) %collective-permute-start.13) | collective-permute-done | bytes 32800 | tf_op jit(solution)/shard_map/ppermute | solution.py:538
  63.7 3.5 %collective-permute-start.14 = (f32[128,128]{1,0:T(8,128)S(1)}, f32[128,128]{1,0:T(8,128)S(1)}, u32[]{:S(2)}, u32[]{:S(2)}) collective-permute-start(f32[128,128]{1,0:T(8,128)S(1)} %pad_maximum_fusion.4), channel_id=1, source_target_pairs={{0,8},{1,9},{4,12},{5,13},{8,0},{9,1},{12,4},{13,5},{16,24},{17,25... | collective-permute-start | bytes 196616 | tf_op jit(solution)/shard_map/ppermute | solution.py:538
  67.3 1.3 %collective-permute-start.6 = (f32[64,1024]{1,0:T(8,128)S(1)}, f32[64,1024]{1,0:T(8,128)S(1)}, u32[]{:S(2)}, u32[]{:S(2)}) collective-permute-start(f32[64,1024]{1,0:T(8,128)S(1)} %get-tuple-element.56.refs_1_), channel_id=1, source_target_pairs={{2,0},{3,1},{6,4},{7,5},{10,8},{11,9},{14,12},{15,13},{18,16},{19,... | collective-permute-start | bytes 786440 | tf_op jit(solution)/shard_map/ppermute | solution.py:530
  68.6 1.5 %collective-permute-done.14 = f32[128,128]{1,0:T(8,128)S(1)} collective-permute-done((f32[128,128]{1,0:T(8,128)S(1)}, f32[128,128]{1,0:T(8,128)S(1)}, u32[]{:S(2)}, u32[]{:S(2)}) %collective-permute-start.14) | collective-permute-done | bytes 65568 | tf_op jit(solution)/shard_map/ppermute | solution.py:538
  70.1 2.5 %collective-permute-start.15 = (f32[256,128]{1,0:T(8,128)S(1)}, f32[256,128]{1,0:T(8,128)S(1)}, u32[]{:S(2)}, u32[]{:S(2)}) collective-permute-start(f32[256,128]{1,0:T(8,128)S(1)} %pad_maximum_fusion.2), channel_id=1, source_target_pairs={{0,16},{1,17},{4,20},{5,21},{8,24},{9,25},{12,28},{13,29},{16,0},{... | collective-permute-start | bytes 393224 | tf_op jit(solution)/shard_map/ppermute | solution.py:538
  72.6 1.6 %shard_map.103 = (f32[32,1024]{1,0:T(8,128)S(1)}, f32[32,1024]{1,0:T(8,128)S(1)}) custom-call(f32[32,1024]{1,0:T(8,128)S(1)} %get-tuple-element.66.f_first.refs_6_, f32[32,1024]{1,0:T(8,128)S(1)} %get-tuple-element.67.f_second.refs_7_, f32[64,1024]{1,0:T(8,128)S(1)} %get-tuple-element.53.k_first, ...), custom_call_target="tpu_custom_call", output_to_operand_aliasing={{0}: (6, {}), {1}: (7, {})} | custom-call | flops 1600000000 | tf_op jit(solution)/shard_map/pallas_call | solution.py:76
  74.2 1.3 %collective-permute-done.6.carried = f32[64,1024]{1,0:T(8,128)S(1)} collective-permute-done((f32[64,1024]{1,0:T(8,128)S(1)}, f32[64,1024]{1,0:T(8,128)S(1)}, u32[]{:S(2)}, u32[]{:S(2)}) %collective-permute-start.6) | collective-permute-done | bytes 262176 | tf_op jit(solution)/shard_map/ppermute | solution.py:530
  75.5 1.4 %shard_map.99 = (f32[64,1024]{1,0:T(8,128)S(1)}, f32[64,1024]{1,0:T(8,128)S(1)}) custom-call(f32[32,1024]{1,0:T(8,128)S(1)} %get-tuple-element.51.f_first.refs_2_, f32[32,1024]{1,0:T(8,128)S(1)} %get-tuple-element.52.f_second.refs_3_, f32[64,1024]{1,0:T(8,128)S(1)} %get-tuple-element.53.k_first, ...), custom_call_target="tpu_custom_call", output_to_operand_aliasing={{0}: (6, {}), {1}: (7, {})} | custom-call | flops 1600000000 | tf_op jit(solution)/shard_map/pallas_call | solution.py:76
  77.0 0.1 shard_map.104
  77.2 2.1 %collective-permute-done.15 = f32[256,128]{1,0:T(8,128)S(1)} collective-permute-done((f32[256,128]{1,0:T(8,128)S(1)}, f32[256,128]{1,0:T(8,128)S(1)}, u32[]{:S(2)}, u32[]{:S(2)}) %collective-permute-start.15) | collective-permute-done | bytes 131104 | tf_op jit(solution)/shard_map/ppermute | solution.py:538
  79.2 3.4 %shard_map.108 = f32[64,128]{1,0:T(8,128)S(1)} custom-call(f32[512,128]{1,0:T(8,128)S(1)} %pad_maximum_fusion.values, f32[448,128]{1,0:T(8,128)S(1)} %pad_maximum_fusion.1.fixed), custom_call_target="tpu_custom_call" | custom-call | flops 400000000 | tf_op jit(solution)/shard_map/pallas_call | solution.py:76
  82.7 1.3 %collective-permute-start.19 = (f32[64,128]{1,0:T(8,128)S(1)}, f32[64,128]{1,0:T(8,128)S(1)}, u32[]{:S(2)}, u32[]{:S(2)}) collective-permute-start(f32[64,128]{1,0:T(8,128)S(1)} %shard_map.108), channel_id=1, source_target_pairs={{0,2},{1,3},{4,6},{5,7},{8,10},{9,11},{12,14},{13,15},{16,18},{17,... | collective-permute-start | bytes 98312 | tf_op jit(solution)/shard_map/ppermute | solution.py:527
  84.0 1.6 %collective-permute-done.19 = f32[64,128]{1,0:T(8,128)S(1)} collective-permute-done((f32[64,128]{1,0:T(8,128)S(1)}, f32[64,128]{1,0:T(8,128)S(1)}, u32[]{:S(2)}, u32[]{:S(2)}) %collective-permute-start.19) | collective-permute-done | bytes 32800 | tf_op jit(solution)/shard_map/ppermute | solution.py:527
  85.6 1.2 %collective-permute-done.20.q_recv = f32[64,128]{1,0:T(8,128)S(1)} collective-permute-done((f32[64,128]{1,0:T(8,128)S(1)}, f32[64,128]{1,0:T(8,128)S(1)}, u32[]{:S(2)}, u32[]{:S(2)}) %collective-permute-start.20) | collective-permute-done | bytes 32800 | tf_op jit(solution)/shard_map/ppermute | solution.py:524
  86.8 1.2 %shard_map.109 = f32[128,1024]{1,0:T(8,128)} custom-call(f32[96,1024]{1,0:T(8,128)S(1)} %get-tuple-element.72.keep, f32[96,1024]{1,0:T(8,128)S(1)} %collective-permute-done.11.recv, f32[64,128]{1,0:T(8,128)S(1)} %broadcast_select_fusion.q_keep, f32[64,128]{1,0:T(8,128)S(1)} %collective-permute-done.20.q_recv, f32[32,1024]{1,0:T(8,128)S(1)} %bitcast.12, ...), custom_call_target="tpu_custom_call" | custom-call | flops 400000000 | tf_op jit(solution)/shard_map/pallas_call | solution.py:76
  (45 shorter events, 0.4 us)
Async XLA Ops:
  0.0 12.5 %copy-start.5 = (s32[1,1,32]{2,1,0:T(1,128)S(1)}, s32[1,1,32]{2,1,0:T(1,128)}, u32[]{:S(2)}) copy-start(s32[1,1,32]{2,1,0:T(1,128)} %param.12) | copy-start | bytes 388
  0.0 7.3 %copy-start.9 = (f32[128,16]{0,1:T(8,128)S(1)}, f32[128,16]{0,1:T(8,128)}, u32[]{:S(2)}) copy-start(f32[128,16]{0,1:T(8,128)} %param.17) | copy-start | bytes 24580
  0.0 7.4 %copy-start.8 = (s32[1,32]{1,0:T(1,128)S(1)}, s32[1,32]{1,0:T(1,128)}, u32[]{:S(2)}) copy-start(s32[1,32]{1,0:T(1,128)} %maps.1) | copy-start | bytes 388
  0.0 25.6 %collective-permute-start.1 = (f32[1024,1024]{1,0:T(8,128)}, f32[1024,1024]{1,0:T(8,128)}, u32[]{:S(2)}, u32[]{:S(2)}) collective-permute-start(f32[1024,1024]{1,0:T(8,128)} %bitcast.19), channel_id=1, source_target_pairs={{0,1},{1,0},{2,3},{3,2},{4,5},{5,4},{6,7},{7,6},{8,9},{9,8},{10,11... | collective-permute-start | bytes 12582920 | tf_op jit(solution)/shard_map/ppermute | solution.py:524
  0.6 0.7 copy-start.4
  1.2 0.7 copy-start.7
  1.9 5.5 %copy-start.6 = (f32[1,32,32]{2,1,0:T(8,128)S(1)}, f32[1,32,32]{2,1,0:T(8,128)}, u32[]{:S(2)}) copy-start(f32[1,32,32]{2,1,0:T(8,128)} %param.14) | copy-start | bytes 12292
  5.3 2.0 %copy-start = (bf16[2,1024,1024]{2,1,0:T(8,128)(2,1)}, bf16[2,1024,1024]{2,1,0:T(8,128)(2,1)S(1)}, u32[]{:S(2)}) copy-start(bf16[2,1024,1024]{2,1,0:T(8,128)(2,1)S(1)} %get-tuple-element.44.own) | copy-start | bytes 12582916
  7.3 18.1 %collective-permute-start = (f32[136,1024]{1,0:T(8,128)S(1)}, f32[136,1024]{1,0:T(8,128)S(1)}, u32[]{:S(2)}, u32[]{:S(2)}) collective-permute-start(f32[136,1024]{1,0:T(8,128)S(1)} %get-tuple-element.43), channel_id=1, source_target_pairs={{0,1},{1,0},{2,3},{3,2},{4,5},{5,4},{6,7},{7,6},{8,9},{9,8},{10,11... | collective-permute-start | bytes 1671176 | tf_op jit(solution)/shard_map/ppermute | solution.py:524
  7.6 6.8 %collective-permute-start.16 = (f32[56,128]{1,0:T(8,128)S(1)}, f32[56,128]{1,0:T(8,128)S(1)}, u32[]{:S(2)}, u32[]{:S(2)}) collective-permute-start(f32[56,128]{1,0:T(8,128)S(1)} %shard_map.107), channel_id=1, source_target_pairs={{0,4},{1,5},{4,0},{5,1},{8,12},{9,13},{12,8},{13,9},{16,20},{17,21... | collective-permute-start | bytes 86024 | tf_op jit(solution)/shard_map/ppermute | solution.py:538
  14.4 6.1 %collective-permute-start.17 = (f32[112,128]{1,0:T(8,128)S(1)}, f32[112,128]{1,0:T(8,128)S(1)}, u32[]{:S(2)}, u32[]{:S(2)}) collective-permute-start(f32[112,128]{1,0:T(8,128)S(1)} %pad_maximum_fusion.5), channel_id=1, source_target_pairs={{0,8},{1,9},{4,12},{5,13},{8,0},{9,1},{12,4},{13,5},{16,24},{17,25... | collective-permute-start | bytes 172040 | tf_op jit(solution)/shard_map/ppermute | solution.py:538
  20.5 35.3 %collective-permute-start.18 = (f32[224,128]{1,0:T(8,128)S(1)}, f32[224,128]{1,0:T(8,128)S(1)}, u32[]{:S(2)}, u32[]{:S(2)}) collective-permute-start(f32[224,128]{1,0:T(8,128)S(1)} %pad_maximum_fusion.3), channel_id=1, source_target_pairs={{0,16},{1,17},{4,20},{5,21},{8,24},{9,25},{12,28},{13,29},{16,0},{... | collective-permute-start | bytes 344072 | tf_op jit(solution)/shard_map/ppermute | solution.py:538
  25.6 2.2 %copy-start.1 = (bf16[2,1024,1024]{2,1,0:T(8,128)(2,1)S(1)}, bf16[2,1024,1024]{2,1,0:T(8,128)(2,1)}, u32[]{:S(2)}) copy-start(bf16[2,1024,1024]{2,1,0:T(8,128)(2,1)} %copy-done) | copy-start | bytes 12582916
  31.0 7.4 %collective-permute-start.2 = (f32[32,1024]{1,0:T(8,128)S(1)}, f32[32,1024]{1,0:T(8,128)S(1)}, u32[]{:S(2)}, u32[]{:S(2)}) collective-permute-start(f32[32,1024]{1,0:T(8,128)S(1)} %get-tuple-element.46.f_second.refs_1_), channel_id=1, source_target_pairs={{0,2},{1,3},{4,6},{5,7},{8,10},{9,11},{12,14},{13,15},{16,18},{17,... | collective-permute-start | bytes 393224 | tf_op jit(solution)/shard_map/ppermute | solution.py:527
  33.2 6.6 %collective-permute-start.7 = (f32[32,1024]{1,0:T(8,128)S(1)}, f32[32,1024]{1,0:T(8,128)S(1)}, u32[]{:S(2)}, u32[]{:S(2)}) collective-permute-start(f32[32,1024]{1,0:T(8,128)S(1)} %get-tuple-element.61.f_second.refs_5_), channel_id=1, source_target_pairs={{0,2},{1,3},{4,6},{5,7},{8,10},{9,11},{12,14},{13,15},{16,18},{17,... | collective-permute-start | bytes 393224 | tf_op jit(solution)/shard_map/ppermute | solution.py:527
  37.1 12.6 %collective-permute-start.5 = (f32[64,1024]{1,0:T(8,128)S(1)}, f32[64,1024]{1,0:T(8,128)S(1)}, u32[]{:S(2)}, u32[]{:S(2)}) collective-permute-start(f32[64,1024]{1,0:T(8,128)S(1)} %get-tuple-element.55), channel_id=1, source_target_pairs={{0,2},{1,3},{4,6},{5,7},{8,10},{9,11},{12,14},{13,15},{16,18},{17,... | collective-permute-start | bytes 786440 | tf_op jit(solution)/shard_map/ppermute | solution.py:527
  38.4 8.2 %collective-permute-start.3 = (f32[32,1024]{1,0:T(8,128)S(1)}, f32[32,1024]{1,0:T(8,128)S(1)}, u32[]{:S(2)}, u32[]{:S(2)}) collective-permute-start(f32[32,1024]{1,0:T(8,128)S(1)} %get-tuple-element.47.refs_1_), channel_id=1, source_target_pairs={{2,0},{3,1},{6,4},{7,5},{10,8},{11,9},{14,12},{15,13},{18,16},{19,... | collective-permute-start | bytes 393224 | tf_op jit(solution)/shard_map/ppermute | solution.py:530
  39.7 11.4 %collective-permute-start.8 = (f32[32,1024]{1,0:T(8,128)S(1)}, f32[32,1024]{1,0:T(8,128)S(1)}, u32[]{:S(2)}, u32[]{:S(2)}) collective-permute-start(f32[32,1024]{1,0:T(8,128)S(1)} %get-tuple-element.62.refs_1_.refs_3_), channel_id=1, source_target_pairs={{2,0},{3,1},{6,4},{7,5},{10,8},{11,9},{14,12},{15,13},{18,16},{19,... | collective-permute-start | bytes 393224 | tf_op jit(solution)/shard_map/ppermute | solution.py:530
  49.9 7.3 %collective-permute-start.12 = (f32[40,1024]{1,0:T(8,128)S(1)}, f32[40,1024]{1,0:T(8,128)S(1)}, u32[]{:S(2)}, u32[]{:S(2)}) collective-permute-start(f32[40,1024]{1,0:T(8,128)S(1)} %get-tuple-element.76), channel_id=1, source_target_pairs={{2,0},{3,1},{6,4},{7,5},{10,8},{11,9},{14,12},{15,13},{18,16},{19,... | collective-permute-start | bytes 491528 | tf_op jit(solution)/shard_map/ppermute | solution.py:530
  54.2 7.2 %collective-permute-start.9 = (f32[32,1024]{1,0:T(8,128)S(1)}, f32[32,1024]{1,0:T(8,128)S(1)}, u32[]{:S(2)}, u32[]{:S(2)}) collective-permute-start(f32[32,1024]{1,0:T(8,128)S(1)} %get-tuple-element.67.f_second.refs_7_), channel_id=1, source_target_pairs={{0,2},{1,3},{4,6},{5,7},{8,10},{9,11},{12,14},{13,15},{16,18},{17,... | collective-permute-start | bytes 393224 | tf_op jit(solution)/shard_map/ppermute | solution.py:527
  55.8 11.4 %collective-permute-start.4 = (f32[32,1024]{1,0:T(8,128)S(1)}, f32[32,1024]{1,0:T(8,128)S(1)}, u32[]{:S(2)}, u32[]{:S(2)}) collective-permute-start(f32[32,1024]{1,0:T(8,128)S(1)} %get-tuple-element.52.f_second.refs_3_), channel_id=1, source_target_pairs={{0,2},{1,3},{4,6},{5,7},{8,10},{9,11},{12,14},{13,15},{16,18},{17,... | collective-permute-start | bytes 393224 | tf_op jit(solution)/shard_map/ppermute | solution.py:527
  57.9 5.8 %collective-permute-start.13 = (f32[64,128]{1,0:T(8,128)S(1)}, f32[64,128]{1,0:T(8,128)S(1)}, u32[]{:S(2)}, u32[]{:S(2)}) collective-permute-start(f32[64,128]{1,0:T(8,128)S(1)} %shard_map.106), channel_id=1, source_target_pairs={{0,4},{1,5},{4,0},{5,1},{8,12},{9,13},{12,8},{13,9},{16,20},{17,21... | collective-permute-start | bytes 98312 | tf_op jit(solution)/shard_map/ppermute | solution.py:538
  61.4 11.2 %collective-permute-start.10 = (f32[32,1024]{1,0:T(8,128)S(1)}, f32[32,1024]{1,0:T(8,128)S(1)}, u32[]{:S(2)}, u32[]{:S(2)}) collective-permute-start(f32[32,1024]{1,0:T(8,128)S(1)} %get-tuple-element.68.refs_1_), channel_id=1, source_target_pairs={{2,0},{3,1},{6,4},{7,5},{10,8},{11,9},{14,12},{15,13},{18,16},{19,... | collective-permute-start | bytes 393224 | tf_op jit(solution)/shard_map/ppermute | solution.py:530
  63.7 6.3 %collective-permute-start.14 = (f32[128,128]{1,0:T(8,128)S(1)}, f32[128,128]{1,0:T(8,128)S(1)}, u32[]{:S(2)}, u32[]{:S(2)}) collective-permute-start(f32[128,128]{1,0:T(8,128)S(1)} %pad_maximum_fusion.4), channel_id=1, source_target_pairs={{0,8},{1,9},{4,12},{5,13},{8,0},{9,1},{12,4},{13,5},{16,24},{17,25... | collective-permute-start | bytes 196616 | tf_op jit(solution)/shard_map/ppermute | solution.py:538
  67.3 8.3 %collective-permute-start.6 = (f32[64,1024]{1,0:T(8,128)S(1)}, f32[64,1024]{1,0:T(8,128)S(1)}, u32[]{:S(2)}, u32[]{:S(2)}) collective-permute-start(f32[64,1024]{1,0:T(8,128)S(1)} %get-tuple-element.56.refs_1_), channel_id=1, source_target_pairs={{2,0},{3,1},{6,4},{7,5},{10,8},{11,9},{14,12},{15,13},{18,16},{19,... | collective-permute-start | bytes 786440 | tf_op jit(solution)/shard_map/ppermute | solution.py:530
  70.1 9.2 %collective-permute-start.15 = (f32[256,128]{1,0:T(8,128)S(1)}, f32[256,128]{1,0:T(8,128)S(1)}, u32[]{:S(2)}, u32[]{:S(2)}) collective-permute-start(f32[256,128]{1,0:T(8,128)S(1)} %pad_maximum_fusion.2), channel_id=1, source_target_pairs={{0,16},{1,17},{4,20},{5,21},{8,24},{9,25},{12,28},{13,29},{16,0},{... | collective-permute-start | bytes 393224 | tf_op jit(solution)/shard_map/ppermute | solution.py:538
  75.5 11.3 %copy-start.2 = (f32[1,1,32,1024]{3,2,1,0:T(8,128)S(1)}, f32[1,1,32,1024]{3,2,1,0:T(8,128)}, u32[]{:S(2)}) copy-start(f32[1,1,32,1024]{3,2,1,0:T(8,128)} %param.15) | copy-start | bytes 393220
  75.5 11.3 %copy-start.3 = (f32[1,1,32,1024]{3,2,1,0:T(8,128)S(1)}, f32[1,1,32,1024]{3,2,1,0:T(8,128)}, u32[]{:S(2)}) copy-start(f32[1,1,32,1024]{3,2,1,0:T(8,128)} %param.16) | copy-start | bytes 393220
  77.1 9.7 %collective-permute-start.11 = (f32[96,1024]{1,0:T(8,128)S(1)}, f32[96,1024]{1,0:T(8,128)S(1)}, u32[]{:S(2)}, u32[]{:S(2)}) collective-permute-start(f32[96,1024]{1,0:T(8,128)S(1)} %get-tuple-element.73), channel_id=1, source_target_pairs={{0,1},{1,0},{2,3},{3,2},{4,5},{5,4},{6,7},{7,6},{8,9},{9,8},{10,11... | collective-permute-start | bytes 1179656 | tf_op jit(solution)/shard_map/ppermute | solution.py:524
  82.7 2.9 %collective-permute-start.19 = (f32[64,128]{1,0:T(8,128)S(1)}, f32[64,128]{1,0:T(8,128)S(1)}, u32[]{:S(2)}, u32[]{:S(2)}) collective-permute-start(f32[64,128]{1,0:T(8,128)S(1)} %shard_map.108), channel_id=1, source_target_pairs={{0,2},{1,3},{4,6},{5,7},{8,10},{9,11},{12,14},{13,15},{16,18},{17,... | collective-permute-start | bytes 98312 | tf_op jit(solution)/shard_map/ppermute | solution.py:527
  85.6 1.2 %collective-permute-start.20 = (f32[64,128]{1,0:T(8,128)S(1)}, f32[64,128]{1,0:T(8,128)S(1)}, u32[]{:S(2)}, u32[]{:S(2)}) collective-permute-start(f32[64,128]{1,0:T(8,128)S(1)} %broadcast_select_fusion.q_keep), channel_id=1, source_target_pairs={{0,1},{1,0},{2,3},{3,2},{4,5},{5,4},{6,7},{7,6},{8,9},{9,8},{10,11... | collective-permute-start | bytes 98312 | tf_op jit(solution)/shard_map/ppermute | solution.py:524

commit v4 on v3

--- a/solution.py
+++ b/solution.py
@@ -104,7 +104,17 @@
             new[...] = old[...]
 
 
-def fix(inverse, schur, maps, out):
+def fix(inverse_far, schur_far, maps_far, out, inverse, schur, maps, sems):
+    copies = [
+        pltpu.make_async_copy(far, near, sems.at[i])
+        for i, (far, near) in enumerate(
+            ((inverse_far, inverse), (schur_far, schur), (maps_far, maps))
+        )
+    ]
+    for copy in copies:
+        copy.start()
+    for copy in copies:
+        copy.wait()
     share, prim = inverse.shape[1], schur.shape[0]
     unit = lax.broadcasted_iota(jnp.int32, (share, share), 0) == lax.broadcasted_iota(
         jnp.int32, (share, share), 1
@@ -119,7 +129,9 @@
     out[share + prim : share + prim + 1, :prim] = maps[...].astype(f32)
 
 
-def first_products(matrix, vector, one, two, diagonal, index, own, keep, send, buffer, x, total, sems):
+def first_products(
+    matrix, vector, one, two, diagonal_far, index_far, own, keep, send, buffer, x, total, diagonal, index, sems
+):
     size = matrix.shape[0]
     step = size // PIECES
     rows, prim = vector.shape[0], one.shape[0]
@@ -128,10 +140,12 @@
         pltpu.make_async_copy(vector, x.at[pl.ds(0, rows)], sems.at[0]),
         pltpu.make_async_copy(one, x.at[pl.ds(rows, prim)], sems.at[1]),
         pltpu.make_async_copy(two, x.at[pl.ds(rows + prim, prim)], sems.at[2]),
+        pltpu.make_async_copy(diagonal_far, diagonal, sems.at[3]),
+        pltpu.make_async_copy(index_far, index, sems.at[4]),
     ]
     pieces = [
         pltpu.make_async_copy(
-            matrix.at[pl.ds(i * step, step)], buffer.at[pl.ds(i * step, step)], sems.at[3 + i]
+            matrix.at[pl.ds(i * step, step)], buffer.at[pl.ds(i * step, step)], sems.at[5 + i]
         )
         for i in range(PIECES)
     ]
@@ -423,7 +437,11 @@
     share = height - prim - 8
     me = lax.axis_index("sub")
     unknown = lax.broadcasted_iota(jnp.int32, (count, width), 0)
-    there = ((unknown // share) ^ me) * share + unknown % share
+    block = unknown // share
+    far = jnp.zeros_like(block)
+    for bit in range(subs.bit_length() - 1):
+        far = far | (((block >> bit) & 1) << (subs.bit_length() - 2 - bit))
+    there = (far ^ me) * share + unknown % share
     unknown, there = unknown.astype(f32), there.astype(f32)
     lane = lax.broadcasted_iota(jnp.int32, (half, width), 1)
 
@@ -455,8 +473,18 @@
     def spot(row, ids):
         return (ids == row).astype(f32)
 
+    def pick_plain(left, spots):
+        top, low = halves(left)
+        both = dot(jnp.concatenate([top, low], axis=0), spots.astype(bf16))
+        return both[:half] + both[half:]
+
+    def pick_rows(left, spots):
+        top, low = halves(left)
+        both = dot_rows(jnp.concatenate([top, low], axis=0), spots.astype(bf16))
+        return both[:half] + both[half:]
+
     def add_first(j, total):
-        return total + times_rows(at(values, j, half), spot(map_of(j), unknown))
+        return total + pick_rows(at(values, j, half), spot(map_of(j), unknown))
 
     inverse = jnp.concatenate([at(fixed, j, height, 0, share) for j in range(subs)], axis=0)
     zero = jnp.zeros((half, count), f32)
@@ -466,32 +494,27 @@
         v = at(values, j, half)
         row = map_of(j)
         schur = at(fixed, j, height, share, share + prim)[:, :width]
-        multiplier = times_plain(v, wide(schur, width))
-        picked = times_plain(found, spot(row, there))
-        change = times_plain(multiplier, wide(v[:prim], width)) - times_plain(
-            picked, wide(v[prim : 2 * prim], width)
-        )
-        return row, schur, multiplier, picked, jnp.where(lane < 2 * prim, v, change)
+        first = pick_plain(found, spot(pltpu.roll(row, prim, 1), there)) - times_plain(
+            v, wide(schur, width)
+        )
+        change = times_plain(first, wide(v[: 2 * prim], width))
+        return row, schur, first, jnp.where(lane < 2 * prim, v, change)
 
     def add_second(j, total):
-        row, _, _, _, p = parts(j)
+        row, _, _, p = parts(j)
         signs = (
             spot(row, unknown)
             - spot(pltpu.roll(row, prim, 1), unknown)
-            + spot(pltpu.roll(row, 2 * prim, 1), unknown)
-        )
-        return total + times_rows(p, signs)
+            - spot(pltpu.roll(row, 2 * prim, 1), unknown)
+        )
+        return total + pick_rows(p, signs)
 
     found_two = times_rows(loop(add_second, zero), inverse)
-    row, schur, multiplier, picked, p = parts(0)
-    multiplier_two = times_plain(p, wide(jnp.concatenate([schur, -schur, schur], axis=0), width))
-    picked_two = times_plain(found_two, spot(row, there))
-    q[...] = (
-        pltpu.roll(picked, prim, 1)
-        - multiplier
-        - pltpu.roll(multiplier + multiplier_two, 2 * prim, 1)
-        + pltpu.roll(picked + picked_two, 3 * prim, 1)
-    )
+    row, schur, first, p = parts(0)
+    second = pick_plain(found_two, spot(pltpu.roll(row, prim, 1), there)) - times_plain(
+        p, wide(jnp.concatenate([schur, -schur, -schur], axis=0), width)
+    )
+    q[...] = first + pltpu.roll(first + second, 2 * prim, 1)
 
 
 def finish(keep, recv, q_keep, q_recv, one, two, out):
@@ -529,15 +552,17 @@
     def fall(x):
         return lax.ppermute(x, "slab", [(2, 0), (3, 1)])
 
-    def gather(x):
-        distance = 1
-        while distance < subs:
+    def gather(x, which):
+        distance = subs // 2
+        while distance:
             pairs = [
-                (i * levels + k, (i ^ distance) * levels + k) for i in range(subs) for k in range(2)
+                (i * levels + k, (i ^ distance) * levels + k)
+                for i in range(subs)
+                for k in (2 * which, 2 * which + 1)
             ]
             other = lax.ppermute(x, ("sub", "slab"), pairs)
             x = jnp.concatenate([x, other], axis=0)
-            distance *= 2
+            distance //= 2
         return x
 
     vector = residual[0, 0]
@@ -563,8 +588,15 @@
         [struct((share + prim + 8, coarse_count))],
         [coarse_inverse, schur_small[0], coarse_map],
         0.1,
-    )
-    fixed = gather(fixed)
+        scratch=[
+            pltpu.VMEM(coarse_inverse.shape, f32),
+            pltpu.VMEM((prim, prim), f32),
+            pltpu.VMEM(coarse_map.shape, jnp.int32),
+            pltpu.SemaphoreType.DMA((3,)),
+        ],
+        hbm=(0, 1, 2),
+    )
+    fixed = gather(fixed, 1)
 
     own, keep, send = call(
         first_products,
@@ -575,9 +607,11 @@
             pltpu.VMEM((size, size), f32),
             pltpu.VMEM((rows + extra, size), f32),
             pltpu.VMEM((rows + extra, size), f32),
-            pltpu.SemaphoreType.DMA((3 + PIECES,)),
+            pltpu.VMEM((1, size), f32),
+            pltpu.VMEM((1, prim), jnp.int32),
+            pltpu.SemaphoreType.DMA((5 + PIECES,)),
         ],
-        hbm=(0, 1, 2, 3),
+        hbm=(0, 1, 2, 3, 4, 5),
     )
     recv = swap(send)
     weights = call(
@@ -650,7 +684,7 @@
         [z_back, y_first, y_second, k_first, k_second, *pieces],
         1,
     )
-    values = gather(values)
+    values = gather(values, 0)
 
     n_two = []
     for i in span:
@@ -677,6 +711,7 @@
     m_keep, m_send = call(settle, like(2, half + prim), pieces, 0.5)
     m_recv = swap(m_send)
 
+    fixed = fall(fixed)
     (q,) = call(
         functools.partial(solve, subs, prim),
         [struct((half, width))],

time: 88.5 us -> 92.5 us (1.045)
  starting transfers between devices: 38.5 us -> 49.3 us
  waiting for transfers between devices: 18.2 us -> 11.7 us
    ppermute x6, starting transfers between devices: 8.09 us -> 28.4 us  [rise(): return lax.ppermute(x, 'slab', [(0, 2), (1, 3)])]
    ppermute x6, starting transfers between devices: 23.3 us -> 12.6 us  [gather(): other = lax.ppermute(x, ('sub', 'slab'), pairs)]
    ppermute x6, waiting for transfers between devices: 8.47 us -> 2.06 us  [gather(): other = lax.ppermute(x, ('sub', 'slab'), pairs)]
    ppermute x5 -> x6, starting transfers between devices: 6.46 us -> 7.75 us  [fall(): return lax.ppermute(x, 'slab', [(2, 0), (3, 1)])]
    unnamed x21 -> x13, local copies, waits for them, and re-layouts: 5.66 us -> 4.96 us
    ppermute x5 -> x6, waiting for transfers between devices: 6.89 us -> 6.85 us  [fall(): return lax.ppermute(x, 'slab', [(2, 0), (3, 1)])]
  transfers between devices with their start and end apart: 21 -> 22, of which waited for: 9 -> 6; matrix products, arithmetic and copies ran while one was open for 0% -> 1% of each run, Pallas kernels for 27% -> 26%
where the time goes in v4:
time: 92.5 us; the launch traced here: 91.9 us
  starting transfers between devices  49.3 us (53%)
  Pallas kernels  25.2 us (27%)
  waiting for transfers between devices  11.7 us (13%)
  local copies, waits for them, and re-layouts  4.96 us (5%)
    ppermute x6, starting transfers between devices, rise(): return lax.ppermute(x, 'slab', [(0, 2), (1, 3)])  28.4 us
    pallas_call x19, Pallas kernels, call(): pl.pallas_call(body, out_shape=outs, in_specs=specs, out_specs=[spec(pltp...  25.2 us
    ppermute x6, starting transfers between devices, gather(): other = lax.ppermute(x, ('sub', 'slab'), pairs)  12.6 us
    ppermute x6, starting transfers between devices, fall(): return lax.ppermute(x, 'slab', [(2, 0), (3, 1)])  7.75 us
    ppermute x6, waiting for transfers between devices, fall(): return lax.ppermute(x, 'slab', [(2, 0), (3, 1)])  6.85 us
    unnamed x13, local copies, waits for them, and re-layouts  4.96 us
    ppermute x6, waiting for transfers between devices, gather(): other = lax.ppermute(x, ('sub', 'slab'), pairs)  2.06 us
  transfers between devices with their start and end apart: 22, of which 6 were waited for; matrix products, arithmetic and copies ran while one was open for 1% of the time, Pallas kernels for 26%

profile of v4, /device:TPU:0, one launch (start us, length us, event | category | flops | bytes accessed | tf_op | source)
XLA Modules:
  0.0 91.9 jit_solution(4483973991463155777)
XLA Ops:
  0.0 0.5 collective-permute-start.1
  0.5 3.4 %shard_map.91 = (bf16[2,1024,1024]{2,1,0:T(8,128)(2,1)S(1)}, f32[136,1024]{1,0:T(8,128)S(1)}, f32[136,1024]{1,0:T(8,128)S(1)}) custom-call(f32[1024,1024]{1,0:T(8,128)} %bitcast.18, f32[128,1024]{1,0:T(8,128)} %bitcast.19, f32[32,1024]{1,0:T(8,128)} %bitcast.11, f32[32,1024]{1,0:T(8,128)} %bitcast.13, f32[1,1024]{1,0:T(1,128)} %bitcast.21, s32[1,32]{1,0:T(1,128)} %bitcast.15), custom_call_target="tpu_custom_call" | custom-call | flops 1600000000 | tf_op jit(solution)/shard_map/pallas_call | solution.py:76
  3.9 2.0 %copy-done = bf16[2,1024,1024]{2,1,0:T(8,128)(2,1)} copy-done((bf16[2,1024,1024]{2,1,0:T(8,128)(2,1)}, bf16[2,1024,1024]{2,1,0:T(8,128)(2,1)S(1)}, u32[]{:S(2)}) %copy-start) | copy-done | bytes 4194328
  6.0 0.0 collective-permute-start
  6.0 0.7 copy.20.inverse_far
  6.7 1.1 %shard_map.107 = f32[56,128]{1,0:T(8,128)S(1)} custom-call(f32[128,16]{1,0:T(8,128)} %copy.20.inverse_far, f32[32,32]{1,0:T(8,128)} %bitcast.20, s32[1,32]{1,0:T(1,128)} %maps_far.1), custom_call_target="tpu_custom_call" | custom-call | flops 80000000 | tf_op jit(solution)/shard_map/pallas_call | solution.py:76
  7.8 0.7 collective-permute-start.16
  8.5 0.1 fusion.own_spots
  8.6 0.7 collective-permute-start.17
  9.3 0.7 collective-permute-start.18
  10.0 0.1 compare_convert_fusion.oth_spots
  10.1 2.2 %copy-done.1 = bf16[2,1024,1024]{2,1,0:T(8,128)(2,1)S(1)} copy-done((bf16[2,1024,1024]{2,1,0:T(8,128)(2,1)S(1)}, bf16[2,1024,1024]{2,1,0:T(8,128)(2,1)}, u32[]{:S(2)}) %copy-start.1) | copy-done | bytes 4194328
  12.3 2.3 %shard_map.92.refs_0_.refs_1_ = bf16[2,2,1024,1024]{3,2,1,0:T(8,128)(2,1)S(1)} custom-call(f32[1024,1024]{1,0:T(8,128)} %collective-permute-done.1.matrix, bf16[2,1024,1024]{2,1,0:T(8,128)(2,1)S(1)} %copy-done.1), custom_call_target="tpu_custom_call" | custom-call | flops 800000000 | tf_op jit(solution)/shard_map/pallas_call | solution.py:76
  14.6 0.8 shard_map.93
  15.5 18.4 %collective-permute-start.2 = (f32[32,1024]{1,0:T(8,128)S(1)}, f32[32,1024]{1,0:T(8,128)S(1)}, u32[]{:S(2)}, u32[]{:S(2)}) collective-permute-start(f32[32,1024]{1,0:T(8,128)S(1)} %get-tuple-element.46.f_second.refs_1_), channel_id=1, source_target_pairs={{0,2},{1,3},{4,6},{5,7},{8,10},{9,11},{12,14},{13,15},{16,18},{17,... | collective-permute-start | bytes 393224 | tf_op jit(solution)/shard_map/ppermute | solution.py:550
  33.8 0.9 shard_map.96
  34.7 1.3 %collective-permute-start.7 = (f32[32,1024]{1,0:T(8,128)S(1)}, f32[32,1024]{1,0:T(8,128)S(1)}, u32[]{:S(2)}, u32[]{:S(2)}) collective-permute-start(f32[32,1024]{1,0:T(8,128)S(1)} %get-tuple-element.61.f_second.refs_5_), channel_id=1, source_target_pairs={{0,2},{1,3},{4,6},{5,7},{8,10},{9,11},{12,14},{13,15},{16,18},{17,... | collective-permute-start | bytes 393224 | tf_op jit(solution)/shard_map/ppermute | solution.py:550
  36.0 2.6 %shard_map.97 = (f32[32,1024]{1,0:T(8,128)S(1)}, f32[32,1024]{1,0:T(8,128)S(1)}, f32[64,1024]{1,0:T(8,128)S(1)}) custom-call(f32[32,1024]{1,0:T(8,128)S(1)} %fusion.own_spots, f32[32,1024]{1,0:T(8,128)S(1)} %compare_convert_fusion.oth_spots, f32[64,1024]{1,0:T(8,128)S(1)} %get-tuple-element.54.k_second, bf16[2,2,1024,1024]{3,2,1,0:T(8,128)(2,1)S(1)} %shard_map.92.refs_0_.refs_1_), custom_call_target="tpu_custom_call" | custom-call | flops 1600000000 | tf_op jit(solution)/shard_map/pallas_call | solution.py:76
  38.6 1.3 %collective-permute-start.5 = (f32[64,1024]{1,0:T(8,128)S(1)}, f32[64,1024]{1,0:T(8,128)S(1)}, u32[]{:S(2)}, u32[]{:S(2)}) collective-permute-start(f32[64,1024]{1,0:T(8,128)S(1)} %get-tuple-element.55), channel_id=1, source_target_pairs={{0,2},{1,3},{4,6},{5,7},{8,10},{9,11},{12,14},{13,15},{16,18},{17,... | collective-permute-start | bytes 786440 | tf_op jit(solution)/shard_map/ppermute | solution.py:550
  40.0 1.3 %collective-permute-start.3 = (f32[32,1024]{1,0:T(8,128)S(1)}, f32[32,1024]{1,0:T(8,128)S(1)}, u32[]{:S(2)}, u32[]{:S(2)}) collective-permute-start(f32[32,1024]{1,0:T(8,128)S(1)} %get-tuple-element.47.refs_1_), channel_id=1, source_target_pairs={{2,0},{3,1},{6,4},{7,5},{10,8},{11,9},{14,12},{15,13},{18,16},{19,... | collective-permute-start | bytes 393224 | tf_op jit(solution)/shard_map/ppermute | solution.py:553
  41.3 1.3 %collective-permute-start.8 = (f32[32,1024]{1,0:T(8,128)S(1)}, f32[32,1024]{1,0:T(8,128)S(1)}, u32[]{:S(2)}, u32[]{:S(2)}) collective-permute-start(f32[32,1024]{1,0:T(8,128)S(1)} %get-tuple-element.62.refs_1_.refs_3_), channel_id=1, source_target_pairs={{2,0},{3,1},{6,4},{7,5},{10,8},{11,9},{14,12},{15,13},{18,16},{19,... | collective-permute-start | bytes 393224 | tf_op jit(solution)/shard_map/ppermute | solution.py:553
  42.6 5.1 %collective-permute-done.3.carried = f32[32,1024]{1,0:T(8,128)S(1)} collective-permute-done((f32[32,1024]{1,0:T(8,128)S(1)}, f32[32,1024]{1,0:T(8,128)S(1)}, u32[]{:S(2)}, u32[]{:S(2)}) %collective-permute-start.3) | collective-permute-done | bytes 131104 | tf_op jit(solution)/shard_map/ppermute | solution.py:553
  47.8 3.0 %shard_map.95 = (f32[32,1024]{1,0:T(8,128)S(1)}, f32[32,1024]{1,0:T(8,128)S(1)}, f32[32,1024]{1,0:T(8,128)S(1)}, f32[32,1024]{1,0:T(8,128)S(1)}) custom-call(f32[136,1024]{1,0:T(8,128)S(1)} %get-tuple-element.42.keep, f32[136,1024]{1,0:T(8,128)S(1)} %collective-permute-done.recv, ...), custom_call_target="tpu_custom_call", output_to_operand_aliasing={{0}: (6, {}), {1}: (7, {})} | custom-call | flops 3200000000 | tf_op jit(solution)/shard_map/pallas_call | solution.py:76
  50.8 0.0 collective-permute-done.5.refs_0_.carried
  50.8 0.2 shard_map.105
  51.0 1.3 %collective-permute-start.12 = (f32[40,1024]{1,0:T(8,128)S(1)}, f32[40,1024]{1,0:T(8,128)S(1)}, u32[]{:S(2)}, u32[]{:S(2)}) collective-permute-start(f32[40,1024]{1,0:T(8,128)S(1)} %get-tuple-element.76), channel_id=1, source_target_pairs={{2,0},{3,1},{6,4},{7,5},{10,8},{11,9},{14,12},{15,13},{18,16},{19,... | collective-permute-start | bytes 491528 | tf_op jit(solution)/shard_map/ppermute | solution.py:553
  52.3 3.0 %shard_map.101 = (f32[32,1024]{1,0:T(8,128)S(1)}, f32[32,1024]{1,0:T(8,128)S(1)}, f32[32,1024]{1,0:T(8,128)S(1)}, f32[32,1024]{1,0:T(8,128)S(1)}) custom-call(f32[136,1024]{1,0:T(8,128)S(1)} %get-tuple-element.42.keep, f32[136,1024]{1,0:T(8,128)S(1)} %collective-permute-done.recv, ...), custom_call_target="tpu_custom_call", output_to_operand_aliasing={{0}: (6, {}), {1}: (7, {})} | custom-call | flops 3200000000 | tf_op jit(solution)/shard_map/pallas_call | solution.py:76
  55.4 1.6 %collective-permute-start.9 = (f32[32,1024]{1,0:T(8,128)S(1)}, f32[32,1024]{1,0:T(8,128)S(1)}, u32[]{:S(2)}, u32[]{:S(2)}) collective-permute-start(f32[32,1024]{1,0:T(8,128)S(1)} %get-tuple-element.67.f_second.refs_7_), channel_id=1, source_target_pairs={{0,2},{1,3},{4,6},{5,7},{8,10},{9,11},{12,14},{13,15},{16,18},{17,... | collective-permute-start | bytes 393224 | tf_op jit(solution)/shard_map/ppermute | solution.py:550
  57.0 1.3 %collective-permute-start.19 = (f32[448,128]{1,0:T(8,128)S(1)}, f32[448,128]{1,0:T(8,128)S(1)}, u32[]{:S(2)}, u32[]{:S(2)}) collective-permute-start(f32[448,128]{1,0:T(8,128)S(1)} %pad_maximum_fusion.1), channel_id=1, source_target_pairs={{2,0},{3,1},{6,4},{7,5},{10,8},{11,9},{14,12},{15,13},{18,16},{19,... | collective-permute-start | bytes 688136 | tf_op jit(solution)/shard_map/ppermute | solution.py:553
  58.3 4.6 %collective-permute-start.4 = (f32[32,1024]{1,0:T(8,128)S(1)}, f32[32,1024]{1,0:T(8,128)S(1)}, u32[]{:S(2)}, u32[]{:S(2)}) collective-permute-start(f32[32,1024]{1,0:T(8,128)S(1)} %get-tuple-element.52.f_second.refs_3_), channel_id=1, source_target_pairs={{0,2},{1,3},{4,6},{5,7},{8,10},{9,11},{12,14},{13,15},{16,18},{17,... | collective-permute-start | bytes 393224 | tf_op jit(solution)/shard_map/ppermute | solution.py:550
  62.9 0.8 shard_map.106
  63.7 4.5 %collective-permute-start.13 = (f32[64,128]{1,0:T(8,128)S(1)}, f32[64,128]{1,0:T(8,128)S(1)}, u32[]{:S(2)}, u32[]{:S(2)}) collective-permute-start(f32[64,128]{1,0:T(8,128)S(1)} %shard_map.106), channel_id=1, source_target_pairs={{0,16},{1,17},{4,20},{5,21},{8,24},{9,25},{12,28},{13,29},{16,0},{... | collective-permute-start | bytes 98312 | tf_op jit(solution)/shard_map/ppermute | solution.py:563
  68.2 1.3 %collective-permute-start.10 = (f32[32,1024]{1,0:T(8,128)S(1)}, f32[32,1024]{1,0:T(8,128)S(1)}, u32[]{:S(2)}, u32[]{:S(2)}) collective-permute-start(f32[32,1024]{1,0:T(8,128)S(1)} %get-tuple-element.68.refs_1_), channel_id=1, source_target_pairs={{2,0},{3,1},{6,4},{7,5},{10,8},{11,9},{14,12},{15,13},{18,16},{19,... | collective-permute-start | bytes 393224 | tf_op jit(solution)/shard_map/ppermute | solution.py:553
  69.5 0.8 collective-permute-done.13
  70.4 3.6 %collective-permute-start.14 = (f32[128,128]{1,0:T(8,128)S(1)}, f32[128,128]{1,0:T(8,128)S(1)}, u32[]{:S(2)}, u32[]{:S(2)}) collective-permute-start(f32[128,128]{1,0:T(8,128)S(1)} %pad_maximum_fusion.4), channel_id=1, source_target_pairs={{0,8},{1,9},{4,12},{5,13},{8,0},{9,1},{12,4},{13,5},{16,24},{17,25... | collective-permute-start | bytes 196616 | tf_op jit(solution)/shard_map/ppermute | solution.py:563
  74.0 1.3 %collective-permute-start.6 = (f32[64,1024]{1,0:T(8,128)S(1)}, f32[64,1024]{1,0:T(8,128)S(1)}, u32[]{:S(2)}, u32[]{:S(2)}) collective-permute-start(f32[64,1024]{1,0:T(8,128)S(1)} %get-tuple-element.56.refs_1_), channel_id=1, source_target_pairs={{2,0},{3,1},{6,4},{7,5},{10,8},{11,9},{14,12},{15,13},{18,16},{19,... | collective-permute-start | bytes 786440 | tf_op jit(solution)/shard_map/ppermute | solution.py:553
  75.3 1.2 %collective-permute-done.14 = f32[128,128]{1,0:T(8,128)S(1)} collective-permute-done((f32[128,128]{1,0:T(8,128)S(1)}, f32[128,128]{1,0:T(8,128)S(1)}, u32[]{:S(2)}, u32[]{:S(2)}) %collective-permute-start.14) | collective-permute-done | bytes 65568 | tf_op jit(solution)/shard_map/ppermute | solution.py:563
  76.5 2.4 %collective-permute-start.15 = (f32[256,128]{1,0:T(8,128)S(1)}, f32[256,128]{1,0:T(8,128)S(1)}, u32[]{:S(2)}, u32[]{:S(2)}) collective-permute-start(f32[256,128]{1,0:T(8,128)S(1)} %pad_maximum_fusion.2), channel_id=1, source_target_pairs={{0,4},{1,5},{4,0},{5,1},{8,12},{9,13},{12,8},{13,9},{16,20},{17,21... | collective-permute-start | bytes 393224 | tf_op jit(solution)/shard_map/ppermute | solution.py:563
  79.0 1.6 %shard_map.103 = (f32[32,1024]{1,0:T(8,128)S(1)}, f32[32,1024]{1,0:T(8,128)S(1)}) custom-call(f32[32,1024]{1,0:T(8,128)S(1)} %get-tuple-element.66.f_first.refs_6_, f32[32,1024]{1,0:T(8,128)S(1)} %get-tuple-element.67.f_second.refs_7_, f32[64,1024]{1,0:T(8,128)S(1)} %get-tuple-element.53.k_first, ...), custom_call_target="tpu_custom_call", output_to_operand_aliasing={{0}: (6, {}), {1}: (7, {})} | custom-call | flops 1600000000 | tf_op jit(solution)/shard_map/pallas_call | solution.py:76
  80.6 1.7 %collective-permute-done.6.carried = f32[64,1024]{1,0:T(8,128)S(1)} collective-permute-done((f32[64,1024]{1,0:T(8,128)S(1)}, f32[64,1024]{1,0:T(8,128)S(1)}, u32[]{:S(2)}, u32[]{:S(2)}) %collective-permute-start.6) | collective-permute-done | bytes 262176 | tf_op jit(solution)/shard_map/ppermute | solution.py:553
  82.3 1.4 %shard_map.99 = (f32[64,1024]{1,0:T(8,128)S(1)}, f32[64,1024]{1,0:T(8,128)S(1)}) custom-call(f32[32,1024]{1,0:T(8,128)S(1)} %get-tuple-element.51.f_first.refs_2_, f32[32,1024]{1,0:T(8,128)S(1)} %get-tuple-element.52.f_second.refs_3_, f32[64,1024]{1,0:T(8,128)S(1)} %get-tuple-element.53.k_first, ...), custom_call_target="tpu_custom_call", output_to_operand_aliasing={{0}: (6, {}), {1}: (7, {})} | custom-call | flops 1600000000 | tf_op jit(solution)/shard_map/pallas_call | solution.py:76
  83.7 0.1 shard_map.104
  83.8 0.1 collective-permute-start.11
  83.9 2.7 %shard_map.108 = f32[64,128]{1,0:T(8,128)S(1)} custom-call(f32[512,128]{1,0:T(8,128)S(1)} %pad_maximum_fusion.values, f32[448,128]{1,0:T(8,128)S(1)} %collective-permute-done.19.fixed), custom_call_target="tpu_custom_call" | custom-call | flops 400000000 | tf_op jit(solution)/shard_map/pallas_call | solution.py:76
  86.6 1.3 %collective-permute-start.20 = (f32[64,128]{1,0:T(8,128)S(1)}, f32[64,128]{1,0:T(8,128)S(1)}, u32[]{:S(2)}, u32[]{:S(2)}) collective-permute-start(f32[64,128]{1,0:T(8,128)S(1)} %shard_map.108), channel_id=1, source_target_pairs={{0,2},{1,3},{4,6},{5,7},{8,10},{9,11},{12,14},{13,15},{16,18},{17,... | collective-permute-start | bytes 98312 | tf_op jit(solution)/shard_map/ppermute | solution.py:550
  87.9 1.6 %collective-permute-done.20 = f32[64,128]{1,0:T(8,128)S(1)} collective-permute-done((f32[64,128]{1,0:T(8,128)S(1)}, f32[64,128]{1,0:T(8,128)S(1)}, u32[]{:S(2)}, u32[]{:S(2)}) %collective-permute-start.20) | collective-permute-done | bytes 32800 | tf_op jit(solution)/shard_map/ppermute | solution.py:550
  89.5 1.2 %collective-permute-done.21.q_recv = f32[64,128]{1,0:T(8,128)S(1)} collective-permute-done((f32[64,128]{1,0:T(8,128)S(1)}, f32[64,128]{1,0:T(8,128)S(1)}, u32[]{:S(2)}, u32[]{:S(2)}) %collective-permute-start.21) | collective-permute-done | bytes 32800 | tf_op jit(solution)/shard_map/ppermute | solution.py:547
  90.7 1.2 %shard_map.109 = f32[128,1024]{1,0:T(8,128)} custom-call(f32[96,1024]{1,0:T(8,128)S(1)} %get-tuple-element.72.keep, f32[96,1024]{1,0:T(8,128)S(1)} %collective-permute-done.11.recv, f32[64,128]{1,0:T(8,128)S(1)} %broadcast_select_fusion.q_keep, f32[64,128]{1,0:T(8,128)S(1)} %collective-permute-done.21.q_recv, f32[32,1024]{1,0:T(8,128)S(1)} %bitcast.12, ...), custom_call_target="tpu_custom_call" | custom-call | flops 400000000 | tf_op jit(solution)/shard_map/pallas_call | solution.py:76
  (39 shorter events, 0.2 us)
Async XLA Ops:
  0.0 8.5 %copy-start.5 = (s32[1,1,32]{2,1,0:T(1,128)S(1)}, s32[1,1,32]{2,1,0:T(1,128)}, u32[]{:S(2)}) copy-start(s32[1,1,32]{2,1,0:T(1,128)} %param.12) | copy-start | bytes 388
  0.0 6.0 %copy-start.4 = (f32[128,16]{0,1:T(8,128)S(1)}, f32[128,16]{0,1:T(8,128)}, u32[]{:S(2)}) copy-start(f32[128,16]{0,1:T(8,128)} %param.17) | copy-start | bytes 24580
  0.0 10.1 %collective-permute-start.1 = (f32[1024,1024]{1,0:T(8,128)}, f32[1024,1024]{1,0:T(8,128)}, u32[]{:S(2)}, u32[]{:S(2)}) collective-permute-start(f32[1024,1024]{1,0:T(8,128)} %bitcast.17), channel_id=1, source_target_pairs={{0,1},{1,0},{2,3},{3,2},{4,5},{5,4},{6,7},{7,6},{8,9},{9,8},{10,11... | collective-permute-start | bytes 12582920 | tf_op jit(solution)/shard_map/ppermute | solution.py:547
  3.9 2.0 %copy-start = (bf16[2,1024,1024]{2,1,0:T(8,128)(2,1)}, bf16[2,1024,1024]{2,1,0:T(8,128)(2,1)S(1)}, u32[]{:S(2)}) copy-start(bf16[2,1024,1024]{2,1,0:T(8,128)(2,1)S(1)} %get-tuple-element.44.own) | copy-start | bytes 12582916
  6.0 4.0 %collective-permute-start = (f32[136,1024]{1,0:T(8,128)S(1)}, f32[136,1024]{1,0:T(8,128)S(1)}, u32[]{:S(2)}, u32[]{:S(2)}) collective-permute-start(f32[136,1024]{1,0:T(8,128)S(1)} %get-tuple-element.43), channel_id=1, source_target_pairs={{0,1},{1,0},{2,3},{3,2},{4,5},{5,4},{6,7},{7,6},{8,9},{9,8},{10,11... | collective-permute-start | bytes 1671176 | tf_op jit(solution)/shard_map/ppermute | solution.py:547
  7.8 0.8 collective-permute-start.16
  8.6 0.7 collective-permute-start.17
  9.3 47.7 %collective-permute-start.18 = (f32[224,128]{1,0:T(8,128)S(1)}, f32[224,128]{1,0:T(8,128)S(1)}, u32[]{:S(2)}, u32[]{:S(2)}) collective-permute-start(f32[224,128]{1,0:T(8,128)S(1)} %pad_maximum_fusion.3), channel_id=1, source_target_pairs={{2,6},{3,7},{6,2},{7,3},{10,14},{11,15},{14,10},{15,11},{18,22},{1... | collective-permute-start | bytes 344072 | tf_op jit(solution)/shard_map/ppermute | solution.py:563
  10.1 2.2 %copy-start.1 = (bf16[2,1024,1024]{2,1,0:T(8,128)(2,1)S(1)}, bf16[2,1024,1024]{2,1,0:T(8,128)(2,1)}, u32[]{:S(2)}) copy-start(bf16[2,1024,1024]{2,1,0:T(8,128)(2,1)} %copy-done) | copy-start | bytes 12582916
  15.5 24.5 %collective-permute-start.2 = (f32[32,1024]{1,0:T(8,128)S(1)}, f32[32,1024]{1,0:T(8,128)S(1)}, u32[]{:S(2)}, u32[]{:S(2)}) collective-permute-start(f32[32,1024]{1,0:T(8,128)S(1)} %get-tuple-element.46.f_second.refs_1_), channel_id=1, source_target_pairs={{0,2},{1,3},{4,6},{5,7},{8,10},{9,11},{12,14},{13,15},{16,18},{17,... | collective-permute-start | bytes 393224 | tf_op jit(solution)/shard_map/ppermute | solution.py:550
  34.7 6.6 %collective-permute-start.7 = (f32[32,1024]{1,0:T(8,128)S(1)}, f32[32,1024]{1,0:T(8,128)S(1)}, u32[]{:S(2)}, u32[]{:S(2)}) collective-permute-start(f32[32,1024]{1,0:T(8,128)S(1)} %get-tuple-element.61.f_second.refs_5_), channel_id=1, source_target_pairs={{0,2},{1,3},{4,6},{5,7},{8,10},{9,11},{12,14},{13,15},{16,18},{17,... | collective-permute-start | bytes 393224 | tf_op jit(solution)/shard_map/ppermute | solution.py:550
  38.6 12.1 %collective-permute-start.5 = (f32[64,1024]{1,0:T(8,128)S(1)}, f32[64,1024]{1,0:T(8,128)S(1)}, u32[]{:S(2)}, u32[]{:S(2)}) collective-permute-start(f32[64,1024]{1,0:T(8,128)S(1)} %get-tuple-element.55), channel_id=1, source_target_pairs={{0,2},{1,3},{4,6},{5,7},{8,10},{9,11},{12,14},{13,15},{16,18},{17,... | collective-permute-start | bytes 786440 | tf_op jit(solution)/shard_map/ppermute | solution.py:550
  40.0 7.8 %collective-permute-start.3 = (f32[32,1024]{1,0:T(8,128)S(1)}, f32[32,1024]{1,0:T(8,128)S(1)}, u32[]{:S(2)}, u32[]{:S(2)}) collective-permute-start(f32[32,1024]{1,0:T(8,128)S(1)} %get-tuple-element.47.refs_1_), channel_id=1, source_target_pairs={{2,0},{3,1},{6,4},{7,5},{10,8},{11,9},{14,12},{15,13},{18,16},{19,... | collective-permute-start | bytes 393224 | tf_op jit(solution)/shard_map/ppermute | solution.py:553
  41.3 11.0 %collective-permute-start.8 = (f32[32,1024]{1,0:T(8,128)S(1)}, f32[32,1024]{1,0:T(8,128)S(1)}, u32[]{:S(2)}, u32[]{:S(2)}) collective-permute-start(f32[32,1024]{1,0:T(8,128)S(1)} %get-tuple-element.62.refs_1_.refs_3_), channel_id=1, source_target_pairs={{2,0},{3,1},{6,4},{7,5},{10,8},{11,9},{14,12},{15,13},{18,16},{19,... | collective-permute-start | bytes 393224 | tf_op jit(solution)/shard_map/ppermute | solution.py:553
  51.0 11.8 %collective-permute-start.12 = (f32[40,1024]{1,0:T(8,128)S(1)}, f32[40,1024]{1,0:T(8,128)S(1)}, u32[]{:S(2)}, u32[]{:S(2)}) collective-permute-start(f32[40,1024]{1,0:T(8,128)S(1)} %get-tuple-element.76), channel_id=1, source_target_pairs={{2,0},{3,1},{6,4},{7,5},{10,8},{11,9},{14,12},{15,13},{18,16},{19,... | collective-permute-start | bytes 491528 | tf_op jit(solution)/shard_map/ppermute | solution.py:553
  55.4 12.8 %collective-permute-start.9 = (f32[32,1024]{1,0:T(8,128)S(1)}, f32[32,1024]{1,0:T(8,128)S(1)}, u32[]{:S(2)}, u32[]{:S(2)}) collective-permute-start(f32[32,1024]{1,0:T(8,128)S(1)} %get-tuple-element.67.f_second.refs_7_), channel_id=1, source_target_pairs={{0,2},{1,3},{4,6},{5,7},{8,10},{9,11},{12,14},{13,15},{16,18},{17,... | collective-permute-start | bytes 393224 | tf_op jit(solution)/shard_map/ppermute | solution.py:550
  57.0 26.9 %collective-permute-start.19 = (f32[448,128]{1,0:T(8,128)S(1)}, f32[448,128]{1,0:T(8,128)S(1)}, u32[]{:S(2)}, u32[]{:S(2)}) collective-permute-start(f32[448,128]{1,0:T(8,128)S(1)} %pad_maximum_fusion.1), channel_id=1, source_target_pairs={{2,0},{3,1},{6,4},{7,5},{10,8},{11,9},{14,12},{15,13},{18,16},{19,... | collective-permute-start | bytes 688136 | tf_op jit(solution)/shard_map/ppermute | solution.py:553
  58.3 15.7 %collective-permute-start.4 = (f32[32,1024]{1,0:T(8,128)S(1)}, f32[32,1024]{1,0:T(8,128)S(1)}, u32[]{:S(2)}, u32[]{:S(2)}) collective-permute-start(f32[32,1024]{1,0:T(8,128)S(1)} %get-tuple-element.52.f_second.refs_3_), channel_id=1, source_target_pairs={{0,2},{1,3},{4,6},{5,7},{8,10},{9,11},{12,14},{13,15},{16,18},{17,... | collective-permute-start | bytes 393224 | tf_op jit(solution)/shard_map/ppermute | solution.py:550
  63.7 6.7 %collective-permute-start.13 = (f32[64,128]{1,0:T(8,128)S(1)}, f32[64,128]{1,0:T(8,128)S(1)}, u32[]{:S(2)}, u32[]{:S(2)}) collective-permute-start(f32[64,128]{1,0:T(8,128)S(1)} %shard_map.106), channel_id=1, source_target_pairs={{0,16},{1,17},{4,20},{5,21},{8,24},{9,25},{12,28},{13,29},{16,0},{... | collective-permute-start | bytes 98312 | tf_op jit(solution)/shard_map/ppermute | solution.py:563
  68.2 10.8 %collective-permute-start.10 = (f32[32,1024]{1,0:T(8,128)S(1)}, f32[32,1024]{1,0:T(8,128)S(1)}, u32[]{:S(2)}, u32[]{:S(2)}) collective-permute-start(f32[32,1024]{1,0:T(8,128)S(1)} %get-tuple-element.68.refs_1_), channel_id=1, source_target_pairs={{2,0},{3,1},{6,4},{7,5},{10,8},{11,9},{14,12},{15,13},{18,16},{19,... | collective-permute-start | bytes 393224 | tf_op jit(solution)/shard_map/ppermute | solution.py:553
  70.4 6.1 %collective-permute-start.14 = (f32[128,128]{1,0:T(8,128)S(1)}, f32[128,128]{1,0:T(8,128)S(1)}, u32[]{:S(2)}, u32[]{:S(2)}) collective-permute-start(f32[128,128]{1,0:T(8,128)S(1)} %pad_maximum_fusion.4), channel_id=1, source_target_pairs={{0,8},{1,9},{4,12},{5,13},{8,0},{9,1},{12,4},{13,5},{16,24},{17,25... | collective-permute-start | bytes 196616 | tf_op jit(solution)/shard_map/ppermute | solution.py:563
  74.0 8.3 %collective-permute-start.6 = (f32[64,1024]{1,0:T(8,128)S(1)}, f32[64,1024]{1,0:T(8,128)S(1)}, u32[]{:S(2)}, u32[]{:S(2)}) collective-permute-start(f32[64,1024]{1,0:T(8,128)S(1)} %get-tuple-element.56.refs_1_), channel_id=1, source_target_pairs={{2,0},{3,1},{6,4},{7,5},{10,8},{11,9},{14,12},{15,13},{18,16},{19,... | collective-permute-start | bytes 786440 | tf_op jit(solution)/shard_map/ppermute | solution.py:553
  76.5 7.4 %collective-permute-start.15 = (f32[256,128]{1,0:T(8,128)S(1)}, f32[256,128]{1,0:T(8,128)S(1)}, u32[]{:S(2)}, u32[]{:S(2)}) collective-permute-start(f32[256,128]{1,0:T(8,128)S(1)} %pad_maximum_fusion.2), channel_id=1, source_target_pairs={{0,4},{1,5},{4,0},{5,1},{8,12},{9,13},{12,8},{13,9},{16,20},{17,21... | collective-permute-start | bytes 393224 | tf_op jit(solution)/shard_map/ppermute | solution.py:563
  82.3 8.5 %copy-start.2 = (f32[1,1,32,1024]{3,2,1,0:T(8,128)S(1)}, f32[1,1,32,1024]{3,2,1,0:T(8,128)}, u32[]{:S(2)}) copy-start(f32[1,1,32,1024]{3,2,1,0:T(8,128)} %param.15) | copy-start | bytes 393220
  82.3 8.5 %copy-start.3 = (f32[1,1,32,1024]{3,2,1,0:T(8,128)S(1)}, f32[1,1,32,1024]{3,2,1,0:T(8,128)}, u32[]{:S(2)}) copy-start(f32[1,1,32,1024]{3,2,1,0:T(8,128)} %param.16) | copy-start | bytes 393220
  83.8 6.9 %collective-permute-start.11 = (f32[96,1024]{1,0:T(8,128)S(1)}, f32[96,1024]{1,0:T(8,128)S(1)}, u32[]{:S(2)}, u32[]{:S(2)}) collective-permute-start(f32[96,1024]{1,0:T(8,128)S(1)} %get-tuple-element.73), channel_id=1, source_target_pairs={{0,1},{1,0},{2,3},{3,2},{4,5},{5,4},{6,7},{7,6},{8,9},{9,8},{10,11... | collective-permute-start | bytes 1179656 | tf_op jit(solution)/shard_map/ppermute | solution.py:547
  86.6 2.9 %collective-permute-start.20 = (f32[64,128]{1,0:T(8,128)S(1)}, f32[64,128]{1,0:T(8,128)S(1)}, u32[]{:S(2)}, u32[]{:S(2)}) collective-permute-start(f32[64,128]{1,0:T(8,128)S(1)} %shard_map.108), channel_id=1, source_target_pairs={{0,2},{1,3},{4,6},{5,7},{8,10},{9,11},{12,14},{13,15},{16,18},{17,... | collective-permute-start | bytes 98312 | tf_op jit(solution)/shard_map/ppermute | solution.py:550
  89.5 1.2 %collective-permute-start.21 = (f32[64,128]{1,0:T(8,128)S(1)}, f32[64,128]{1,0:T(8,128)S(1)}, u32[]{:S(2)}, u32[]{:S(2)}) collective-permute-start(f32[64,128]{1,0:T(8,128)S(1)} %broadcast_select_fusion.q_keep), channel_id=1, source_target_pairs={{0,1},{1,0},{2,3},{3,2},{4,5},{5,4},{6,7},{7,6},{8,9},{9,8},{10,11... | collective-permute-start | bytes 98312 | tf_op jit(solution)/shard_map/ppermute | solution.py:547

commit v5 on v4

--- a/solution.py
+++ b/solution.py
@@ -115,14 +115,8 @@
         copy.start()
     for copy in copies:
         copy.wait()
-    share, prim = inverse.shape[1], schur.shape[0]
-    unit = lax.broadcasted_iota(jnp.int32, (share, share), 0) == lax.broadcasted_iota(
-        jnp.int32, (share, share), 1
-    )
-    unit = unit.astype(f32).astype(bf16)
-    top, low = halves(inverse[...])
-    rest = (inverse[...] - top.astype(f32) - low.astype(f32)).astype(bf16)
-    out[:share, :] = dot_rows(unit, top) + dot_rows(unit, low) + dot_rows(unit, rest)
+    share, prim = inverse.shape[0], schur.shape[0]
+    out[:share, :] = inverse[...]
     out[share : share + prim, :] = jnp.zeros_like(out[share : share + prim, :])
     out[share : share + prim, :prim] = schur[...]
     out[share + prim :, :] = jnp.full_like(out[share + prim :, :], -1.0)
@@ -175,24 +169,12 @@
         out[half + extra + 1 : half + extra + 2, :prim] = index[...].astype(f32)
 
 
-def split(matrix, own, weights, buffer, sems):
-    step = matrix.shape[0] // PIECES
-    pieces = [
-        pltpu.make_async_copy(
-            matrix.at[pl.ds(i * step, step)], buffer.at[pl.ds(i * step, step)], sems.at[i]
-        )
-        for i in range(PIECES)
-    ]
-    for copy in pieces:
-        copy.start()
+def split(matrix, own, weights):
     here = member()
     weights[here] = own[...]
-    for i, copy in enumerate(pieces):
-        cols = pl.ds(i * step, step)
-        copy.wait()
-        top, low = halves(buffer[cols, :])
-        weights[1 - here, 0, cols, :] = top
-        weights[1 - here, 1, cols, :] = low
+    top, low = halves(matrix[...])
+    weights[1 - here, 0] = top
+    weights[1 - here, 1] = low
 
 
 def diagonals(keep, recv):
@@ -586,17 +568,17 @@
     (fixed,) = call(
         fix,
         [struct((share + prim + 8, coarse_count))],
-        [coarse_inverse, schur_small[0], coarse_map],
+        [coarse_inverse.T, schur_small[0], coarse_map],
         0.1,
         scratch=[
-            pltpu.VMEM(coarse_inverse.shape, f32),
+            pltpu.VMEM((share, coarse_count), f32),
             pltpu.VMEM((prim, prim), f32),
             pltpu.VMEM(coarse_map.shape, jnp.int32),
             pltpu.SemaphoreType.DMA((3,)),
         ],
         hbm=(0, 1, 2),
     )
-    fixed = gather(fixed, 1)
+    fixed = gather(fixed, 0)
 
     own, keep, send = call(
         first_products,
@@ -614,14 +596,7 @@
         hbm=(0, 1, 2, 3, 4, 5),
     )
     recv = swap(send)
-    weights = call(
-        split,
-        [struct((2, 2, size, size), bf16)],
-        [other_matrix, own],
-        1,
-        scratch=[pltpu.VMEM((size, size), f32), pltpu.SemaphoreType.DMA((PIECES,))],
-        hbm=(0,),
-    )
+    weights = call(split, [struct((2, 2, size, size), bf16)], [other_matrix, own], 1)
     place = jnp.arange(size, dtype=jnp.int32)
     own_spots = (primal_index[0, 0][:, None] == place).astype(f32)
     oth_spots = (recv[half + extra + 1, :prim][:, None] == place.astype(f32)).astype(f32)
@@ -711,7 +686,6 @@
     m_keep, m_send = call(settle, like(2, half + prim), pieces, 0.5)
     m_recv = swap(m_send)
 
-    fixed = fall(fixed)
     (q,) = call(
         functools.partial(solve, subs, prim),
         [struct((half, width))],

time: 92.5 us -> 80.1 us (0.87)
  starting transfers between devices: 49.3 us -> 38.9 us
  local copies, waits for them, and re-layouts: 4.96 us -> 0.02 us
  waiting for transfers between devices: 11.7 us -> 16.5 us
  Pallas kernels: 25.2 us -> 23.6 us
    ppermute x6, starting transfers between devices: 28.4 us -> 8.1 us  [rise(): return lax.ppermute(x, 'slab', [(0, 2), (1, 3)])]
    ppermute x6, starting transfers between devices: 12.6 us -> 23.7 us  [gather(): other = lax.ppermute(x, ('sub', 'slab'), pairs)]
    unnamed x13 -> x6, local copies, waits for them, and re-layouts: 4.96 us -> 0.01 us
    ppermute x6, waiting for transfers between devices: 2.06 us -> 6.41 us  [gather(): other = lax.ppermute(x, ('sub', 'slab'), pairs)]
    pallas_call x19, Pallas kernels: 25.2 us -> 23.6 us  [call(): pl.pallas_call(body, out_shape=outs, in_specs=specs, out_specs=[spec(pltp...]
    ppermute x6 -> x5, starting transfers between devices: 7.75 us -> 6.46 us  [fall(): return lax.ppermute(x, 'slab', [(2, 0), (3, 1)])]
    ppermute x6 -> x5, waiting for transfers between devices: 6.85 us -> 7.3 us  [fall(): return lax.ppermute(x, 'slab', [(2, 0), (3, 1)])]
  transfers between devices with their start and end apart: 22 -> 21, of which waited for: 6 -> 8; matrix products, arithmetic and copies ran while one was open for 1% -> 0% of each run, Pallas kernels for 26% -> 28%
where the time goes in v5:
time: 80.1 us; the launch traced here: 79.6 us
  starting transfers between devices  38.9 us (49%)
  Pallas kernels  23.6 us (29%)
  waiting for transfers between devices  16.5 us (21%)
    ppermute x6, starting transfers between devices, gather(): other = lax.ppermute(x, ('sub', 'slab'), pairs)  23.7 us
    pallas_call x19, Pallas kernels, call(): pl.pallas_call(body, out_shape=outs, in_specs=specs, out_specs=[spec(pltp...  23.6 us
    ppermute x6, starting transfers between devices, rise(): return lax.ppermute(x, 'slab', [(0, 2), (1, 3)])  8.1 us
    ppermute x5, waiting for transfers between devices, fall(): return lax.ppermute(x, 'slab', [(2, 0), (3, 1)])  7.3 us
    ppermute x5, starting transfers between devices, fall(): return lax.ppermute(x, 'slab', [(2, 0), (3, 1)])  6.46 us
    ppermute x6, waiting for transfers between devices, gather(): other = lax.ppermute(x, ('sub', 'slab'), pairs)  6.41 us
  transfers between devices with their start and end apart: 21, of which 8 were waited for; matrix products, arithmetic and copies ran while one was open for 0% of the time, Pallas kernels for 28%

profile of v5, /device:TPU:0, one launch (start us, length us, event | category | flops | bytes accessed | tf_op | source)
XLA Modules:
  0.0 79.6 jit_solution(15492290589662970847)
XLA Ops:
  0.0 0.5 collective-permute-start.1
  0.5 3.4 %shard_map.91 = (bf16[2,1024,1024]{2,1,0:T(8,128)(2,1)S(1)}, f32[136,1024]{1,0:T(8,128)S(1)}, f32[136,1024]{1,0:T(8,128)S(1)}) custom-call(f32[1024,1024]{1,0:T(8,128)} %bitcast.19, f32[128,1024]{1,0:T(8,128)} %bitcast.20, f32[32,1024]{1,0:T(8,128)} %bitcast.12, f32[32,1024]{1,0:T(8,128)} %bitcast.14, f32[1,1024]{1,0:T(1,128)} %bitcast.23, s32[1,32]{1,0:T(1,128)} %bitcast.16), custom_call_target="tpu_custom_call" | custom-call | flops 1600000000 | tf_op jit(solution)/shard_map/pallas_call | solution.py:76
  3.9 0.1 collective-permute-start
  4.0 0.8 shard_map.107
  4.8 6.0 %collective-permute-start.16 = (f32[56,128]{1,0:T(8,128)S(1)}, f32[56,128]{1,0:T(8,128)S(1)}, u32[]{:S(2)}, u32[]{:S(2)}) collective-permute-start(f32[56,128]{1,0:T(8,128)S(1)} %shard_map.107), channel_id=1, source_target_pairs={{0,16},{1,17},{4,20},{5,21},{8,24},{9,25},{12,28},{13,29},{16,0},{... | collective-permute-start | bytes 86024 | tf_op jit(solution)/shard_map/ppermute | solution.py:545
  10.8 0.1 fusion.own_spots
  10.9 1.7 %collective-permute-done.16 = f32[56,128]{1,0:T(8,128)S(1)} collective-permute-done((f32[56,128]{1,0:T(8,128)S(1)}, f32[56,128]{1,0:T(8,128)S(1)}, u32[]{:S(2)}, u32[]{:S(2)}) %collective-permute-start.16) | collective-permute-done | bytes 28704 | tf_op jit(solution)/shard_map/ppermute | solution.py:545
  12.6 3.8 %collective-permute-start.17 = (f32[112,128]{1,0:T(8,128)S(1)}, f32[112,128]{1,0:T(8,128)S(1)}, u32[]{:S(2)}, u32[]{:S(2)}) collective-permute-start(f32[112,128]{1,0:T(8,128)S(1)} %pad_maximum_fusion.5), channel_id=1, source_target_pairs={{0,8},{1,9},{4,12},{5,13},{8,0},{9,1},{12,4},{13,5},{16,24},{17,25... | collective-permute-start | bytes 172040 | tf_op jit(solution)/shard_map/ppermute | solution.py:545
  16.4 2.3 %collective-permute-done.17 = f32[112,128]{1,0:T(8,128)S(1)} collective-permute-done((f32[112,128]{1,0:T(8,128)S(1)}, f32[112,128]{1,0:T(8,128)S(1)}, u32[]{:S(2)}, u32[]{:S(2)}) %collective-permute-start.17) | collective-permute-done | bytes 57376 | tf_op jit(solution)/shard_map/ppermute | solution.py:545
  18.7 4.0 %collective-permute-start.18 = (f32[224,128]{1,0:T(8,128)S(1)}, f32[224,128]{1,0:T(8,128)S(1)}, u32[]{:S(2)}, u32[]{:S(2)}) collective-permute-start(f32[224,128]{1,0:T(8,128)S(1)} %pad_maximum_fusion.3), channel_id=1, source_target_pairs={{0,4},{1,5},{4,0},{5,1},{8,12},{9,13},{12,8},{13,9},{16,20},{17,21... | collective-permute-start | bytes 344072 | tf_op jit(solution)/shard_map/ppermute | solution.py:545
  22.7 0.0 collective-permute-done.recv
  22.7 0.1 compare_convert_fusion.oth_spots
  22.8 0.0 collective-permute-done.1.matrix
  22.8 1.0 %shard_map.92.refs_0_.refs_1_ = bf16[2,2,1024,1024]{3,2,1,0:T(8,128)(2,1)S(1)} custom-call(f32[1024,1024]{1,0:T(8,128)S(1)} %collective-permute-done.1.matrix, bf16[2,1024,1024]{2,1,0:T(8,128)(2,1)S(1)} %get-tuple-element.44.own), custom_call_target="tpu_custom_call" | custom-call | flops 800000000 | tf_op jit(solution)/shard_map/pallas_call | solution.py:76
  23.8 0.8 %shard_map.93 = (f32[32,1024]{1,0:T(8,128)S(1)}, f32[32,1024]{1,0:T(8,128)S(1)}) custom-call(f32[136,1024]{1,0:T(8,128)S(1)} %get-tuple-element.42.keep, f32[136,1024]{1,0:T(8,128)S(1)} %collective-permute-done.recv, bf16[2,2,1024,1024]{3,2,1,0:T(8,128)(2,1)S(1)} %shard_map.92.refs_0_.refs_1_), custom_call_target="tpu_custom_call" | custom-call | flops 800000000 | tf_op jit(solution)/shard_map/pallas_call | solution.py:76
  24.7 1.3 %collective-permute-start.2 = (f32[32,1024]{1,0:T(8,128)S(1)}, f32[32,1024]{1,0:T(8,128)S(1)}, u32[]{:S(2)}, u32[]{:S(2)}) collective-permute-start(f32[32,1024]{1,0:T(8,128)S(1)} %get-tuple-element.46.f_second.refs_1_), channel_id=1, source_target_pairs={{0,2},{1,3},{4,6},{5,7},{8,10},{9,11},{12,14},{13,15},{16,18},{17,... | collective-permute-start | bytes 393224 | tf_op jit(solution)/shard_map/ppermute | solution.py:532
  26.0 0.9 %shard_map.96 = (f32[32,1024]{1,0:T(8,128)S(1)}, f32[32,1024]{1,0:T(8,128)S(1)}, f32[64,1024]{1,0:T(8,128)S(1)}, f32[64,1024]{1,0:T(8,128)S(1)}) custom-call(f32[136,1024]{1,0:T(8,128)S(1)} %get-tuple-element.42.keep, f32[136,1024]{1,0:T(8,128)S(1)} %collective-permute-done.recv, bf16[2,2,1024,1024]{3,2,1,0:T(8,128)(2,1)S(1)} %shard_map.92.refs_0_.refs_1_), custom_call_target="tpu_custom_call" | custom-call | flops 800000000 | tf_op jit(solution)/shard_map/pallas_call | solution.py:76
  26.9 1.3 %collective-permute-start.7 = (f32[32,1024]{1,0:T(8,128)S(1)}, f32[32,1024]{1,0:T(8,128)S(1)}, u32[]{:S(2)}, u32[]{:S(2)}) collective-permute-start(f32[32,1024]{1,0:T(8,128)S(1)} %get-tuple-element.61.f_second.refs_5_), channel_id=1, source_target_pairs={{0,2},{1,3},{4,6},{5,7},{8,10},{9,11},{12,14},{13,15},{16,18},{17,... | collective-permute-start | bytes 393224 | tf_op jit(solution)/shard_map/ppermute | solution.py:532
  28.2 2.6 %shard_map.97 = (f32[32,1024]{1,0:T(8,128)S(1)}, f32[32,1024]{1,0:T(8,128)S(1)}, f32[64,1024]{1,0:T(8,128)S(1)}) custom-call(f32[32,1024]{1,0:T(8,128)S(1)} %fusion.own_spots, f32[32,1024]{1,0:T(8,128)S(1)} %compare_convert_fusion.oth_spots, f32[64,1024]{1,0:T(8,128)S(1)} %get-tuple-element.54.k_second, bf16[2,2,1024,1024]{3,2,1,0:T(8,128)(2,1)S(1)} %shard_map.92.refs_0_.refs_1_), custom_call_target="tpu_custom_call" | custom-call | flops 1600000000 | tf_op jit(solution)/shard_map/pallas_call | solution.py:76
  30.8 1.3 %collective-permute-start.5 = (f32[64,1024]{1,0:T(8,128)S(1)}, f32[64,1024]{1,0:T(8,128)S(1)}, u32[]{:S(2)}, u32[]{:S(2)}) collective-permute-start(f32[64,1024]{1,0:T(8,128)S(1)} %get-tuple-element.55), channel_id=1, source_target_pairs={{0,2},{1,3},{4,6},{5,7},{8,10},{9,11},{12,14},{13,15},{16,18},{17,... | collective-permute-start | bytes 786440 | tf_op jit(solution)/shard_map/ppermute | solution.py:532
  32.1 1.3 %collective-permute-start.3 = (f32[32,1024]{1,0:T(8,128)S(1)}, f32[32,1024]{1,0:T(8,128)S(1)}, u32[]{:S(2)}, u32[]{:S(2)}) collective-permute-start(f32[32,1024]{1,0:T(8,128)S(1)} %get-tuple-element.47.refs_1_), channel_id=1, source_target_pairs={{2,0},{3,1},{6,4},{7,5},{10,8},{11,9},{14,12},{15,13},{18,16},{19,... | collective-permute-start | bytes 393224 | tf_op jit(solution)/shard_map/ppermute | solution.py:535
  33.5 1.3 %collective-permute-start.8 = (f32[32,1024]{1,0:T(8,128)S(1)}, f32[32,1024]{1,0:T(8,128)S(1)}, u32[]{:S(2)}, u32[]{:S(2)}) collective-permute-start(f32[32,1024]{1,0:T(8,128)S(1)} %get-tuple-element.62.refs_1_.refs_3_), channel_id=1, source_target_pairs={{2,0},{3,1},{6,4},{7,5},{10,8},{11,9},{14,12},{15,13},{18,16},{19,... | collective-permute-start | bytes 393224 | tf_op jit(solution)/shard_map/ppermute | solution.py:535
  34.8 5.4 %collective-permute-done.3.carried = f32[32,1024]{1,0:T(8,128)S(1)} collective-permute-done((f32[32,1024]{1,0:T(8,128)S(1)}, f32[32,1024]{1,0:T(8,128)S(1)}, u32[]{:S(2)}, u32[]{:S(2)}) %collective-permute-start.3) | collective-permute-done | bytes 131104 | tf_op jit(solution)/shard_map/ppermute | solution.py:535
  40.2 3.0 %shard_map.95 = (f32[32,1024]{1,0:T(8,128)S(1)}, f32[32,1024]{1,0:T(8,128)S(1)}, f32[32,1024]{1,0:T(8,128)S(1)}, f32[32,1024]{1,0:T(8,128)S(1)}) custom-call(f32[136,1024]{1,0:T(8,128)S(1)} %get-tuple-element.42.keep, f32[136,1024]{1,0:T(8,128)S(1)} %collective-permute-done.recv, ...), custom_call_target="tpu_custom_call", output_to_operand_aliasing={{0}: (6, {}), {1}: (7, {})} | custom-call | flops 3200000000 | tf_op jit(solution)/shard_map/pallas_call | solution.py:76
  43.2 0.0 collective-permute-done.5.refs_0_.carried
  43.2 0.2 shard_map.105
  43.4 1.3 %collective-permute-start.12 = (f32[40,1024]{1,0:T(8,128)S(1)}, f32[40,1024]{1,0:T(8,128)S(1)}, u32[]{:S(2)}, u32[]{:S(2)}) collective-permute-start(f32[40,1024]{1,0:T(8,128)S(1)} %get-tuple-element.76), channel_id=1, source_target_pairs={{2,0},{3,1},{6,4},{7,5},{10,8},{11,9},{14,12},{15,13},{18,16},{19,... | collective-permute-start | bytes 491528 | tf_op jit(solution)/shard_map/ppermute | solution.py:535
  44.7 3.0 %shard_map.101 = (f32[32,1024]{1,0:T(8,128)S(1)}, f32[32,1024]{1,0:T(8,128)S(1)}, f32[32,1024]{1,0:T(8,128)S(1)}, f32[32,1024]{1,0:T(8,128)S(1)}) custom-call(f32[136,1024]{1,0:T(8,128)S(1)} %get-tuple-element.42.keep, f32[136,1024]{1,0:T(8,128)S(1)} %collective-permute-done.recv, ...), custom_call_target="tpu_custom_call", output_to_operand_aliasing={{0}: (6, {}), {1}: (7, {})} | custom-call | flops 3200000000 | tf_op jit(solution)/shard_map/pallas_call | solution.py:76
  47.8 1.6 %collective-permute-start.9 = (f32[32,1024]{1,0:T(8,128)S(1)}, f32[32,1024]{1,0:T(8,128)S(1)}, u32[]{:S(2)}, u32[]{:S(2)}) collective-permute-start(f32[32,1024]{1,0:T(8,128)S(1)} %get-tuple-element.67.f_second.refs_7_), channel_id=1, source_target_pairs={{0,2},{1,3},{4,6},{5,7},{8,10},{9,11},{12,14},{13,15},{16,18},{17,... | collective-permute-start | bytes 393224 | tf_op jit(solution)/shard_map/ppermute | solution.py:532
  49.4 1.3 %collective-permute-start.4 = (f32[32,1024]{1,0:T(8,128)S(1)}, f32[32,1024]{1,0:T(8,128)S(1)}, u32[]{:S(2)}, u32[]{:S(2)}) collective-permute-start(f32[32,1024]{1,0:T(8,128)S(1)} %get-tuple-element.52.f_second.refs_3_), channel_id=1, source_target_pairs={{0,2},{1,3},{4,6},{5,7},{8,10},{9,11},{12,14},{13,15},{16,18},{17,... | collective-permute-start | bytes 393224 | tf_op jit(solution)/shard_map/ppermute | solution.py:532
  50.7 0.8 shard_map.106
  51.5 4.3 %collective-permute-start.13 = (f32[64,128]{1,0:T(8,128)S(1)}, f32[64,128]{1,0:T(8,128)S(1)}, u32[]{:S(2)}, u32[]{:S(2)}) collective-permute-start(f32[64,128]{1,0:T(8,128)S(1)} %shard_map.106), channel_id=1, source_target_pairs={{0,16},{1,17},{4,20},{5,21},{8,24},{9,25},{12,28},{13,29},{16,0},{... | collective-permute-start | bytes 98312 | tf_op jit(solution)/shard_map/ppermute | solution.py:545
  55.9 1.3 %collective-permute-start.10 = (f32[32,1024]{1,0:T(8,128)S(1)}, f32[32,1024]{1,0:T(8,128)S(1)}, u32[]{:S(2)}, u32[]{:S(2)}) collective-permute-start(f32[32,1024]{1,0:T(8,128)S(1)} %get-tuple-element.68.refs_1_), channel_id=1, source_target_pairs={{2,0},{3,1},{6,4},{7,5},{10,8},{11,9},{14,12},{15,13},{18,16},{19,... | collective-permute-start | bytes 393224 | tf_op jit(solution)/shard_map/ppermute | solution.py:535
  57.2 1.0 %collective-permute-done.13 = f32[64,128]{1,0:T(8,128)S(1)} collective-permute-done((f32[64,128]{1,0:T(8,128)S(1)}, f32[64,128]{1,0:T(8,128)S(1)}, u32[]{:S(2)}, u32[]{:S(2)}) %collective-permute-start.13) | collective-permute-done | bytes 32800 | tf_op jit(solution)/shard_map/ppermute | solution.py:545
  58.2 3.4 %collective-permute-start.14 = (f32[128,128]{1,0:T(8,128)S(1)}, f32[128,128]{1,0:T(8,128)S(1)}, u32[]{:S(2)}, u32[]{:S(2)}) collective-permute-start(f32[128,128]{1,0:T(8,128)S(1)} %pad_maximum_fusion.4), channel_id=1, source_target_pairs={{0,8},{1,9},{4,12},{5,13},{8,0},{9,1},{12,4},{13,5},{16,24},{17,25... | collective-permute-start | bytes 196616 | tf_op jit(solution)/shard_map/ppermute | solution.py:545
  61.7 1.3 %collective-permute-start.6 = (f32[64,1024]{1,0:T(8,128)S(1)}, f32[64,1024]{1,0:T(8,128)S(1)}, u32[]{:S(2)}, u32[]{:S(2)}) collective-permute-start(f32[64,1024]{1,0:T(8,128)S(1)} %get-tuple-element.56.refs_1_), channel_id=1, source_target_pairs={{2,0},{3,1},{6,4},{7,5},{10,8},{11,9},{14,12},{15,13},{18,16},{19,... | collective-permute-start | bytes 786440 | tf_op jit(solution)/shard_map/ppermute | solution.py:535
  63.0 1.4 %collective-permute-done.14 = f32[128,128]{1,0:T(8,128)S(1)} collective-permute-done((f32[128,128]{1,0:T(8,128)S(1)}, f32[128,128]{1,0:T(8,128)S(1)}, u32[]{:S(2)}, u32[]{:S(2)}) %collective-permute-start.14) | collective-permute-done | bytes 65568 | tf_op jit(solution)/shard_map/ppermute | solution.py:545
  64.4 2.1 %collective-permute-start.15 = (f32[256,128]{1,0:T(8,128)S(1)}, f32[256,128]{1,0:T(8,128)S(1)}, u32[]{:S(2)}, u32[]{:S(2)}) collective-permute-start(f32[256,128]{1,0:T(8,128)S(1)} %pad_maximum_fusion.2), channel_id=1, source_target_pairs={{0,4},{1,5},{4,0},{5,1},{8,12},{9,13},{12,8},{13,9},{16,20},{17,21... | collective-permute-start | bytes 393224 | tf_op jit(solution)/shard_map/ppermute | solution.py:545
  66.5 1.6 %shard_map.103 = (f32[32,1024]{1,0:T(8,128)S(1)}, f32[32,1024]{1,0:T(8,128)S(1)}) custom-call(f32[32,1024]{1,0:T(8,128)S(1)} %get-tuple-element.66.f_first.refs_6_, f32[32,1024]{1,0:T(8,128)S(1)} %get-tuple-element.67.f_second.refs_7_, f32[64,1024]{1,0:T(8,128)S(1)} %get-tuple-element.53.k_first, ...), custom_call_target="tpu_custom_call", output_to_operand_aliasing={{0}: (6, {}), {1}: (7, {})} | custom-call | flops 1600000000 | tf_op jit(solution)/shard_map/pallas_call | solution.py:76
  68.1 1.9 %collective-permute-done.6.carried = f32[64,1024]{1,0:T(8,128)S(1)} collective-permute-done((f32[64,1024]{1,0:T(8,128)S(1)}, f32[64,1024]{1,0:T(8,128)S(1)}, u32[]{:S(2)}, u32[]{:S(2)}) %collective-permute-start.6) | collective-permute-done | bytes 262176 | tf_op jit(solution)/shard_map/ppermute | solution.py:535
  70.0 1.4 %shard_map.99 = (f32[64,1024]{1,0:T(8,128)S(1)}, f32[64,1024]{1,0:T(8,128)S(1)}) custom-call(f32[32,1024]{1,0:T(8,128)S(1)} %get-tuple-element.51.f_first.refs_2_, f32[32,1024]{1,0:T(8,128)S(1)} %get-tuple-element.52.f_second.refs_3_, f32[64,1024]{1,0:T(8,128)S(1)} %get-tuple-element.53.k_first, ...), custom_call_target="tpu_custom_call", output_to_operand_aliasing={{0}: (6, {}), {1}: (7, {})} | custom-call | flops 1600000000 | tf_op jit(solution)/shard_map/pallas_call | solution.py:76
  71.4 0.1 shard_map.104
  71.5 0.1 collective-permute-start.11
  71.6 2.7 %shard_map.108 = f32[64,128]{1,0:T(8,128)S(1)} custom-call(f32[512,128]{1,0:T(8,128)S(1)} %pad_maximum_fusion.values, f32[448,128]{1,0:T(8,128)S(1)} %pad_maximum_fusion.1.fixed), custom_call_target="tpu_custom_call" | custom-call | flops 400000000 | tf_op jit(solution)/shard_map/pallas_call | solution.py:76
  74.3 1.3 %collective-permute-start.19 = (f32[64,128]{1,0:T(8,128)S(1)}, f32[64,128]{1,0:T(8,128)S(1)}, u32[]{:S(2)}, u32[]{:S(2)}) collective-permute-start(f32[64,128]{1,0:T(8,128)S(1)} %shard_map.108), channel_id=1, source_target_pairs={{0,2},{1,3},{4,6},{5,7},{8,10},{9,11},{12,14},{13,15},{16,18},{17,... | collective-permute-start | bytes 98312 | tf_op jit(solution)/shard_map/ppermute | solution.py:532
  75.6 1.6 %collective-permute-done.19 = f32[64,128]{1,0:T(8,128)S(1)} collective-permute-done((f32[64,128]{1,0:T(8,128)S(1)}, f32[64,128]{1,0:T(8,128)S(1)}, u32[]{:S(2)}, u32[]{:S(2)}) %collective-permute-start.19) | collective-permute-done | bytes 32800 | tf_op jit(solution)/shard_map/ppermute | solution.py:532
  77.2 1.2 %collective-permute-done.20.q_recv = f32[64,128]{1,0:T(8,128)S(1)} collective-permute-done((f32[64,128]{1,0:T(8,128)S(1)}, f32[64,128]{1,0:T(8,128)S(1)}, u32[]{:S(2)}, u32[]{:S(2)}) %collective-permute-start.20) | collective-permute-done | bytes 32800 | tf_op jit(solution)/shard_map/ppermute | solution.py:529
  78.4 1.2 %shard_map.109 = f32[128,1024]{1,0:T(8,128)} custom-call(f32[96,1024]{1,0:T(8,128)S(1)} %get-tuple-element.72.keep, f32[96,1024]{1,0:T(8,128)S(1)} %collective-permute-done.11.recv, f32[64,128]{1,0:T(8,128)S(1)} %broadcast_select_fusion.q_keep, f32[64,128]{1,0:T(8,128)S(1)} %collective-permute-done.20.q_recv, f32[32,1024]{1,0:T(8,128)S(1)} %bitcast.13, ...), custom_call_target="tpu_custom_call" | custom-call | flops 400000000 | tf_op jit(solution)/shard_map/pallas_call | solution.py:76
  (30 shorter events, 0.2 us)
Async XLA Ops:
  0.0 10.8 %copy-start.2 = (s32[1,1,32]{2,1,0:T(1,128)S(1)}, s32[1,1,32]{2,1,0:T(1,128)}, u32[]{:S(2)}) copy-start(s32[1,1,32]{2,1,0:T(1,128)} %param.12) | copy-start | bytes 388
  0.0 22.8 %collective-permute-start.1 = (f32[1024,1024]{1,0:T(8,128)}, f32[1024,1024]{1,0:T(8,128)S(1)}, u32[]{:S(2)}, u32[]{:S(2)}) collective-permute-start(f32[1024,1024]{1,0:T(8,128)} %bitcast.18), channel_id=1, source_target_pairs={{0,1},{1,0},{2,3},{3,2},{4,5},{5,4},{6,7},{7,6},{8,9},{9,8},{10,11... | collective-permute-start | bytes 12582920 | tf_op jit(solution)/shard_map/ppermute | solution.py:529
  3.9 18.8 %collective-permute-start = (f32[136,1024]{1,0:T(8,128)S(1)}, f32[136,1024]{1,0:T(8,128)S(1)}, u32[]{:S(2)}, u32[]{:S(2)}) collective-permute-start(f32[136,1024]{1,0:T(8,128)S(1)} %get-tuple-element.43), channel_id=1, source_target_pairs={{0,1},{1,0},{2,3},{3,2},{4,5},{5,4},{6,7},{7,6},{8,9},{9,8},{10,11... | collective-permute-start | bytes 1671176 | tf_op jit(solution)/shard_map/ppermute | solution.py:529
  4.8 7.8 %collective-permute-start.16 = (f32[56,128]{1,0:T(8,128)S(1)}, f32[56,128]{1,0:T(8,128)S(1)}, u32[]{:S(2)}, u32[]{:S(2)}) collective-permute-start(f32[56,128]{1,0:T(8,128)S(1)} %shard_map.107), channel_id=1, source_target_pairs={{0,16},{1,17},{4,20},{5,21},{8,24},{9,25},{12,28},{13,29},{16,0},{... | collective-permute-start | bytes 86024 | tf_op jit(solution)/shard_map/ppermute | solution.py:545
  12.6 6.1 %collective-permute-start.17 = (f32[112,128]{1,0:T(8,128)S(1)}, f32[112,128]{1,0:T(8,128)S(1)}, u32[]{:S(2)}, u32[]{:S(2)}) collective-permute-start(f32[112,128]{1,0:T(8,128)S(1)} %pad_maximum_fusion.5), channel_id=1, source_target_pairs={{0,8},{1,9},{4,12},{5,13},{8,0},{9,1},{12,4},{13,5},{16,24},{17,25... | collective-permute-start | bytes 172040 | tf_op jit(solution)/shard_map/ppermute | solution.py:545
  18.7 30.7 %collective-permute-start.18 = (f32[224,128]{1,0:T(8,128)S(1)}, f32[224,128]{1,0:T(8,128)S(1)}, u32[]{:S(2)}, u32[]{:S(2)}) collective-permute-start(f32[224,128]{1,0:T(8,128)S(1)} %pad_maximum_fusion.3), channel_id=1, source_target_pairs={{0,4},{1,5},{4,0},{5,1},{8,12},{9,13},{12,8},{13,9},{16,20},{17,21... | collective-permute-start | bytes 344072 | tf_op jit(solution)/shard_map/ppermute | solution.py:545
  24.7 7.4 %collective-permute-start.2 = (f32[32,1024]{1,0:T(8,128)S(1)}, f32[32,1024]{1,0:T(8,128)S(1)}, u32[]{:S(2)}, u32[]{:S(2)}) collective-permute-start(f32[32,1024]{1,0:T(8,128)S(1)} %get-tuple-element.46.f_second.refs_1_), channel_id=1, source_target_pairs={{0,2},{1,3},{4,6},{5,7},{8,10},{9,11},{12,14},{13,15},{16,18},{17,... | collective-permute-start | bytes 393224 | tf_op jit(solution)/shard_map/ppermute | solution.py:532
  26.9 6.6 %collective-permute-start.7 = (f32[32,1024]{1,0:T(8,128)S(1)}, f32[32,1024]{1,0:T(8,128)S(1)}, u32[]{:S(2)}, u32[]{:S(2)}) collective-permute-start(f32[32,1024]{1,0:T(8,128)S(1)} %get-tuple-element.61.f_second.refs_5_), channel_id=1, source_target_pairs={{0,2},{1,3},{4,6},{5,7},{8,10},{9,11},{12,14},{13,15},{16,18},{17,... | collective-permute-start | bytes 393224 | tf_op jit(solution)/shard_map/ppermute | solution.py:532
  30.8 12.4 %collective-permute-start.5 = (f32[64,1024]{1,0:T(8,128)S(1)}, f32[64,1024]{1,0:T(8,128)S(1)}, u32[]{:S(2)}, u32[]{:S(2)}) collective-permute-start(f32[64,1024]{1,0:T(8,128)S(1)} %get-tuple-element.55), channel_id=1, source_target_pairs={{0,2},{1,3},{4,6},{5,7},{8,10},{9,11},{12,14},{13,15},{16,18},{17,... | collective-permute-start | bytes 786440 | tf_op jit(solution)/shard_map/ppermute | solution.py:532
  32.1 8.0 %collective-permute-start.3 = (f32[32,1024]{1,0:T(8,128)S(1)}, f32[32,1024]{1,0:T(8,128)S(1)}, u32[]{:S(2)}, u32[]{:S(2)}) collective-permute-start(f32[32,1024]{1,0:T(8,128)S(1)} %get-tuple-element.47.refs_1_), channel_id=1, source_target_pairs={{2,0},{3,1},{6,4},{7,5},{10,8},{11,9},{14,12},{15,13},{18,16},{19,... | collective-permute-start | bytes 393224 | tf_op jit(solution)/shard_map/ppermute | solution.py:535
  33.5 11.3 %collective-permute-start.8 = (f32[32,1024]{1,0:T(8,128)S(1)}, f32[32,1024]{1,0:T(8,128)S(1)}, u32[]{:S(2)}, u32[]{:S(2)}) collective-permute-start(f32[32,1024]{1,0:T(8,128)S(1)} %get-tuple-element.62.refs_1_.refs_3_), channel_id=1, source_target_pairs={{2,0},{3,1},{6,4},{7,5},{10,8},{11,9},{14,12},{15,13},{18,16},{19,... | collective-permute-start | bytes 393224 | tf_op jit(solution)/shard_map/ppermute | solution.py:535
  43.4 7.3 %collective-permute-start.12 = (f32[40,1024]{1,0:T(8,128)S(1)}, f32[40,1024]{1,0:T(8,128)S(1)}, u32[]{:S(2)}, u32[]{:S(2)}) collective-permute-start(f32[40,1024]{1,0:T(8,128)S(1)} %get-tuple-element.76), channel_id=1, source_target_pairs={{2,0},{3,1},{6,4},{7,5},{10,8},{11,9},{14,12},{15,13},{18,16},{19,... | collective-permute-start | bytes 491528 | tf_op jit(solution)/shard_map/ppermute | solution.py:535
  47.8 8.1 %collective-permute-start.9 = (f32[32,1024]{1,0:T(8,128)S(1)}, f32[32,1024]{1,0:T(8,128)S(1)}, u32[]{:S(2)}, u32[]{:S(2)}) collective-permute-start(f32[32,1024]{1,0:T(8,128)S(1)} %get-tuple-element.67.f_second.refs_7_), channel_id=1, source_target_pairs={{0,2},{1,3},{4,6},{5,7},{8,10},{9,11},{12,14},{13,15},{16,18},{17,... | collective-permute-start | bytes 393224 | tf_op jit(solution)/shard_map/ppermute | solution.py:532
  49.4 12.3 %collective-permute-start.4 = (f32[32,1024]{1,0:T(8,128)S(1)}, f32[32,1024]{1,0:T(8,128)S(1)}, u32[]{:S(2)}, u32[]{:S(2)}) collective-permute-start(f32[32,1024]{1,0:T(8,128)S(1)} %get-tuple-element.52.f_second.refs_3_), channel_id=1, source_target_pairs={{0,2},{1,3},{4,6},{5,7},{8,10},{9,11},{12,14},{13,15},{16,18},{17,... | collective-permute-start | bytes 393224 | tf_op jit(solution)/shard_map/ppermute | solution.py:532
  51.5 6.7 %collective-permute-start.13 = (f32[64,128]{1,0:T(8,128)S(1)}, f32[64,128]{1,0:T(8,128)S(1)}, u32[]{:S(2)}, u32[]{:S(2)}) collective-permute-start(f32[64,128]{1,0:T(8,128)S(1)} %shard_map.106), channel_id=1, source_target_pairs={{0,16},{1,17},{4,20},{5,21},{8,24},{9,25},{12,28},{13,29},{16,0},{... | collective-permute-start | bytes 98312 | tf_op jit(solution)/shard_map/ppermute | solution.py:545
  55.9 10.6 %collective-permute-start.10 = (f32[32,1024]{1,0:T(8,128)S(1)}, f32[32,1024]{1,0:T(8,128)S(1)}, u32[]{:S(2)}, u32[]{:S(2)}) collective-permute-start(f32[32,1024]{1,0:T(8,128)S(1)} %get-tuple-element.68.refs_1_), channel_id=1, source_target_pairs={{2,0},{3,1},{6,4},{7,5},{10,8},{11,9},{14,12},{15,13},{18,16},{19,... | collective-permute-start | bytes 393224 | tf_op jit(solution)/shard_map/ppermute | solution.py:535
  58.2 6.1 %collective-permute-start.14 = (f32[128,128]{1,0:T(8,128)S(1)}, f32[128,128]{1,0:T(8,128)S(1)}, u32[]{:S(2)}, u32[]{:S(2)}) collective-permute-start(f32[128,128]{1,0:T(8,128)S(1)} %pad_maximum_fusion.4), channel_id=1, source_target_pairs={{0,8},{1,9},{4,12},{5,13},{8,0},{9,1},{12,4},{13,5},{16,24},{17,25... | collective-permute-start | bytes 196616 | tf_op jit(solution)/shard_map/ppermute | solution.py:545
  61.7 8.3 %collective-permute-start.6 = (f32[64,1024]{1,0:T(8,128)S(1)}, f32[64,1024]{1,0:T(8,128)S(1)}, u32[]{:S(2)}, u32[]{:S(2)}) collective-permute-start(f32[64,1024]{1,0:T(8,128)S(1)} %get-tuple-element.56.refs_1_), channel_id=1, source_target_pairs={{2,0},{3,1},{6,4},{7,5},{10,8},{11,9},{14,12},{15,13},{18,16},{19,... | collective-permute-start | bytes 786440 | tf_op jit(solution)/shard_map/ppermute | solution.py:535
  64.4 7.2 %collective-permute-start.15 = (f32[256,128]{1,0:T(8,128)S(1)}, f32[256,128]{1,0:T(8,128)S(1)}, u32[]{:S(2)}, u32[]{:S(2)}) collective-permute-start(f32[256,128]{1,0:T(8,128)S(1)} %pad_maximum_fusion.2), channel_id=1, source_target_pairs={{0,4},{1,5},{4,0},{5,1},{8,12},{9,13},{12,8},{13,9},{16,20},{17,21... | collective-permute-start | bytes 393224 | tf_op jit(solution)/shard_map/ppermute | solution.py:545
  70.0 8.5 %copy-start = (f32[1,1,32,1024]{3,2,1,0:T(8,128)S(1)}, f32[1,1,32,1024]{3,2,1,0:T(8,128)}, u32[]{:S(2)}) copy-start(f32[1,1,32,1024]{3,2,1,0:T(8,128)} %param.15) | copy-start | bytes 393220
  70.0 8.5 %copy-start.1 = (f32[1,1,32,1024]{3,2,1,0:T(8,128)S(1)}, f32[1,1,32,1024]{3,2,1,0:T(8,128)}, u32[]{:S(2)}) copy-start(f32[1,1,32,1024]{3,2,1,0:T(8,128)} %param.16) | copy-start | bytes 393220
  71.5 6.9 %collective-permute-start.11 = (f32[96,1024]{1,0:T(8,128)S(1)}, f32[96,1024]{1,0:T(8,128)S(1)}, u32[]{:S(2)}, u32[]{:S(2)}) collective-permute-start(f32[96,1024]{1,0:T(8,128)S(1)} %get-tuple-element.73), channel_id=1, source_target_pairs={{0,1},{1,0},{2,3},{3,2},{4,5},{5,4},{6,7},{7,6},{8,9},{9,8},{10,11... | collective-permute-start | bytes 1179656 | tf_op jit(solution)/shard_map/ppermute | solution.py:529
  74.3 2.9 %collective-permute-start.19 = (f32[64,128]{1,0:T(8,128)S(1)}, f32[64,128]{1,0:T(8,128)S(1)}, u32[]{:S(2)}, u32[]{:S(2)}) collective-permute-start(f32[64,128]{1,0:T(8,128)S(1)} %shard_map.108), channel_id=1, source_target_pairs={{0,2},{1,3},{4,6},{5,7},{8,10},{9,11},{12,14},{13,15},{16,18},{17,... | collective-permute-start | bytes 98312 | tf_op jit(solution)/shard_map/ppermute | solution.py:532
  77.2 1.2 %collective-permute-start.20 = (f32[64,128]{1,0:T(8,128)S(1)}, f32[64,128]{1,0:T(8,128)S(1)}, u32[]{:S(2)}, u32[]{:S(2)}) collective-permute-start(f32[64,128]{1,0:T(8,128)S(1)} %broadcast_select_fusion.q_keep), channel_id=1, source_target_pairs={{0,1},{1,0},{2,3},{3,2},{4,5},{5,4},{6,7},{7,6},{8,9},{9,8},{10,11... | collective-permute-start | bytes 98312 | tf_op jit(solution)/shard_map/ppermute | solution.py:529

commit v6 on v5

--- a/solution.py
+++ b/solution.py
@@ -102,25 +102,6 @@
     def _():
         for old, new in zip(before, after):
             new[...] = old[...]
-
-
-def fix(inverse_far, schur_far, maps_far, out, inverse, schur, maps, sems):
-    copies = [
-        pltpu.make_async_copy(far, near, sems.at[i])
-        for i, (far, near) in enumerate(
-            ((inverse_far, inverse), (schur_far, schur), (maps_far, maps))
-        )
-    ]
-    for copy in copies:
-        copy.start()
-    for copy in copies:
-        copy.wait()
-    share, prim = inverse.shape[0], schur.shape[0]
-    out[:share, :] = inverse[...]
-    out[share : share + prim, :] = jnp.zeros_like(out[share : share + prim, :])
-    out[share : share + prim, :prim] = schur[...]
-    out[share + prim :, :] = jnp.full_like(out[share + prim :, :], -1.0)
-    out[share + prim : share + prim + 1, :prim] = maps[...].astype(f32)
 
 
 def first_products(
@@ -371,7 +352,7 @@
     hold(pair() != 1, old, (y_first, y_second))
 
 
-def score_turn(carried, y_first, y_second, k_first, k_second, *refs):
+def score_turn(carried, schur, maps, y_first, y_second, k_first, k_second, *refs):
     blocks, values = refs[:-1], refs[-1]
     prim = y_first.shape[0]
     half, width = values.shape
@@ -394,6 +375,8 @@
             + only(w[half : half + extra], 2, prim)
             + only(w[half + extra :], 1, prim)
         )
+        values[:prim, 3 * prim : 4 * prim] = schur[...]
+        values[prim : prim + 1, 3 * prim : 4 * prim] = maps[...]
 
 
 def settle(*refs):
@@ -415,8 +398,7 @@
 def solve(subs, prim, values, fixed, q):
     half, width = q.shape
     count = fixed.shape[1]
-    height = fixed.shape[0] // subs
-    share = height - prim - 8
+    share = fixed.shape[0] // subs
     me = lax.axis_index("sub")
     unknown = lax.broadcasted_iota(jnp.int32, (count, width), 0)
     block = unknown // share
@@ -449,8 +431,14 @@
         top, low = halves(right)
         return three(left, top, low)
 
-    def map_of(j):
-        return at(fixed, j, height, share + prim, height)[0:1, :width]
+    def map_of(v):
+        row = pltpu.roll(v[prim : prim + 8, :], width - 3 * prim, 1)[0:1]
+        return jnp.where(lane[0:1] < prim, row, -1.0)
+
+    def times_schur(left, v, signs):
+        rows = [v[:prim] if sign > 0 else -v[:prim] for sign in signs]
+        out = times_plain(left, wide(jnp.concatenate(rows, axis=0), width))
+        return jnp.where(lane < prim, pltpu.roll(out, width - 3 * prim, 1), 0.0)
 
     def spot(row, ids):
         return (ids == row).astype(f32)
@@ -466,24 +454,22 @@
         return both[:half] + both[half:]
 
     def add_first(j, total):
-        return total + pick_rows(at(values, j, half), spot(map_of(j), unknown))
-
-    inverse = jnp.concatenate([at(fixed, j, height, 0, share) for j in range(subs)], axis=0)
+        v = at(values, j, half)
+        return total + pick_rows(v, spot(map_of(v), unknown))
+
+    inverse = fixed[...]
     zero = jnp.zeros((half, count), f32)
     found = times_rows(loop(add_first, zero), inverse)
 
     def parts(j):
         v = at(values, j, half)
-        row = map_of(j)
-        schur = at(fixed, j, height, share, share + prim)[:, :width]
-        first = pick_plain(found, spot(pltpu.roll(row, prim, 1), there)) - times_plain(
-            v, wide(schur, width)
-        )
+        row = map_of(v)
+        first = pick_plain(found, spot(pltpu.roll(row, prim, 1), there)) - times_schur(v, v, (1,))
         change = times_plain(first, wide(v[: 2 * prim], width))
-        return row, schur, first, jnp.where(lane < 2 * prim, v, change)
+        return v, row, first, jnp.where(lane < 2 * prim, v, change)
 
     def add_second(j, total):
-        row, _, _, p = parts(j)
+        _, row, _, p = parts(j)
         signs = (
             spot(row, unknown)
             - spot(pltpu.roll(row, prim, 1), unknown)
@@ -492,9 +478,9 @@
         return total + pick_rows(p, signs)
 
     found_two = times_rows(loop(add_second, zero), inverse)
-    row, schur, first, p = parts(0)
-    second = pick_plain(found_two, spot(pltpu.roll(row, prim, 1), there)) - times_plain(
-        p, wide(jnp.concatenate([schur, -schur, -schur], axis=0), width)
+    v, row, first, p = parts(0)
+    second = pick_plain(found_two, spot(pltpu.roll(row, prim, 1), there)) - times_schur(
+        p, v, (1, -1, -1)
     )
     q[...] = first + pltpu.roll(first + second, 2 * prim, 1)
 
@@ -534,25 +520,21 @@
     def fall(x):
         return lax.ppermute(x, "slab", [(2, 0), (3, 1)])
 
-    def gather(x, which):
-        distance = subs // 2
-        while distance:
-            pairs = [
-                (i * levels + k, (i ^ distance) * levels + k)
-                for i in range(subs)
-                for k in (2 * which, 2 * which + 1)
-            ]
-            other = lax.ppermute(x, ("sub", "slab"), pairs)
-            x = jnp.concatenate([x, other], axis=0)
-            distance //= 2
-        return x
+    def trade(x, distance):
+        pairs = [
+            (i * levels + k, (i ^ distance) * levels + k) for i in range(subs) for k in range(2)
+        ]
+        return lax.ppermute(x, ("sub", "slab"), pairs)
+
+    def join(x, y):
+        return jnp.concatenate([x, y], axis=0)
 
     vector = residual[0, 0]
     matrix = inverse_slab[0, 0]
     one, two = constraint_basis[0, 0], coarse_basis[0, 0]
     rows, size = vector.shape
     prim = primal_index.shape[-1]
-    coarse_count, share = coarse_inverse.shape
+    coarse_count, _ = coarse_inverse.shape
     half = rows // 2
     block = half // BLOCKS
     extra = 2 * prim
@@ -565,20 +547,11 @@
 
     other_matrix = swap(matrix)
 
-    (fixed,) = call(
-        fix,
-        [struct((share + prim + 8, coarse_count))],
-        [coarse_inverse.T, schur_small[0], coarse_map],
-        0.1,
-        scratch=[
-            pltpu.VMEM((share, coarse_count), f32),
-            pltpu.VMEM((prim, prim), f32),
-            pltpu.VMEM(coarse_map.shape, jnp.int32),
-            pltpu.SemaphoreType.DMA((3,)),
-        ],
-        hbm=(0, 1, 2),
-    )
-    fixed = gather(fixed, 0)
+    inverse = coarse_inverse.T
+    distance = subs // 2
+    while distance > 1:
+        inverse = join(inverse, trade(inverse, distance))
+        distance //= 2
 
     own, keep, send = call(
         first_products,
@@ -656,10 +629,20 @@
     (values,) = call(
         score_turn,
         [struct((half, width))],
-        [z_back, y_first, y_second, k_first, k_second, *pieces],
+        [z_back, schur_small[0], coarse_map.astype(f32), y_first, y_second, k_first, k_second, *pieces],
         1,
     )
-    values = gather(values, 0)
+    distance = subs // 2
+    while distance > 1:
+        values = join(values, trade(values, distance))
+        distance //= 2
+    if coarse_count == width:
+        others = trade(join(values, inverse), 1)
+        inverse = join(inverse, others[values.shape[0] :])
+        values = join(values, others[: values.shape[0]])
+    else:
+        inverse = join(inverse, trade(inverse, 1))
+        values = join(values, trade(values, 1))
 
     n_two = []
     for i in span:
@@ -689,9 +672,9 @@
     (q,) = call(
         functools.partial(solve, subs, prim),
         [struct((half, width))],
-        [values, fixed],
+        [values, inverse],
         0.5,
-        limit=VMEM_LIMIT + 8 * (values.size + fixed.size),
+        limit=VMEM_LIMIT + 8 * (values.size + inverse.size),
     )
     q_upper = rise(q)
     q = jnp.where(pair() == 0, q, q_upper)

time: 80.1 us -> 85.2 us (1.064)
  waiting for transfers between devices: 16.5 us -> 21.7 us
    ppermute x6 -> x5, starting transfers between devices: 23.7 us -> 18 us  [trade(): return lax.ppermute(x, ('sub', 'slab'), pairs)]
    ppermute x6, starting transfers between devices: 8.1 us -> 13.7 us  [rise(): return lax.ppermute(x, 'slab', [(0, 2), (1, 3)])]
    ppermute x4, waiting for transfers between devices: 1.21 us -> 5.39 us  [swap(): return lax.ppermute(x, 'slab', [(i, i ^ 1) for i in range(levels)])]
    ppermute x5, waiting for transfers between devices: 7.3 us -> 4.88 us  [fall(): return lax.ppermute(x, 'slab', [(2, 0), (3, 1)])]
    ppermute x6 -> x5, waiting for transfers between devices: 6.41 us -> 8.69 us  [trade(): return lax.ppermute(x, ('sub', 'slab'), pairs)]
    ppermute x6, waiting for transfers between devices: 1.59 us -> 2.73 us  [rise(): return lax.ppermute(x, 'slab', [(0, 2), (1, 3)])]
    pallas_call x19 -> x18, Pallas kernels: 23.6 us -> 23.4 us  [call(): pl.pallas_call(body, out_shape=outs, in_specs=specs, out_specs=[spec(pltp...]
  transfers between devices with their start and end apart: 21 -> 20, of which waited for: 8 -> 10; matrix products, arithmetic and copies ran while one was open for 0% -> 0% of each run, Pallas kernels for 28% -> 21%
where the time goes in v6:
time: 85.2 us; the launch traced here: 84.7 us
  starting transfers between devices  38.8 us (46%)
  Pallas kernels  23.4 us (27%)
  waiting for transfers between devices  21.7 us (25%)
    pallas_call x18, Pallas kernels, call(): pl.pallas_call(body, out_shape=outs, in_specs=specs, out_specs=[spec(pltp...  23.4 us
    ppermute x5, starting transfers between devices, trade(): return lax.ppermute(x, ('sub', 'slab'), pairs)  18 us
    ppermute x6, starting transfers between devices, rise(): return lax.ppermute(x, 'slab', [(0, 2), (1, 3)])  13.7 us
    ppermute x5, waiting for transfers between devices, trade(): return lax.ppermute(x, ('sub', 'slab'), pairs)  8.69 us
    ppermute x5, starting transfers between devices, fall(): return lax.ppermute(x, 'slab', [(2, 0), (3, 1)])  6.45 us
    ppermute x4, waiting for transfers between devices, swap(): return lax.ppermute(x, 'slab', [(i, i ^ 1) for i in range(levels)])  5.39 us
    ppermute x5, waiting for transfers between devices, fall(): return lax.ppermute(x, 'slab', [(2, 0), (3, 1)])  4.88 us
    ppermute x6, waiting for transfers between devices, rise(): return lax.ppermute(x, 'slab', [(0, 2), (1, 3)])  2.73 us
  transfers between devices with their start and end apart: 20, of which 10 were waited for; matrix products, arithmetic and copies ran while one was open for 0% of the time, Pallas kernels for 21%

profile of v6, /device:TPU:0, one launch (start us, length us, event | category | flops | bytes accessed | tf_op | source)
XLA Modules:
  0.0 84.7 jit_solution(15809297450689329386)
XLA Ops:
  0.0 0.5 collective-permute-start.1
  0.5 3.4 %shard_map.91 = (bf16[2,1024,1024]{2,1,0:T(8,128)(2,1)S(1)}, f32[136,1024]{1,0:T(8,128)S(1)}, f32[136,1024]{1,0:T(8,128)S(1)}) custom-call(f32[1024,1024]{1,0:T(8,128)} %bitcast.24, f32[128,1024]{1,0:T(8,128)} %bitcast.25, f32[32,1024]{1,0:T(8,128)} %bitcast.13, f32[32,1024]{1,0:T(8,128)} %bitcast.15, f32[1,1024]{1,0:T(1,128)} %bitcast.26, s32[1,32]{1,0:T(1,128)} %bitcast.21), custom_call_target="tpu_custom_call" | custom-call | flops 1600000000 | tf_op jit(solution)/shard_map/pallas_call | solution.py:76
  3.9 0.1 collective-permute-start
  4.0 0.1 fusion.own_spots
  4.1 4.2 %collective-permute-done.recv = f32[136,1024]{1,0:T(8,128)S(1)} collective-permute-done((f32[136,1024]{1,0:T(8,128)S(1)}, f32[136,1024]{1,0:T(8,128)S(1)}, u32[]{:S(2)}, u32[]{:S(2)}) %collective-permute-start) | collective-permute-done | bytes 557088 | tf_op jit(solution)/shard_map/ppermute | solution.py:515
  8.3 0.1 compare_convert_fusion.oth_spots
  8.4 1.0 %shard_map.92.refs_0_.refs_1_ = bf16[2,2,1024,1024]{3,2,1,0:T(8,128)(2,1)S(1)} custom-call(f32[1024,1024]{1,0:T(8,128)S(1)} %collective-permute-done.1.matrix, bf16[2,1024,1024]{2,1,0:T(8,128)(2,1)S(1)} %get-tuple-element.44.own), custom_call_target="tpu_custom_call" | custom-call | flops 800000000 | tf_op jit(solution)/shard_map/pallas_call | solution.py:76
  9.4 0.8 shard_map.93
  10.2 4.0 %collective-permute-start.2 = (f32[32,1024]{1,0:T(8,128)S(1)}, f32[32,1024]{1,0:T(8,128)S(1)}, u32[]{:S(2)}, u32[]{:S(2)}) collective-permute-start(f32[32,1024]{1,0:T(8,128)S(1)} %get-tuple-element.46.f_second.refs_1_), channel_id=1, source_target_pairs={{0,2},{1,3},{4,6},{5,7},{8,10},{9,11},{12,14},{13,15},{16,18},{17,... | collective-permute-start | bytes 393224 | tf_op jit(solution)/shard_map/ppermute | solution.py:518
  14.2 0.9 %shard_map.96 = (f32[32,1024]{1,0:T(8,128)S(1)}, f32[32,1024]{1,0:T(8,128)S(1)}, f32[64,1024]{1,0:T(8,128)S(1)}, f32[64,1024]{1,0:T(8,128)S(1)}) custom-call(f32[136,1024]{1,0:T(8,128)S(1)} %get-tuple-element.42.keep, f32[136,1024]{1,0:T(8,128)S(1)} %collective-permute-done.recv, bf16[2,2,1024,1024]{3,2,1,0:T(8,128)(2,1)S(1)} %shard_map.92.refs_0_.refs_1_), custom_call_target="tpu_custom_call" | custom-call | flops 800000000 | tf_op jit(solution)/shard_map/pallas_call | solution.py:76
  15.1 1.3 %collective-permute-start.7 = (f32[32,1024]{1,0:T(8,128)S(1)}, f32[32,1024]{1,0:T(8,128)S(1)}, u32[]{:S(2)}, u32[]{:S(2)}) collective-permute-start(f32[32,1024]{1,0:T(8,128)S(1)} %get-tuple-element.61.f_second.refs_5_), channel_id=1, source_target_pairs={{0,2},{1,3},{4,6},{5,7},{8,10},{9,11},{12,14},{13,15},{16,18},{17,... | collective-permute-start | bytes 393224 | tf_op jit(solution)/shard_map/ppermute | solution.py:518
  16.4 2.6 %shard_map.97 = (f32[32,1024]{1,0:T(8,128)S(1)}, f32[32,1024]{1,0:T(8,128)S(1)}, f32[64,1024]{1,0:T(8,128)S(1)}) custom-call(f32[32,1024]{1,0:T(8,128)S(1)} %fusion.own_spots, f32[32,1024]{1,0:T(8,128)S(1)} %compare_convert_fusion.oth_spots, f32[64,1024]{1,0:T(8,128)S(1)} %get-tuple-element.54.k_second, bf16[2,2,1024,1024]{3,2,1,0:T(8,128)(2,1)S(1)} %shard_map.92.refs_0_.refs_1_), custom_call_target="tpu_custom_call" | custom-call | flops 1600000000 | tf_op jit(solution)/shard_map/pallas_call | solution.py:76
  19.0 1.3 %collective-permute-start.5 = (f32[64,1024]{1,0:T(8,128)S(1)}, f32[64,1024]{1,0:T(8,128)S(1)}, u32[]{:S(2)}, u32[]{:S(2)}) collective-permute-start(f32[64,1024]{1,0:T(8,128)S(1)} %get-tuple-element.55), channel_id=1, source_target_pairs={{0,2},{1,3},{4,6},{5,7},{8,10},{9,11},{12,14},{13,15},{16,18},{17,... | collective-permute-start | bytes 786440 | tf_op jit(solution)/shard_map/ppermute | solution.py:518
  20.4 1.3 %collective-permute-start.3 = (f32[32,1024]{1,0:T(8,128)S(1)}, f32[32,1024]{1,0:T(8,128)S(1)}, u32[]{:S(2)}, u32[]{:S(2)}) collective-permute-start(f32[32,1024]{1,0:T(8,128)S(1)} %get-tuple-element.47.refs_1_), channel_id=1, source_target_pairs={{2,0},{3,1},{6,4},{7,5},{10,8},{11,9},{14,12},{15,13},{18,16},{19,... | collective-permute-start | bytes 393224 | tf_op jit(solution)/shard_map/ppermute | solution.py:521
  21.7 1.3 %collective-permute-start.8 = (f32[32,1024]{1,0:T(8,128)S(1)}, f32[32,1024]{1,0:T(8,128)S(1)}, u32[]{:S(2)}, u32[]{:S(2)}) collective-permute-start(f32[32,1024]{1,0:T(8,128)S(1)} %get-tuple-element.62.refs_1_.refs_3_), channel_id=1, source_target_pairs={{2,0},{3,1},{6,4},{7,5},{10,8},{11,9},{14,12},{15,13},{18,16},{19,... | collective-permute-start | bytes 393224 | tf_op jit(solution)/shard_map/ppermute | solution.py:521
  23.0 4.5 %collective-permute-done.3.carried = f32[32,1024]{1,0:T(8,128)S(1)} collective-permute-done((f32[32,1024]{1,0:T(8,128)S(1)}, f32[32,1024]{1,0:T(8,128)S(1)}, u32[]{:S(2)}, u32[]{:S(2)}) %collective-permute-start.3) | collective-permute-done | bytes 131104 | tf_op jit(solution)/shard_map/ppermute | solution.py:521
  27.5 3.0 %shard_map.95 = (f32[32,1024]{1,0:T(8,128)S(1)}, f32[32,1024]{1,0:T(8,128)S(1)}, f32[32,1024]{1,0:T(8,128)S(1)}, f32[32,1024]{1,0:T(8,128)S(1)}) custom-call(f32[136,1024]{1,0:T(8,128)S(1)} %get-tuple-element.42.keep, f32[136,1024]{1,0:T(8,128)S(1)} %collective-permute-done.recv, ...), custom_call_target="tpu_custom_call", output_to_operand_aliasing={{0}: (6, {}), {1}: (7, {})} | custom-call | flops 3200000000 | tf_op jit(solution)/shard_map/pallas_call | solution.py:76
  30.5 0.0 collective-permute-done.5.refs_0_.carried
  30.5 0.2 shard_map.105
  30.8 0.4 collective-permute-done.8.carried
  31.1 3.0 %shard_map.101 = (f32[32,1024]{1,0:T(8,128)S(1)}, f32[32,1024]{1,0:T(8,128)S(1)}, f32[32,1024]{1,0:T(8,128)S(1)}, f32[32,1024]{1,0:T(8,128)S(1)}) custom-call(f32[136,1024]{1,0:T(8,128)S(1)} %get-tuple-element.42.keep, f32[136,1024]{1,0:T(8,128)S(1)} %collective-permute-done.recv, ...), custom_call_target="tpu_custom_call", output_to_operand_aliasing={{0}: (6, {}), {1}: (7, {})} | custom-call | flops 3200000000 | tf_op jit(solution)/shard_map/pallas_call | solution.py:76
  34.1 1.3 %collective-permute-start.9 = (f32[32,1024]{1,0:T(8,128)S(1)}, f32[32,1024]{1,0:T(8,128)S(1)}, u32[]{:S(2)}, u32[]{:S(2)}) collective-permute-start(f32[32,1024]{1,0:T(8,128)S(1)} %get-tuple-element.67.f_second.refs_7_), channel_id=1, source_target_pairs={{0,2},{1,3},{4,6},{5,7},{8,10},{9,11},{12,14},{13,15},{16,18},{17,... | collective-permute-start | bytes 393224 | tf_op jit(solution)/shard_map/ppermute | solution.py:518
  35.5 4.5 %collective-permute-start.15 = (f32[16,128]{1,0:T(8,128)S(1)}, f32[16,128]{1,0:T(8,128)S(1)}, u32[]{:S(2)}, u32[]{:S(2)}) collective-permute-start(f32[16,128]{1,0:T(8,128)S(1)} %bitcast.18), channel_id=1, source_target_pairs={{0,16},{1,17},{4,20},{5,21},{8,24},{9,25},{12,28},{13,29},{16,0},{... | collective-permute-start | bytes 24584 | tf_op jit(solution)/shard_map/ppermute | solution.py:527
  40.0 1.9 %collective-permute-done.15 = f32[16,128]{1,0:T(8,128)S(1)} collective-permute-done((f32[16,128]{1,0:T(8,128)S(1)}, f32[16,128]{1,0:T(8,128)S(1)}, u32[]{:S(2)}, u32[]{:S(2)}) %collective-permute-start.15) | collective-permute-done | bytes 8224 | tf_op jit(solution)/shard_map/ppermute | solution.py:527
  41.9 3.5 %collective-permute-start.16 = (f32[32,128]{1,0:T(8,128)S(1)}, f32[32,128]{1,0:T(8,128)S(1)}, u32[]{:S(2)}, u32[]{:S(2)}) collective-permute-start(f32[32,128]{1,0:T(8,128)S(1)} %pad_maximum_fusion.3), channel_id=1, source_target_pairs={{0,8},{1,9},{4,12},{5,13},{8,0},{9,1},{12,4},{13,5},{16,24},{17,25... | collective-permute-start | bytes 49160 | tf_op jit(solution)/shard_map/ppermute | solution.py:527
  45.4 1.3 %collective-permute-start.12 = (f32[40,1024]{1,0:T(8,128)S(1)}, f32[40,1024]{1,0:T(8,128)S(1)}, u32[]{:S(2)}, u32[]{:S(2)}) collective-permute-start(f32[40,1024]{1,0:T(8,128)S(1)} %get-tuple-element.76), channel_id=1, source_target_pairs={{2,0},{3,1},{6,4},{7,5},{10,8},{11,9},{14,12},{15,13},{18,16},{19,... | collective-permute-start | bytes 491528 | tf_op jit(solution)/shard_map/ppermute | solution.py:521
  46.7 4.6 %collective-permute-start.4 = (f32[32,1024]{1,0:T(8,128)S(1)}, f32[32,1024]{1,0:T(8,128)S(1)}, u32[]{:S(2)}, u32[]{:S(2)}) collective-permute-start(f32[32,1024]{1,0:T(8,128)S(1)} %get-tuple-element.52.f_second.refs_3_), channel_id=1, source_target_pairs={{0,2},{1,3},{4,6},{5,7},{8,10},{9,11},{12,14},{13,15},{16,18},{17,... | collective-permute-start | bytes 393224 | tf_op jit(solution)/shard_map/ppermute | solution.py:518
  51.3 1.3 %collective-permute-start.10 = (f32[32,1024]{1,0:T(8,128)S(1)}, f32[32,1024]{1,0:T(8,128)S(1)}, u32[]{:S(2)}, u32[]{:S(2)}) collective-permute-start(f32[32,1024]{1,0:T(8,128)S(1)} %get-tuple-element.68.refs_1_), channel_id=1, source_target_pairs={{2,0},{3,1},{6,4},{7,5},{10,8},{11,9},{14,12},{15,13},{18,16},{19,... | collective-permute-start | bytes 393224 | tf_op jit(solution)/shard_map/ppermute | solution.py:521
  52.6 1.1 %collective-permute-done.4.carried = f32[32,1024]{1,0:T(8,128)S(1)} collective-permute-done((f32[32,1024]{1,0:T(8,128)S(1)}, f32[32,1024]{1,0:T(8,128)S(1)}, u32[]{:S(2)}, u32[]{:S(2)}) %collective-permute-start.4) | collective-permute-done | bytes 131104 | tf_op jit(solution)/shard_map/ppermute | solution.py:518
  53.7 1.3 %collective-permute-start.6 = (f32[64,1024]{1,0:T(8,128)S(1)}, f32[64,1024]{1,0:T(8,128)S(1)}, u32[]{:S(2)}, u32[]{:S(2)}) collective-permute-start(f32[64,1024]{1,0:T(8,128)S(1)} %get-tuple-element.56.refs_1_), channel_id=1, source_target_pairs={{2,0},{3,1},{6,4},{7,5},{10,8},{11,9},{14,12},{15,13},{18,16},{19,... | collective-permute-start | bytes 786440 | tf_op jit(solution)/shard_map/ppermute | solution.py:521
  55.1 0.8 shard_map.106
  55.8 4.5 %collective-permute-start.13 = (f32[64,128]{1,0:T(8,128)S(1)}, f32[64,128]{1,0:T(8,128)S(1)}, u32[]{:S(2)}, u32[]{:S(2)}) collective-permute-start(f32[64,128]{1,0:T(8,128)S(1)} %shard_map.106), channel_id=1, source_target_pairs={{0,16},{1,17},{4,20},{5,21},{8,24},{9,25},{12,28},{13,29},{16,0},{... | collective-permute-start | bytes 98312 | tf_op jit(solution)/shard_map/ppermute | solution.py:527
  60.4 2.4 %collective-permute-done.13 = f32[64,128]{1,0:T(8,128)S(1)} collective-permute-done((f32[64,128]{1,0:T(8,128)S(1)}, f32[64,128]{1,0:T(8,128)S(1)}, u32[]{:S(2)}, u32[]{:S(2)}) %collective-permute-start.13) | collective-permute-done | bytes 32800 | tf_op jit(solution)/shard_map/ppermute | solution.py:527
  62.8 2.1 %collective-permute-start.14 = (f32[128,128]{1,0:T(8,128)S(1)}, f32[128,128]{1,0:T(8,128)S(1)}, u32[]{:S(2)}, u32[]{:S(2)}) collective-permute-start(f32[128,128]{1,0:T(8,128)S(1)} %pad_maximum_fusion.1), channel_id=1, source_target_pairs={{0,8},{1,9},{4,12},{5,13},{8,0},{9,1},{12,4},{13,5},{16,24},{17,25... | collective-permute-start | bytes 196616 | tf_op jit(solution)/shard_map/ppermute | solution.py:527
  64.9 4.0 %collective-permute-done.14 = f32[128,128]{1,0:T(8,128)S(1)} collective-permute-done((f32[128,128]{1,0:T(8,128)S(1)}, f32[128,128]{1,0:T(8,128)S(1)}, u32[]{:S(2)}, u32[]{:S(2)}) %collective-permute-start.14) | collective-permute-done | bytes 65568 | tf_op jit(solution)/shard_map/ppermute | solution.py:527
  69.0 3.4 %collective-permute-start.17 = (f32[320,128]{1,0:T(8,128)S(1)}, f32[320,128]{1,0:T(8,128)S(1)}, u32[]{:S(2)}, u32[]{:S(2)}) collective-permute-start(f32[320,128]{1,0:T(8,128)S(1)} %constant_dynamic-update-slice_fusion), channel_id=1, source_target_pairs={{0,4},{1,5},{4,0},{5,1},{8,12},{9,13},{12,8},{13,9},{16,20},{17,21... | collective-permute-start | bytes 491528 | tf_op jit(solution)/shard_map/ppermute | solution.py:527
  72.4 1.6 %shard_map.103 = (f32[32,1024]{1,0:T(8,128)S(1)}, f32[32,1024]{1,0:T(8,128)S(1)}) custom-call(f32[32,1024]{1,0:T(8,128)S(1)} %get-tuple-element.66.f_first.refs_6_, f32[32,1024]{1,0:T(8,128)S(1)} %get-tuple-element.67.f_second.refs_7_, f32[64,1024]{1,0:T(8,128)S(1)} %get-tuple-element.53.k_first, ...), custom_call_target="tpu_custom_call", output_to_operand_aliasing={{0}: (6, {}), {1}: (7, {})} | custom-call | flops 1600000000 | tf_op jit(solution)/shard_map/pallas_call | solution.py:76
  74.0 0.0 collective-permute-done.6.carried
  74.0 0.0 copy-start.1
  74.0 1.7 %shard_map.99 = (f32[64,1024]{1,0:T(8,128)S(1)}, f32[64,1024]{1,0:T(8,128)S(1)}) custom-call(f32[32,1024]{1,0:T(8,128)S(1)} %get-tuple-element.51.f_first.refs_2_, f32[32,1024]{1,0:T(8,128)S(1)} %get-tuple-element.52.f_second.refs_3_, f32[64,1024]{1,0:T(8,128)S(1)} %get-tuple-element.53.k_first, ...), custom_call_target="tpu_custom_call", output_to_operand_aliasing={{0}: (6, {}), {1}: (7, {})} | custom-call | flops 1600000000 | tf_op jit(solution)/shard_map/pallas_call | solution.py:76
  75.7 0.1 shard_map.104
  75.8 0.1 collective-permute-start.11
  75.9 0.3 collective-permute-done.17
  76.3 3.1 %shard_map.107 = f32[64,128]{1,0:T(8,128)S(1)} custom-call(f32[512,128]{1,0:T(8,128)S(1)} %pad_maximum_fusion.values, f32[128,128]{1,0:T(8,128)S(1)} %pad_maximum_fusion.2.fixed), custom_call_target="tpu_custom_call" | custom-call | flops 400000000 | tf_op jit(solution)/shard_map/pallas_call | solution.py:76
  79.4 1.3 %collective-permute-start.18 = (f32[64,128]{1,0:T(8,128)S(1)}, f32[64,128]{1,0:T(8,128)S(1)}, u32[]{:S(2)}, u32[]{:S(2)}) collective-permute-start(f32[64,128]{1,0:T(8,128)S(1)} %shard_map.107), channel_id=1, source_target_pairs={{0,2},{1,3},{4,6},{5,7},{8,10},{9,11},{12,14},{13,15},{16,18},{17,... | collective-permute-start | bytes 98312 | tf_op jit(solution)/shard_map/ppermute | solution.py:518
  80.7 1.6 %collective-permute-done.18 = f32[64,128]{1,0:T(8,128)S(1)} collective-permute-done((f32[64,128]{1,0:T(8,128)S(1)}, f32[64,128]{1,0:T(8,128)S(1)}, u32[]{:S(2)}, u32[]{:S(2)}) %collective-permute-start.18) | collective-permute-done | bytes 32800 | tf_op jit(solution)/shard_map/ppermute | solution.py:518
  82.3 1.2 %collective-permute-done.19.q_recv = f32[64,128]{1,0:T(8,128)S(1)} collective-permute-done((f32[64,128]{1,0:T(8,128)S(1)}, f32[64,128]{1,0:T(8,128)S(1)}, u32[]{:S(2)}, u32[]{:S(2)}) %collective-permute-start.19) | collective-permute-done | bytes 32800 | tf_op jit(solution)/shard_map/ppermute | solution.py:515
  83.5 1.2 %shard_map.108 = f32[128,1024]{1,0:T(8,128)} custom-call(f32[96,1024]{1,0:T(8,128)S(1)} %get-tuple-element.72.keep, f32[96,1024]{1,0:T(8,128)S(1)} %collective-permute-done.11.recv, f32[64,128]{1,0:T(8,128)S(1)} %broadcast_select_fusion.q_keep, f32[64,128]{1,0:T(8,128)S(1)} %collective-permute-done.19.q_recv, f32[32,1024]{1,0:T(8,128)S(1)} %bitcast.14, ...), custom_call_target="tpu_custom_call" | custom-call | flops 400000000 | tf_op jit(solution)/shard_map/pallas_call | solution.py:76
  (40 shorter events, 0.2 us)
Async XLA Ops:
  0.0 4.0 %copy-start.4 = (s32[1,1,32]{2,1,0:T(1,128)S(1)}, s32[1,1,32]{2,1,0:T(1,128)}, u32[]{:S(2)}) copy-start(s32[1,1,32]{2,1,0:T(1,128)} %param.12) | copy-start | bytes 388
  0.0 8.4 %collective-permute-start.1 = (f32[1024,1024]{1,0:T(8,128)}, f32[1024,1024]{1,0:T(8,128)S(1)}, u32[]{:S(2)}, u32[]{:S(2)}) collective-permute-start(f32[1024,1024]{1,0:T(8,128)} %bitcast.23), channel_id=1, source_target_pairs={{0,1},{1,0},{2,3},{3,2},{4,5},{5,4},{6,7},{7,6},{8,9},{9,8},{10,11... | collective-permute-start | bytes 12582920 | tf_op jit(solution)/shard_map/ppermute | solution.py:515
  3.9 4.4 %collective-permute-start = (f32[136,1024]{1,0:T(8,128)S(1)}, f32[136,1024]{1,0:T(8,128)S(1)}, u32[]{:S(2)}, u32[]{:S(2)}) collective-permute-start(f32[136,1024]{1,0:T(8,128)S(1)} %get-tuple-element.43), channel_id=1, source_target_pairs={{0,1},{1,0},{2,3},{3,2},{4,5},{5,4},{6,7},{7,6},{8,9},{9,8},{10,11... | collective-permute-start | bytes 1671176 | tf_op jit(solution)/shard_map/ppermute | solution.py:515
  10.2 10.1 %collective-permute-start.2 = (f32[32,1024]{1,0:T(8,128)S(1)}, f32[32,1024]{1,0:T(8,128)S(1)}, u32[]{:S(2)}, u32[]{:S(2)}) collective-permute-start(f32[32,1024]{1,0:T(8,128)S(1)} %get-tuple-element.46.f_second.refs_1_), channel_id=1, source_target_pairs={{0,2},{1,3},{4,6},{5,7},{8,10},{9,11},{12,14},{13,15},{16,18},{17,... | collective-permute-start | bytes 393224 | tf_op jit(solution)/shard_map/ppermute | solution.py:518
  15.1 6.6 %collective-permute-start.7 = (f32[32,1024]{1,0:T(8,128)S(1)}, f32[32,1024]{1,0:T(8,128)S(1)}, u32[]{:S(2)}, u32[]{:S(2)}) collective-permute-start(f32[32,1024]{1,0:T(8,128)S(1)} %get-tuple-element.61.f_second.refs_5_), channel_id=1, source_target_pairs={{0,2},{1,3},{4,6},{5,7},{8,10},{9,11},{12,14},{13,15},{16,18},{17,... | collective-permute-start | bytes 393224 | tf_op jit(solution)/shard_map/ppermute | solution.py:518
  19.0 11.5 %collective-permute-start.5 = (f32[64,1024]{1,0:T(8,128)S(1)}, f32[64,1024]{1,0:T(8,128)S(1)}, u32[]{:S(2)}, u32[]{:S(2)}) collective-permute-start(f32[64,1024]{1,0:T(8,128)S(1)} %get-tuple-element.55), channel_id=1, source_target_pairs={{0,2},{1,3},{4,6},{5,7},{8,10},{9,11},{12,14},{13,15},{16,18},{17,... | collective-permute-start | bytes 786440 | tf_op jit(solution)/shard_map/ppermute | solution.py:518
  20.4 7.1 %collective-permute-start.3 = (f32[32,1024]{1,0:T(8,128)S(1)}, f32[32,1024]{1,0:T(8,128)S(1)}, u32[]{:S(2)}, u32[]{:S(2)}) collective-permute-start(f32[32,1024]{1,0:T(8,128)S(1)} %get-tuple-element.47.refs_1_), channel_id=1, source_target_pairs={{2,0},{3,1},{6,4},{7,5},{10,8},{11,9},{14,12},{15,13},{18,16},{19,... | collective-permute-start | bytes 393224 | tf_op jit(solution)/shard_map/ppermute | solution.py:521
  21.7 9.4 %collective-permute-start.8 = (f32[32,1024]{1,0:T(8,128)S(1)}, f32[32,1024]{1,0:T(8,128)S(1)}, u32[]{:S(2)}, u32[]{:S(2)}) collective-permute-start(f32[32,1024]{1,0:T(8,128)S(1)} %get-tuple-element.62.refs_1_.refs_3_), channel_id=1, source_target_pairs={{2,0},{3,1},{6,4},{7,5},{10,8},{11,9},{14,12},{15,13},{18,16},{19,... | collective-permute-start | bytes 393224 | tf_op jit(solution)/shard_map/ppermute | solution.py:521
  31.1 4.3 %copy-start.3 = (f32[128,16]{0,1:T(8,128)S(1)}, f32[128,16]{0,1:T(8,128)}, u32[]{:S(2)}) copy-start(f32[128,16]{0,1:T(8,128)} %param.17) | copy-start | bytes 24580
  31.1 8.8 %copy-start.5 = (s32[1,32]{1,0:T(1,128)S(1)}, s32[1,32]{1,0:T(1,128)}, u32[]{:S(2)}) copy-start(s32[1,32]{1,0:T(1,128)} %param.13) | copy-start | bytes 388
  34.1 17.1 %collective-permute-start.9 = (f32[32,1024]{1,0:T(8,128)S(1)}, f32[32,1024]{1,0:T(8,128)S(1)}, u32[]{:S(2)}, u32[]{:S(2)}) collective-permute-start(f32[32,1024]{1,0:T(8,128)S(1)} %get-tuple-element.67.f_second.refs_7_), channel_id=1, source_target_pairs={{0,2},{1,3},{4,6},{5,7},{8,10},{9,11},{12,14},{13,15},{16,18},{17,... | collective-permute-start | bytes 393224 | tf_op jit(solution)/shard_map/ppermute | solution.py:518
  35.5 6.4 %collective-permute-start.15 = (f32[16,128]{1,0:T(8,128)S(1)}, f32[16,128]{1,0:T(8,128)S(1)}, u32[]{:S(2)}, u32[]{:S(2)}) collective-permute-start(f32[16,128]{1,0:T(8,128)S(1)} %bitcast.18), channel_id=1, source_target_pairs={{0,16},{1,17},{4,20},{5,21},{8,24},{9,25},{12,28},{13,29},{16,0},{... | collective-permute-start | bytes 24584 | tf_op jit(solution)/shard_map/ppermute | solution.py:527
  41.9 27.1 %collective-permute-start.16 = (f32[32,128]{1,0:T(8,128)S(1)}, f32[32,128]{1,0:T(8,128)S(1)}, u32[]{:S(2)}, u32[]{:S(2)}) collective-permute-start(f32[32,128]{1,0:T(8,128)S(1)} %pad_maximum_fusion.3), channel_id=1, source_target_pairs={{0,8},{1,9},{4,12},{5,13},{8,0},{9,1},{12,4},{13,5},{16,24},{17,25... | collective-permute-start | bytes 49160 | tf_op jit(solution)/shard_map/ppermute | solution.py:527
  45.4 9.7 %collective-permute-start.12 = (f32[40,1024]{1,0:T(8,128)S(1)}, f32[40,1024]{1,0:T(8,128)S(1)}, u32[]{:S(2)}, u32[]{:S(2)}) collective-permute-start(f32[40,1024]{1,0:T(8,128)S(1)} %get-tuple-element.76), channel_id=1, source_target_pairs={{2,0},{3,1},{6,4},{7,5},{10,8},{11,9},{14,12},{15,13},{18,16},{19,... | collective-permute-start | bytes 491528 | tf_op jit(solution)/shard_map/ppermute | solution.py:521
  46.7 7.1 %collective-permute-start.4 = (f32[32,1024]{1,0:T(8,128)S(1)}, f32[32,1024]{1,0:T(8,128)S(1)}, u32[]{:S(2)}, u32[]{:S(2)}) collective-permute-start(f32[32,1024]{1,0:T(8,128)S(1)} %get-tuple-element.52.f_second.refs_3_), channel_id=1, source_target_pairs={{0,2},{1,3},{4,6},{5,7},{8,10},{9,11},{12,14},{13,15},{16,18},{17,... | collective-permute-start | bytes 393224 | tf_op jit(solution)/shard_map/ppermute | solution.py:518
  51.3 3.8 %copy-start.2 = (f32[1,32,32]{2,1,0:T(8,128)S(1)}, f32[1,32,32]{2,1,0:T(8,128)}, u32[]{:S(2)}) copy-start(f32[1,32,32]{2,1,0:T(8,128)} %param.14) | copy-start | bytes 12292
  51.3 21.1 %collective-permute-start.10 = (f32[32,1024]{1,0:T(8,128)S(1)}, f32[32,1024]{1,0:T(8,128)S(1)}, u32[]{:S(2)}, u32[]{:S(2)}) collective-permute-start(f32[32,1024]{1,0:T(8,128)S(1)} %get-tuple-element.68.refs_1_), channel_id=1, source_target_pairs={{2,0},{3,1},{6,4},{7,5},{10,8},{11,9},{14,12},{15,13},{18,16},{19,... | collective-permute-start | bytes 393224 | tf_op jit(solution)/shard_map/ppermute | solution.py:521
  53.7 20.3 %collective-permute-start.6 = (f32[64,1024]{1,0:T(8,128)S(1)}, f32[64,1024]{1,0:T(8,128)S(1)}, u32[]{:S(2)}, u32[]{:S(2)}) collective-permute-start(f32[64,1024]{1,0:T(8,128)S(1)} %get-tuple-element.56.refs_1_), channel_id=1, source_target_pairs={{2,0},{3,1},{6,4},{7,5},{10,8},{11,9},{14,12},{15,13},{18,16},{19,... | collective-permute-start | bytes 786440 | tf_op jit(solution)/shard_map/ppermute | solution.py:521
  55.8 7.0 %collective-permute-start.13 = (f32[64,128]{1,0:T(8,128)S(1)}, f32[64,128]{1,0:T(8,128)S(1)}, u32[]{:S(2)}, u32[]{:S(2)}) collective-permute-start(f32[64,128]{1,0:T(8,128)S(1)} %shard_map.106), channel_id=1, source_target_pairs={{0,16},{1,17},{4,20},{5,21},{8,24},{9,25},{12,28},{13,29},{16,0},{... | collective-permute-start | bytes 98312 | tf_op jit(solution)/shard_map/ppermute | solution.py:527
  62.8 6.1 %collective-permute-start.14 = (f32[128,128]{1,0:T(8,128)S(1)}, f32[128,128]{1,0:T(8,128)S(1)}, u32[]{:S(2)}, u32[]{:S(2)}) collective-permute-start(f32[128,128]{1,0:T(8,128)S(1)} %pad_maximum_fusion.1), channel_id=1, source_target_pairs={{0,8},{1,9},{4,12},{5,13},{8,0},{9,1},{12,4},{13,5},{16,24},{17,25... | collective-permute-start | bytes 196616 | tf_op jit(solution)/shard_map/ppermute | solution.py:527
  69.0 7.2 %collective-permute-start.17 = (f32[320,128]{1,0:T(8,128)S(1)}, f32[320,128]{1,0:T(8,128)S(1)}, u32[]{:S(2)}, u32[]{:S(2)}) collective-permute-start(f32[320,128]{1,0:T(8,128)S(1)} %constant_dynamic-update-slice_fusion), channel_id=1, source_target_pairs={{0,4},{1,5},{4,0},{5,1},{8,12},{9,13},{12,8},{13,9},{16,20},{17,21... | collective-permute-start | bytes 491528 | tf_op jit(solution)/shard_map/ppermute | solution.py:527
  74.0 9.5 %copy-start = (f32[1,1,32,1024]{3,2,1,0:T(8,128)S(1)}, f32[1,1,32,1024]{3,2,1,0:T(8,128)}, u32[]{:S(2)}) copy-start(f32[1,1,32,1024]{3,2,1,0:T(8,128)} %param.15) | copy-start | bytes 393220
  74.0 9.5 %copy-start.1 = (f32[1,1,32,1024]{3,2,1,0:T(8,128)S(1)}, f32[1,1,32,1024]{3,2,1,0:T(8,128)}, u32[]{:S(2)}) copy-start(f32[1,1,32,1024]{3,2,1,0:T(8,128)} %param.16) | copy-start | bytes 393220
  75.8 7.7 %collective-permute-start.11 = (f32[96,1024]{1,0:T(8,128)S(1)}, f32[96,1024]{1,0:T(8,128)S(1)}, u32[]{:S(2)}, u32[]{:S(2)}) collective-permute-start(f32[96,1024]{1,0:T(8,128)S(1)} %get-tuple-element.73), channel_id=1, source_target_pairs={{0,1},{1,0},{2,3},{3,2},{4,5},{5,4},{6,7},{7,6},{8,9},{9,8},{10,11... | collective-permute-start | bytes 1179656 | tf_op jit(solution)/shard_map/ppermute | solution.py:515
  79.4 2.9 %collective-permute-start.18 = (f32[64,128]{1,0:T(8,128)S(1)}, f32[64,128]{1,0:T(8,128)S(1)}, u32[]{:S(2)}, u32[]{:S(2)}) collective-permute-start(f32[64,128]{1,0:T(8,128)S(1)} %shard_map.107), channel_id=1, source_target_pairs={{0,2},{1,3},{4,6},{5,7},{8,10},{9,11},{12,14},{13,15},{16,18},{17,... | collective-permute-start | bytes 98312 | tf_op jit(solution)/shard_map/ppermute | solution.py:518
  82.3 1.2 %collective-permute-start.19 = (f32[64,128]{1,0:T(8,128)S(1)}, f32[64,128]{1,0:T(8,128)S(1)}, u32[]{:S(2)}, u32[]{:S(2)}) collective-permute-start(f32[64,128]{1,0:T(8,128)S(1)} %broadcast_select_fusion.q_keep), channel_id=1, source_target_pairs={{0,1},{1,0},{2,3},{3,2},{4,5},{5,4},{6,7},{7,6},{8,9},{9,8},{10,11... | collective-permute-start | bytes 98312 | tf_op jit(solution)/shard_map/ppermute | solution.py:515

commit v7 on v6

--- a/solution.py
+++ b/solution.py
@@ -352,10 +352,12 @@
     hold(pair() != 1, old, (y_first, y_second))
 
 
-def score_turn(carried, schur, maps, y_first, y_second, k_first, k_second, *refs):
-    blocks, values = refs[:-1], refs[-1]
+def score_turn(subs, carried, schur, maps, inverse, y_first, y_second, k_first, k_second, *refs):
+    blocks, copies, values = refs[:-2], refs[-2], refs[-1]
     prim = y_first.shape[0]
-    half, width = values.shape
+    width = values.shape[1]
+    half = BLOCKS * blocks[0].shape[0]
+    share = inverse.shape[0]
 
     @pl.when(pair() == 0)
     def _():
@@ -369,7 +371,7 @@
             second, placed(y_second[...] + carried[:prim, :], (0, 1, 2), width)
         )
         extra = k_first.shape[0]
-        values[...] = (
+        values[:half, :] = (
             unpack(carried, prim, half, width)
             + only(w[:half], 0, prim)
             + only(w[half : half + extra], 2, prim)
@@ -377,6 +379,10 @@
         )
         values[:prim, 3 * prim : 4 * prim] = schur[...]
         values[prim : prim + 1, 3 * prim : 4 * prim] = maps[...]
+        for i in range(inverse.shape[1] // width):
+            values[half + i * share : half + (i + 1) * share, :] = inverse[:, i * width : (i + 1) * width]
+        for j in range(subs):
+            copies[j] = values[...]
 
 
 def settle(*refs):
@@ -395,94 +401,90 @@
     return jnp.concatenate([x, jnp.zeros((rows - x.shape[0], x.shape[1]), f32)], axis=0)
 
 
-def solve(subs, prim, values, fixed, q):
-    half, width = q.shape
-    count = fixed.shape[1]
-    share = fixed.shape[0] // subs
-    me = lax.axis_index("sub")
-    unknown = lax.broadcasted_iota(jnp.int32, (count, width), 0)
-    block = unknown // share
-    far = jnp.zeros_like(block)
-    for bit in range(subs.bit_length() - 1):
-        far = far | (((block >> bit) & 1) << (subs.bit_length() - 2 - bit))
-    there = (far ^ me) * share + unknown % share
-    unknown, there = unknown.astype(f32), there.astype(f32)
-    lane = lax.broadcasted_iota(jnp.int32, (half, width), 1)
-
-    def at(ref, j, size, start=0, stop=None):
-        stop = size if stop is None else stop
-        base = j * size + start
-        if not isinstance(base, int):
-            base = pl.multiple_of(base, 8)
-        return ref[pl.ds(base, stop - start), :]
-
-    def loop(body, begin):
-        if subs <= 8:
-            for j in range(subs):
-                begin = body(j, begin)
-            return begin
-        return lax.fori_loop(0, subs, body, begin)
-
-    def times_rows(left, right):
-        top, low = halves(right)
-        return three(left, top, low, dot_rows)
-
-    def times_plain(left, right):
-        top, low = halves(right)
-        return three(left, top, low)
-
-    def map_of(v):
-        row = pltpu.roll(v[prim : prim + 8, :], width - 3 * prim, 1)[0:1]
-        return jnp.where(lane[0:1] < prim, row, -1.0)
-
-    def times_schur(left, v, signs):
-        rows = [v[:prim] if sign > 0 else -v[:prim] for sign in signs]
-        out = times_plain(left, wide(jnp.concatenate(rows, axis=0), width))
-        return jnp.where(lane < prim, pltpu.roll(out, width - 3 * prim, 1), 0.0)
-
-    def spot(row, ids):
-        return (ids == row).astype(f32)
-
-    def pick_plain(left, spots):
-        top, low = halves(left)
-        both = dot(jnp.concatenate([top, low], axis=0), spots.astype(bf16))
-        return both[:half] + both[half:]
-
-    def pick_rows(left, spots):
-        top, low = halves(left)
-        both = dot_rows(jnp.concatenate([top, low], axis=0), spots.astype(bf16))
-        return both[:half] + both[half:]
-
-    def add_first(j, total):
-        v = at(values, j, half)
-        return total + pick_rows(v, spot(map_of(v), unknown))
-
-    inverse = fixed[...]
-    zero = jnp.zeros((half, count), f32)
-    found = times_rows(loop(add_first, zero), inverse)
-
-    def parts(j):
-        v = at(values, j, half)
-        row = map_of(v)
-        first = pick_plain(found, spot(pltpu.roll(row, prim, 1), there)) - times_schur(v, v, (1,))
-        change = times_plain(first, wide(v[: 2 * prim], width))
-        return v, row, first, jnp.where(lane < 2 * prim, v, change)
-
-    def add_second(j, total):
-        _, row, _, p = parts(j)
-        signs = (
-            spot(row, unknown)
-            - spot(pltpu.roll(row, prim, 1), unknown)
-            - spot(pltpu.roll(row, 2 * prim, 1), unknown)
-        )
-        return total + pick_rows(p, signs)
-
-    found_two = times_rows(loop(add_second, zero), inverse)
-    v, row, first, p = parts(0)
-    second = pick_plain(found_two, spot(pltpu.roll(row, prim, 1), there)) - times_schur(
-        p, v, (1, -1, -1)
-    )
-    q[...] = first + pltpu.roll(first + second, 2 * prim, 1)
+def solve(prim, share, values, q):
+    @pl.when(pair() == 0)
+    def _():
+        half, width = q.shape
+        subs, height = values.shape[:2]
+        count = subs * share
+        unknown = lax.broadcasted_iota(jnp.int32, (count, width), 0).astype(f32)
+        lane = lax.broadcasted_iota(jnp.int32, (half, width), 1)
+
+        def at(j):
+            return values[j, :half, :]
+
+        def share_of(j):
+            return jnp.concatenate(
+                [values[j, i : i + share, :] for i in range(half, height, share)], axis=1
+            )
+
+        def loop(body, begin):
+            if subs <= 8:
+                for j in range(subs):
+                    begin = body(j, begin)
+                return begin
+            return lax.fori_loop(0, subs, body, begin)
+
+        def times_rows(left, right):
+            top, low = halves(right)
+            return three(left, top, low, dot_rows)
+
+        def times_plain(left, right):
+            top, low = halves(right)
+            return three(left, top, low)
+
+        def map_of(v):
+            row = pltpu.roll(v[prim : prim + 8, :], width - 3 * prim, 1)[0:1]
+            return jnp.where(lane[0:1] < prim, row, -1.0)
+
+        def times_schur(left, v, signs):
+            rows = [v[:prim] if sign > 0 else -v[:prim] for sign in signs]
+            out = times_plain(left, wide(jnp.concatenate(rows, axis=0), width))
+            return jnp.where(lane < prim, pltpu.roll(out, width - 3 * prim, 1), 0.0)
+
+        def spot(row, ids):
+            return (ids == row).astype(f32)
+
+        def pick_plain(left, spots):
+            top, low = halves(left)
+            both = dot(jnp.concatenate([top, low], axis=0), spots.astype(bf16))
+            return both[:half] + both[half:]
+
+        def pick_rows(left, spots):
+            top, low = halves(left)
+            both = dot_rows(jnp.concatenate([top, low], axis=0), spots.astype(bf16))
+            return both[:half] + both[half:]
+
+        def add_first(j, total):
+            v = at(j)
+            return total + pick_rows(v, spot(map_of(v), unknown))
+
+        inverse = jnp.concatenate([share_of(j) for j in range(subs)], axis=0)
+        zero = jnp.zeros((half, count), f32)
+        found = times_rows(loop(add_first, zero), inverse)
+
+        def parts(j):
+            v = at(j)
+            row = map_of(v)
+            first = pick_plain(found, spot(pltpu.roll(row, prim, 1), unknown)) - times_schur(v, v, (1,))
+            change = times_plain(first, wide(v[: 2 * prim], width))
+            return v, row, first, jnp.where(lane < 2 * prim, v, change)
+
+        def add_second(j, total):
+            _, row, _, p = parts(j)
+            signs = (
+                spot(row, unknown)
+                - spot(pltpu.roll(row, prim, 1), unknown)
+                - spot(pltpu.roll(row, 2 * prim, 1), unknown)
+            )
+            return total + pick_rows(p, signs)
+
+        found_two = times_rows(loop(add_second, zero), inverse)
+        v, row, first, p = parts(lax.axis_index("sub"))
+        second = pick_plain(found_two, spot(pltpu.roll(row, prim, 1), unknown)) - times_schur(
+            p, v, (1, -1, -1)
+        )
+        q[...] = first + pltpu.roll(first + second, 2 * prim, 1)
 
 
 def finish(keep, recv, q_keep, q_recv, one, two, out):
@@ -509,7 +511,7 @@
 ):
     levels = lax.axis_size("slab")
     subs = lax.axis_size("sub")
-    assert levels == 4 and subs & (subs - 1) == 0
+    assert levels == 4
 
     def swap(x):
         return lax.ppermute(x, "slab", [(i, i ^ 1) for i in range(levels)])
@@ -519,39 +521,24 @@
 
     def fall(x):
         return lax.ppermute(x, "slab", [(2, 0), (3, 1)])
-
-    def trade(x, distance):
-        pairs = [
-            (i * levels + k, (i ^ distance) * levels + k) for i in range(subs) for k in range(2)
-        ]
-        return lax.ppermute(x, ("sub", "slab"), pairs)
-
-    def join(x, y):
-        return jnp.concatenate([x, y], axis=0)
 
     vector = residual[0, 0]
     matrix = inverse_slab[0, 0]
     one, two = constraint_basis[0, 0], coarse_basis[0, 0]
     rows, size = vector.shape
     prim = primal_index.shape[-1]
-    coarse_count, _ = coarse_inverse.shape
+    coarse_count, share = coarse_inverse.shape
     half = rows // 2
     block = half // BLOCKS
     extra = 2 * prim
     width = -(-3 * prim // LANES) * LANES
     packed = -(-half * width // (8 * size)) * 8
-    assert half == extra and prim <= coarse_count and size % width == 0 and 4 * prim <= width
+    assert half == extra and prim <= coarse_count and size % width == 0 and 4 * prim <= width and coarse_count % width == 0
 
     def like(count, *heights):
         return [struct((h, size)) for h in heights for _ in range(count)]
 
     other_matrix = swap(matrix)
-
-    inverse = coarse_inverse.T
-    distance = subs // 2
-    while distance > 1:
-        inverse = join(inverse, trade(inverse, distance))
-        distance //= 2
 
     own, keep, send = call(
         first_products,
@@ -626,23 +613,25 @@
     pieces = []
     for i in span:
         pieces += [*f[i], *g[i]]
+    height = half + coarse_count // width * share
     (values,) = call(
-        score_turn,
-        [struct((half, width))],
-        [z_back, schur_small[0], coarse_map.astype(f32), y_first, y_second, k_first, k_second, *pieces],
+        functools.partial(score_turn, subs),
+        [struct((subs, height, width))],
+        [
+            z_back,
+            schur_small[0],
+            coarse_map.astype(f32),
+            coarse_inverse.T,
+            y_first,
+            y_second,
+            k_first,
+            k_second,
+            *pieces,
+        ],
         1,
-    )
-    distance = subs // 2
-    while distance > 1:
-        values = join(values, trade(values, distance))
-        distance //= 2
-    if coarse_count == width:
-        others = trade(join(values, inverse), 1)
-        inverse = join(inverse, others[values.shape[0] :])
-        values = join(values, others[: values.shape[0]])
-    else:
-        inverse = join(inverse, trade(inverse, 1))
-        values = join(values, trade(values, 1))
+        scratch=[pltpu.VMEM((height, width), f32)],
+    )
+    values = lax.all_to_all(values, "sub", 0, 0)
 
     n_two = []
     for i in span:
@@ -670,11 +659,11 @@
     m_recv = swap(m_send)
 
     (q,) = call(
-        functools.partial(solve, subs, prim),
+        functools.partial(solve, prim, share),
         [struct((half, width))],
-        [values, inverse],
+        [values],
         0.5,
-        limit=VMEM_LIMIT + 8 * (values.size + inverse.size),
+        limit=VMEM_LIMIT + 8 * values.size,
     )
     q_upper = rise(q)
     q = jnp.where(pair() == 0, q, q_upper)

time: 85.2 us -> 76.3 us (0.90)
  starting transfers between devices: 38.8 us -> 26.9 us
  local copies, waits for them, and re-layouts: 0.07 us -> 7.51 us
  waiting for transfers between devices: 21.7 us -> 16.3 us
    ppermute x5 -> x0, starting transfers between devices: 18 us -> none  [trade(): return lax.ppermute(x, ('sub', 'slab'), pairs)]
    ppermute x5 -> x0, waiting for transfers between devices: 8.69 us -> none  [trade(): return lax.ppermute(x, ('sub', 'slab'), pairs)]
    unnamed x17 -> x26, local copies, waits for them, and re-layouts: 0.05 us -> 7.51 us
    all_to_all x0 -> x1, starting transfers between devices: none -> 5.81 us  [on_device(): values = lax.all_to_all(values, 'sub', 0, 0)]
    ppermute x5, waiting for transfers between devices: 4.88 us -> 9.34 us  [fall(): return lax.ppermute(x, 'slab', [(2, 0), (3, 1)])]
    ppermute x6, waiting for transfers between devices: 2.73 us -> 1.59 us  [rise(): return lax.ppermute(x, 'slab', [(0, 2), (1, 3)])]
  transfers between devices with their start and end apart: 20 -> 16, of which waited for: 10 -> 5; matrix products, arithmetic and copies ran while one was open for 0% -> 0% of each run, Pallas kernels for 21% -> 24%
where the time goes in v7:
time: 76.3 us; the launch traced here: 75.5 us
  starting transfers between devices  26.9 us (35%)
  Pallas kernels  24.2 us (32%)
  waiting for transfers between devices  16.3 us (21%)
  local copies, waits for them, and re-layouts  7.51 us (10%)
    pallas_call x18, Pallas kernels, call(): pl.pallas_call(body, out_shape=outs, in_specs=specs, out_specs=[spec(pltp...  24.2 us
    ppermute x6, starting transfers between devices, rise(): return lax.ppermute(x, 'slab', [(0, 2), (1, 3)])  13.7 us
    ppermute x5, waiting for transfers between devices, fall(): return lax.ppermute(x, 'slab', [(2, 0), (3, 1)])  9.34 us
    unnamed x26, local copies, waits for them, and re-layouts  7.51 us
    ppermute x5, starting transfers between devices, fall(): return lax.ppermute(x, 'slab', [(2, 0), (3, 1)])  6.71 us
    all_to_all x1, starting transfers between devices, on_device(): values = lax.all_to_all(values, 'sub', 0, 0)  5.81 us
    ppermute x4, waiting for transfers between devices, swap(): return lax.ppermute(x, 'slab', [(i, i ^ 1) for i in range(levels)])  5.38 us
    ppermute x6, waiting for transfers between devices, rise(): return lax.ppermute(x, 'slab', [(0, 2), (1, 3)])  1.59 us
  transfers between devices with their start and end apart: 16, of which 5 were waited for; matrix products, arithmetic and copies ran while one was open for 0% of the time, Pallas kernels for 24%

profile of v7, /device:TPU:0, one launch (start us, length us, event | category | flops | bytes accessed | tf_op | source)
XLA Modules:
  0.0 75.5 jit_solution(2279653201698623857)
XLA Ops:
  0.0 0.5 collective-permute-start.1
  0.5 3.4 %shard_map.91 = (bf16[2,1024,1024]{2,1,0:T(8,128)(2,1)S(1)}, f32[136,1024]{1,0:T(8,128)S(1)}, f32[136,1024]{1,0:T(8,128)S(1)}) custom-call(f32[1024,1024]{1,0:T(8,128)} %bitcast.21, f32[128,1024]{1,0:T(8,128)} %bitcast.22, f32[32,1024]{1,0:T(8,128)} %bitcast.12, f32[32,1024]{1,0:T(8,128)} %bitcast.14, f32[1,1024]{1,0:T(1,128)} %bitcast.23, s32[1,32]{1,0:T(1,128)} %bitcast.18), custom_call_target="tpu_custom_call" | custom-call | flops 1600000000 | tf_op jit(solution)/shard_map/pallas_call | solution.py:76
  3.9 0.1 collective-permute-start
  4.0 0.1 fusion.own_spots
  4.1 4.2 %collective-permute-done.recv = f32[136,1024]{1,0:T(8,128)S(1)} collective-permute-done((f32[136,1024]{1,0:T(8,128)S(1)}, f32[136,1024]{1,0:T(8,128)S(1)}, u32[]{:S(2)}, u32[]{:S(2)}) %collective-permute-start) | collective-permute-done | bytes 557088 | tf_op jit(solution)/shard_map/ppermute | solution.py:517
  8.3 0.1 compare_convert_fusion.oth_spots
  8.4 0.0 collective-permute-done.1.matrix
  8.4 1.0 %shard_map.92.refs_0_.refs_1_ = bf16[2,2,1024,1024]{3,2,1,0:T(8,128)(2,1)S(1)} custom-call(f32[1024,1024]{1,0:T(8,128)S(1)} %collective-permute-done.1.matrix, bf16[2,1024,1024]{2,1,0:T(8,128)(2,1)S(1)} %get-tuple-element.44.own), custom_call_target="tpu_custom_call" | custom-call | flops 800000000 | tf_op jit(solution)/shard_map/pallas_call | solution.py:76
  9.4 0.8 %shard_map.93 = (f32[32,1024]{1,0:T(8,128)S(1)}, f32[32,1024]{1,0:T(8,128)S(1)}) custom-call(f32[136,1024]{1,0:T(8,128)S(1)} %get-tuple-element.42.keep, f32[136,1024]{1,0:T(8,128)S(1)} %collective-permute-done.recv, bf16[2,2,1024,1024]{3,2,1,0:T(8,128)(2,1)S(1)} %shard_map.92.refs_0_.refs_1_), custom_call_target="tpu_custom_call" | custom-call | flops 800000000 | tf_op jit(solution)/shard_map/pallas_call | solution.py:76
  10.2 4.0 %collective-permute-start.2 = (f32[32,1024]{1,0:T(8,128)S(1)}, f32[32,1024]{1,0:T(8,128)S(1)}, u32[]{:S(2)}, u32[]{:S(2)}) collective-permute-start(f32[32,1024]{1,0:T(8,128)S(1)} %get-tuple-element.46.f_second.refs_1_), channel_id=1, source_target_pairs={{0,2},{1,3},{4,6},{5,7},{8,10},{9,11},{12,14},{13,15},{16,18},{17,... | collective-permute-start | bytes 393224 | tf_op jit(solution)/shard_map/ppermute | solution.py:520
  14.2 0.9 %shard_map.96 = (f32[32,1024]{1,0:T(8,128)S(1)}, f32[32,1024]{1,0:T(8,128)S(1)}, f32[64,1024]{1,0:T(8,128)S(1)}, f32[64,1024]{1,0:T(8,128)S(1)}) custom-call(f32[136,1024]{1,0:T(8,128)S(1)} %get-tuple-element.42.keep, f32[136,1024]{1,0:T(8,128)S(1)} %collective-permute-done.recv, bf16[2,2,1024,1024]{3,2,1,0:T(8,128)(2,1)S(1)} %shard_map.92.refs_0_.refs_1_), custom_call_target="tpu_custom_call" | custom-call | flops 800000000 | tf_op jit(solution)/shard_map/pallas_call | solution.py:76
  15.1 1.3 %collective-permute-start.7 = (f32[32,1024]{1,0:T(8,128)S(1)}, f32[32,1024]{1,0:T(8,128)S(1)}, u32[]{:S(2)}, u32[]{:S(2)}) collective-permute-start(f32[32,1024]{1,0:T(8,128)S(1)} %get-tuple-element.61.f_second.refs_5_), channel_id=1, source_target_pairs={{0,2},{1,3},{4,6},{5,7},{8,10},{9,11},{12,14},{13,15},{16,18},{17,... | collective-permute-start | bytes 393224 | tf_op jit(solution)/shard_map/ppermute | solution.py:520
  16.4 2.6 %shard_map.97 = (f32[32,1024]{1,0:T(8,128)S(1)}, f32[32,1024]{1,0:T(8,128)S(1)}, f32[64,1024]{1,0:T(8,128)S(1)}) custom-call(f32[32,1024]{1,0:T(8,128)S(1)} %fusion.own_spots, f32[32,1024]{1,0:T(8,128)S(1)} %compare_convert_fusion.oth_spots, f32[64,1024]{1,0:T(8,128)S(1)} %get-tuple-element.54.k_second, bf16[2,2,1024,1024]{3,2,1,0:T(8,128)(2,1)S(1)} %shard_map.92.refs_0_.refs_1_), custom_call_target="tpu_custom_call" | custom-call | flops 1600000000 | tf_op jit(solution)/shard_map/pallas_call | solution.py:76
  19.0 1.3 %collective-permute-start.5 = (f32[64,1024]{1,0:T(8,128)S(1)}, f32[64,1024]{1,0:T(8,128)S(1)}, u32[]{:S(2)}, u32[]{:S(2)}) collective-permute-start(f32[64,1024]{1,0:T(8,128)S(1)} %get-tuple-element.55), channel_id=1, source_target_pairs={{0,2},{1,3},{4,6},{5,7},{8,10},{9,11},{12,14},{13,15},{16,18},{17,... | collective-permute-start | bytes 786440 | tf_op jit(solution)/shard_map/ppermute | solution.py:520
  20.3 0.0 collective-permute-done.2.carried
  20.4 1.3 %collective-permute-start.3 = (f32[32,1024]{1,0:T(8,128)S(1)}, f32[32,1024]{1,0:T(8,128)S(1)}, u32[]{:S(2)}, u32[]{:S(2)}) collective-permute-start(f32[32,1024]{1,0:T(8,128)S(1)} %get-tuple-element.47.refs_1_), channel_id=1, source_target_pairs={{2,0},{3,1},{6,4},{7,5},{10,8},{11,9},{14,12},{15,13},{18,16},{19,... | collective-permute-start | bytes 393224 | tf_op jit(solution)/shard_map/ppermute | solution.py:523
  21.7 1.3 %collective-permute-start.8 = (f32[32,1024]{1,0:T(8,128)S(1)}, f32[32,1024]{1,0:T(8,128)S(1)}, u32[]{:S(2)}, u32[]{:S(2)}) collective-permute-start(f32[32,1024]{1,0:T(8,128)S(1)} %get-tuple-element.62.refs_1_.refs_3_), channel_id=1, source_target_pairs={{2,0},{3,1},{6,4},{7,5},{10,8},{11,9},{14,12},{15,13},{18,16},{19,... | collective-permute-start | bytes 393224 | tf_op jit(solution)/shard_map/ppermute | solution.py:523
  23.0 4.5 %collective-permute-done.3.carried = f32[32,1024]{1,0:T(8,128)S(1)} collective-permute-done((f32[32,1024]{1,0:T(8,128)S(1)}, f32[32,1024]{1,0:T(8,128)S(1)}, u32[]{:S(2)}, u32[]{:S(2)}) %collective-permute-start.3) | collective-permute-done | bytes 131104 | tf_op jit(solution)/shard_map/ppermute | solution.py:523
  27.5 3.0 %shard_map.95 = (f32[32,1024]{1,0:T(8,128)S(1)}, f32[32,1024]{1,0:T(8,128)S(1)}, f32[32,1024]{1,0:T(8,128)S(1)}, f32[32,1024]{1,0:T(8,128)S(1)}) custom-call(f32[136,1024]{1,0:T(8,128)S(1)} %get-tuple-element.42.keep, f32[136,1024]{1,0:T(8,128)S(1)} %collective-permute-done.recv, ...), custom_call_target="tpu_custom_call", output_to_operand_aliasing={{0}: (6, {}), {1}: (7, {})} | custom-call | flops 3200000000 | tf_op jit(solution)/shard_map/pallas_call | solution.py:76
  30.5 0.0 copy-start.5
  30.6 0.2 shard_map.105
  30.8 0.4 copy-done.3
  31.2 0.1 copy-done.5
  31.3 0.0 collective-permute-done.8.carried
  31.3 3.0 %shard_map.101 = (f32[32,1024]{1,0:T(8,128)S(1)}, f32[32,1024]{1,0:T(8,128)S(1)}, f32[32,1024]{1,0:T(8,128)S(1)}, f32[32,1024]{1,0:T(8,128)S(1)}) custom-call(f32[136,1024]{1,0:T(8,128)S(1)} %get-tuple-element.42.keep, f32[136,1024]{1,0:T(8,128)S(1)} %collective-permute-done.recv, ...), custom_call_target="tpu_custom_call", output_to_operand_aliasing={{0}: (6, {}), {1}: (7, {})} | custom-call | flops 3200000000 | tf_op jit(solution)/shard_map/pallas_call | solution.py:76
  34.3 1.3 %collective-permute-start.9 = (f32[32,1024]{1,0:T(8,128)S(1)}, f32[32,1024]{1,0:T(8,128)S(1)}, u32[]{:S(2)}, u32[]{:S(2)}) collective-permute-start(f32[32,1024]{1,0:T(8,128)S(1)} %get-tuple-element.67.f_second.refs_7_), channel_id=1, source_target_pairs={{0,2},{1,3},{4,6},{5,7},{8,10},{9,11},{12,14},{13,15},{16,18},{17,... | collective-permute-start | bytes 393224 | tf_op jit(solution)/shard_map/ppermute | solution.py:520
  35.6 1.3 %collective-permute-start.12 = (f32[40,1024]{1,0:T(8,128)S(1)}, f32[40,1024]{1,0:T(8,128)S(1)}, u32[]{:S(2)}, u32[]{:S(2)}) collective-permute-start(f32[40,1024]{1,0:T(8,128)S(1)} %get-tuple-element.76), channel_id=1, source_target_pairs={{2,0},{3,1},{6,4},{7,5},{10,8},{11,9},{14,12},{15,13},{18,16},{19,... | collective-permute-start | bytes 491528 | tf_op jit(solution)/shard_map/ppermute | solution.py:523
  36.9 4.6 %collective-permute-start.4 = (f32[32,1024]{1,0:T(8,128)S(1)}, f32[32,1024]{1,0:T(8,128)S(1)}, u32[]{:S(2)}, u32[]{:S(2)}) collective-permute-start(f32[32,1024]{1,0:T(8,128)S(1)} %get-tuple-element.52.f_second.refs_3_), channel_id=1, source_target_pairs={{0,2},{1,3},{4,6},{5,7},{8,10},{9,11},{12,14},{13,15},{16,18},{17,... | collective-permute-start | bytes 393224 | tf_op jit(solution)/shard_map/ppermute | solution.py:520
  41.5 0.0 copy-start.9
  41.5 0.0 copy-start.10
  41.5 1.3 %collective-permute-start.10 = (f32[32,1024]{1,0:T(8,128)S(1)}, f32[32,1024]{1,0:T(8,128)S(1)}, u32[]{:S(2)}, u32[]{:S(2)}) collective-permute-start(f32[32,1024]{1,0:T(8,128)S(1)} %get-tuple-element.68.refs_1_), channel_id=1, source_target_pairs={{2,0},{3,1},{6,4},{7,5},{10,8},{11,9},{14,12},{15,13},{18,16},{19,... | collective-permute-start | bytes 393224 | tf_op jit(solution)/shard_map/ppermute | solution.py:523
  42.9 1.5 %shard_map.106 = f32[8,80,128]{2,1,0:T(8,128)} custom-call(f32[40,1024]{1,0:T(8,128)S(1)} %collective-permute-done.12.carried, f32[32,32]{1,0:T(8,128)S(1)} %bitcast.16, f32[1,32]{1,0:T(1,128)S(1)} %convert_element_type.19.maps, f32[16,128]{1,0:T(8,128)S(1)} %bitcast.17, f32[32,1024]{1,0:T(8,128)S(1)} %get-tuple-element.77.y_first, ...), custom_call_target="tpu_custom_call" | custom-call | flops 800000000 | tf_op jit(solution)/shard_map/pallas_call | solution.py:76
  44.4 5.8 %all-to-all-start = ((f32[8,80,128]{2,1,0:T(8,128)}), f32[8,80,128]{2,1,0:T(8,128)S(1)}, u32[]{:S(2)}, u32[]{:S(2)}) async-start(f32[8,80,128]{2,1,0:T(8,128)} %shard_map.106), calls=%async_computation | async-start | bytes 655360 | tf_op jit(solution)/shard_map/all_to_all | solution.py:634
  50.2 3.4 %copy-done.1 = bf16[2,2,1024,1024]{3,2,1,0:T(8,128)(2,1)S(1)} copy-done((bf16[2,2,1024,1024]{3,2,1,0:T(8,128)(2,1)S(1)}, bf16[2,2,1024,1024]{3,2,1,0:T(8,128)(2,1)}, u32[]{:S(2)}) %copy-start.1) | copy-done | bytes 8388632
  53.6 0.9 %copy-done.4 = f32[32,1024]{1,0:T(8,128)S(1)} copy-done((f32[32,1024]{1,0:T(8,128)S(1)}, f32[32,1024]{1,0:T(8,128)}, u32[]{:S(2)}) %copy-start.4) | copy-done | bytes 131096
  54.5 0.9 %copy-done.6 = f32[32,1024]{1,0:T(8,128)S(1)} copy-done((f32[32,1024]{1,0:T(8,128)S(1)}, f32[32,1024]{1,0:T(8,128)}, u32[]{:S(2)}) %copy-start.6) | copy-done | bytes 131096
  55.4 1.5 %collective-permute-start.6 = (f32[64,1024]{1,0:T(8,128)S(1)}, f32[64,1024]{1,0:T(8,128)S(1)}, u32[]{:S(2)}, u32[]{:S(2)}) collective-permute-start(f32[64,1024]{1,0:T(8,128)S(1)} %get-tuple-element.56.refs_1_), channel_id=1, source_target_pairs={{2,0},{3,1},{6,4},{7,5},{10,8},{11,9},{14,12},{15,13},{18,16},{19,... | collective-permute-start | bytes 786440 | tf_op jit(solution)/shard_map/ppermute | solution.py:523
  57.0 1.8 %copy-done.2 = bf16[2,2,1024,1024]{3,2,1,0:T(8,128)(2,1)S(1)} copy-done((bf16[2,2,1024,1024]{3,2,1,0:T(8,128)(2,1)S(1)}, bf16[2,2,1024,1024]{3,2,1,0:T(8,128)(2,1)}, u32[]{:S(2)}) %copy-start.2) | copy-done | bytes 8388632
  58.8 1.5 %shard_map.103 = (f32[32,1024]{1,0:T(8,128)S(1)}, f32[32,1024]{1,0:T(8,128)S(1)}) custom-call(f32[32,1024]{1,0:T(8,128)S(1)} %get-tuple-element.66.f_first.refs_6_, f32[32,1024]{1,0:T(8,128)S(1)} %get-tuple-element.67.f_second.refs_7_, f32[64,1024]{1,0:T(8,128)S(1)} %get-tuple-element.53.k_first, ...), custom_call_target="tpu_custom_call", output_to_operand_aliasing={{0}: (6, {}), {1}: (7, {})} | custom-call | flops 1600000000 | tf_op jit(solution)/shard_map/pallas_call | solution.py:76
  60.3 4.8 %collective-permute-done.6.carried = f32[64,1024]{1,0:T(8,128)S(1)} collective-permute-done((f32[64,1024]{1,0:T(8,128)S(1)}, f32[64,1024]{1,0:T(8,128)S(1)}, u32[]{:S(2)}, u32[]{:S(2)}) %collective-permute-start.6) | collective-permute-done | bytes 262176 | tf_op jit(solution)/shard_map/ppermute | solution.py:523
  65.1 1.4 %shard_map.99 = (f32[64,1024]{1,0:T(8,128)S(1)}, f32[64,1024]{1,0:T(8,128)S(1)}) custom-call(f32[32,1024]{1,0:T(8,128)S(1)} %get-tuple-element.51.f_first.refs_2_, f32[32,1024]{1,0:T(8,128)S(1)} %get-tuple-element.52.f_second.refs_3_, f32[64,1024]{1,0:T(8,128)S(1)} %get-tuple-element.53.k_first, ...), custom_call_target="tpu_custom_call", output_to_operand_aliasing={{0}: (6, {}), {1}: (7, {})} | custom-call | flops 1600000000 | tf_op jit(solution)/shard_map/pallas_call | solution.py:76
  66.6 0.1 shard_map.104
  66.7 0.1 collective-permute-start.11
  66.8 3.4 %shard_map.107 = f32[64,128]{1,0:T(8,128)S(1)} custom-call(f32[8,80,128]{2,1,0:T(8,128)S(1)} %all-to-all-done.values), custom_call_target="tpu_custom_call" | custom-call | flops 400000000 | tf_op jit(solution)/shard_map/pallas_call | solution.py:76
  70.2 1.3 %collective-permute-start.13 = (f32[64,128]{1,0:T(8,128)S(1)}, f32[64,128]{1,0:T(8,128)S(1)}, u32[]{:S(2)}, u32[]{:S(2)}) collective-permute-start(f32[64,128]{1,0:T(8,128)S(1)} %shard_map.107), channel_id=1, source_target_pairs={{0,2},{1,3},{4,6},{5,7},{8,10},{9,11},{12,14},{13,15},{16,18},{17,... | collective-permute-start | bytes 98312 | tf_op jit(solution)/shard_map/ppermute | solution.py:520
  71.5 1.6 %collective-permute-done.13 = f32[64,128]{1,0:T(8,128)S(1)} collective-permute-done((f32[64,128]{1,0:T(8,128)S(1)}, f32[64,128]{1,0:T(8,128)S(1)}, u32[]{:S(2)}, u32[]{:S(2)}) %collective-permute-start.13) | collective-permute-done | bytes 32800 | tf_op jit(solution)/shard_map/ppermute | solution.py:520
  73.1 1.2 %collective-permute-done.14.q_recv = f32[64,128]{1,0:T(8,128)S(1)} collective-permute-done((f32[64,128]{1,0:T(8,128)S(1)}, f32[64,128]{1,0:T(8,128)S(1)}, u32[]{:S(2)}, u32[]{:S(2)}) %collective-permute-start.14) | collective-permute-done | bytes 32800 | tf_op jit(solution)/shard_map/ppermute | solution.py:517
  74.3 1.2 %shard_map.108 = f32[128,1024]{1,0:T(8,128)} custom-call(f32[96,1024]{1,0:T(8,128)S(1)} %get-tuple-element.72.keep, f32[96,1024]{1,0:T(8,128)S(1)} %collective-permute-done.11.recv, f32[64,128]{1,0:T(8,128)S(1)} %broadcast_select_fusion.q_keep, f32[64,128]{1,0:T(8,128)S(1)} %collective-permute-done.14.q_recv, f32[32,1024]{1,0:T(8,128)S(1)} %bitcast.13, ...), custom_call_target="tpu_custom_call" | custom-call | flops 400000000 | tf_op jit(solution)/shard_map/pallas_call | solution.py:76
  (34 shorter events, 0.1 us)
Async XLA Ops:
  0.0 4.0 %copy-start.11 = (s32[1,1,32]{2,1,0:T(1,128)S(1)}, s32[1,1,32]{2,1,0:T(1,128)}, u32[]{:S(2)}) copy-start(s32[1,1,32]{2,1,0:T(1,128)} %param.12) | copy-start | bytes 388
  0.0 8.4 %collective-permute-start.1 = (f32[1024,1024]{1,0:T(8,128)}, f32[1024,1024]{1,0:T(8,128)S(1)}, u32[]{:S(2)}, u32[]{:S(2)}) collective-permute-start(f32[1024,1024]{1,0:T(8,128)} %bitcast.20), channel_id=1, source_target_pairs={{0,1},{1,0},{2,3},{3,2},{4,5},{5,4},{6,7},{7,6},{8,9},{9,8},{10,11... | collective-permute-start | bytes 12582920 | tf_op jit(solution)/shard_map/ppermute | solution.py:517
  3.9 4.4 %collective-permute-start = (f32[136,1024]{1,0:T(8,128)S(1)}, f32[136,1024]{1,0:T(8,128)S(1)}, u32[]{:S(2)}, u32[]{:S(2)}) collective-permute-start(f32[136,1024]{1,0:T(8,128)S(1)} %get-tuple-element.43), channel_id=1, source_target_pairs={{0,1},{1,0},{2,3},{3,2},{4,5},{5,4},{6,7},{7,6},{8,9},{9,8},{10,11... | collective-permute-start | bytes 1671176 | tf_op jit(solution)/shard_map/ppermute | solution.py:517
  9.4 32.1 %copy-start = (bf16[2,2,1024,1024]{3,2,1,0:T(8,128)(2,1)}, bf16[2,2,1024,1024]{3,2,1,0:T(8,128)(2,1)S(1)}, u32[]{:S(2)}) copy-start(bf16[2,2,1024,1024]{3,2,1,0:T(8,128)(2,1)S(1)} %shard_map.92.refs_0_.refs_1_) | copy-start | bytes 25165828
  10.2 10.1 %collective-permute-start.2 = (f32[32,1024]{1,0:T(8,128)S(1)}, f32[32,1024]{1,0:T(8,128)S(1)}, u32[]{:S(2)}, u32[]{:S(2)}) collective-permute-start(f32[32,1024]{1,0:T(8,128)S(1)} %get-tuple-element.46.f_second.refs_1_), channel_id=1, source_target_pairs={{0,2},{1,3},{4,6},{5,7},{8,10},{9,11},{12,14},{13,15},{16,18},{17,... | collective-permute-start | bytes 393224 | tf_op jit(solution)/shard_map/ppermute | solution.py:520
  15.1 6.6 %collective-permute-start.7 = (f32[32,1024]{1,0:T(8,128)S(1)}, f32[32,1024]{1,0:T(8,128)S(1)}, u32[]{:S(2)}, u32[]{:S(2)}) collective-permute-start(f32[32,1024]{1,0:T(8,128)S(1)} %get-tuple-element.61.f_second.refs_5_), channel_id=1, source_target_pairs={{0,2},{1,3},{4,6},{5,7},{8,10},{9,11},{12,14},{13,15},{16,18},{17,... | collective-permute-start | bytes 393224 | tf_op jit(solution)/shard_map/ppermute | solution.py:520
  19.0 11.5 %collective-permute-start.5 = (f32[64,1024]{1,0:T(8,128)S(1)}, f32[64,1024]{1,0:T(8,128)S(1)}, u32[]{:S(2)}, u32[]{:S(2)}) collective-permute-start(f32[64,1024]{1,0:T(8,128)S(1)} %get-tuple-element.55), channel_id=1, source_target_pairs={{0,2},{1,3},{4,6},{5,7},{8,10},{9,11},{12,14},{13,15},{16,18},{17,... | collective-permute-start | bytes 786440 | tf_op jit(solution)/shard_map/ppermute | solution.py:520
  20.4 7.2 %collective-permute-start.3 = (f32[32,1024]{1,0:T(8,128)S(1)}, f32[32,1024]{1,0:T(8,128)S(1)}, u32[]{:S(2)}, u32[]{:S(2)}) collective-permute-start(f32[32,1024]{1,0:T(8,128)S(1)} %get-tuple-element.47.refs_1_), channel_id=1, source_target_pairs={{2,0},{3,1},{6,4},{7,5},{10,8},{11,9},{14,12},{15,13},{18,16},{19,... | collective-permute-start | bytes 393224 | tf_op jit(solution)/shard_map/ppermute | solution.py:523
  21.7 9.6 %collective-permute-start.8 = (f32[32,1024]{1,0:T(8,128)S(1)}, f32[32,1024]{1,0:T(8,128)S(1)}, u32[]{:S(2)}, u32[]{:S(2)}) collective-permute-start(f32[32,1024]{1,0:T(8,128)S(1)} %get-tuple-element.62.refs_1_.refs_3_), channel_id=1, source_target_pairs={{2,0},{3,1},{6,4},{7,5},{10,8},{11,9},{14,12},{15,13},{18,16},{19,... | collective-permute-start | bytes 393224 | tf_op jit(solution)/shard_map/ppermute | solution.py:523
  30.5 0.7 copy-start.3
  30.5 0.7 copy-start.5
  31.3 4.3 %copy-start.12 = (s32[1,32]{1,0:T(1,128)S(1)}, s32[1,32]{1,0:T(1,128)}, u32[]{:S(2)}) copy-start(s32[1,32]{1,0:T(1,128)} %param.13) | copy-start | bytes 388
  34.3 7.2 %collective-permute-start.9 = (f32[32,1024]{1,0:T(8,128)S(1)}, f32[32,1024]{1,0:T(8,128)S(1)}, u32[]{:S(2)}, u32[]{:S(2)}) collective-permute-start(f32[32,1024]{1,0:T(8,128)S(1)} %get-tuple-element.67.f_second.refs_7_), channel_id=1, source_target_pairs={{0,2},{1,3},{4,6},{5,7},{8,10},{9,11},{12,14},{13,15},{16,18},{17,... | collective-permute-start | bytes 393224 | tf_op jit(solution)/shard_map/ppermute | solution.py:520
  35.6 7.2 %collective-permute-start.12 = (f32[40,1024]{1,0:T(8,128)S(1)}, f32[40,1024]{1,0:T(8,128)S(1)}, u32[]{:S(2)}, u32[]{:S(2)}) collective-permute-start(f32[40,1024]{1,0:T(8,128)S(1)} %get-tuple-element.76), channel_id=1, source_target_pairs={{2,0},{3,1},{6,4},{7,5},{10,8},{11,9},{14,12},{15,13},{18,16},{19,... | collective-permute-start | bytes 491528 | tf_op jit(solution)/shard_map/ppermute | solution.py:523
  36.9 13.3 %collective-permute-start.4 = (f32[32,1024]{1,0:T(8,128)S(1)}, f32[32,1024]{1,0:T(8,128)S(1)}, u32[]{:S(2)}, u32[]{:S(2)}) collective-permute-start(f32[32,1024]{1,0:T(8,128)S(1)} %get-tuple-element.52.f_second.refs_3_), channel_id=1, source_target_pairs={{0,2},{1,3},{4,6},{5,7},{8,10},{9,11},{12,14},{13,15},{16,18},{17,... | collective-permute-start | bytes 393224 | tf_op jit(solution)/shard_map/ppermute | solution.py:520
  41.5 1.4 %copy-start.9 = (f32[1,32,32]{2,1,0:T(8,128)S(1)}, f32[1,32,32]{2,1,0:T(8,128)}, u32[]{:S(2)}) copy-start(f32[1,32,32]{2,1,0:T(8,128)} %param.14) | copy-start | bytes 12292
  41.5 1.4 %copy-start.10 = (f32[128,16]{0,1:T(8,128)S(1)}, f32[128,16]{0,1:T(8,128)}, u32[]{:S(2)}) copy-start(f32[128,16]{0,1:T(8,128)} %param.17) | copy-start | bytes 24580
  41.5 15.4 %collective-permute-start.10 = (f32[32,1024]{1,0:T(8,128)S(1)}, f32[32,1024]{1,0:T(8,128)S(1)}, u32[]{:S(2)}, u32[]{:S(2)}) collective-permute-start(f32[32,1024]{1,0:T(8,128)S(1)} %get-tuple-element.68.refs_1_), channel_id=1, source_target_pairs={{2,0},{3,1},{6,4},{7,5},{10,8},{11,9},{14,12},{15,13},{18,16},{19,... | collective-permute-start | bytes 393224 | tf_op jit(solution)/shard_map/ppermute | solution.py:523
  44.4 22.4 %all-to-all-start = ((f32[8,80,128]{2,1,0:T(8,128)}), f32[8,80,128]{2,1,0:T(8,128)S(1)}, u32[]{:S(2)}, u32[]{:S(2)}) async-start(f32[8,80,128]{2,1,0:T(8,128)} %shard_map.106), calls=%async_computation | async-start | bytes 655360 | tf_op jit(solution)/shard_map/all_to_all | solution.py:634
  50.2 3.4 %copy-start.1 = (bf16[2,2,1024,1024]{3,2,1,0:T(8,128)(2,1)S(1)}, bf16[2,2,1024,1024]{3,2,1,0:T(8,128)(2,1)}, u32[]{:S(2)}) copy-start(bf16[2,2,1024,1024]{3,2,1,0:T(8,128)(2,1)} %copy-done) | copy-start | bytes 25165828
  53.6 0.9 %copy-start.4 = (f32[32,1024]{1,0:T(8,128)S(1)}, f32[32,1024]{1,0:T(8,128)}, u32[]{:S(2)}) copy-start(f32[32,1024]{1,0:T(8,128)} %copy-done.3) | copy-start | bytes 393220
  54.5 0.9 %copy-start.6 = (f32[32,1024]{1,0:T(8,128)S(1)}, f32[32,1024]{1,0:T(8,128)}, u32[]{:S(2)}) copy-start(f32[32,1024]{1,0:T(8,128)} %copy-done.5) | copy-start | bytes 393220
  55.4 3.4 %copy-start.2 = (bf16[2,2,1024,1024]{3,2,1,0:T(8,128)(2,1)S(1)}, bf16[2,2,1024,1024]{3,2,1,0:T(8,128)(2,1)}, u32[]{:S(2)}) copy-start(bf16[2,2,1024,1024]{3,2,1,0:T(8,128)(2,1)} %copy-done) | copy-start | bytes 25165828
  55.4 9.7 %collective-permute-start.6 = (f32[64,1024]{1,0:T(8,128)S(1)}, f32[64,1024]{1,0:T(8,128)S(1)}, u32[]{:S(2)}, u32[]{:S(2)}) collective-permute-start(f32[64,1024]{1,0:T(8,128)S(1)} %get-tuple-element.56.refs_1_), channel_id=1, source_target_pairs={{2,0},{3,1},{6,4},{7,5},{10,8},{11,9},{14,12},{15,13},{18,16},{19,... | collective-permute-start | bytes 786440 | tf_op jit(solution)/shard_map/ppermute | solution.py:523
  65.1 9.2 %copy-start.7 = (f32[1,1,32,1024]{3,2,1,0:T(8,128)S(1)}, f32[1,1,32,1024]{3,2,1,0:T(8,128)}, u32[]{:S(2)}) copy-start(f32[1,1,32,1024]{3,2,1,0:T(8,128)} %param.15) | copy-start | bytes 393220
  65.1 9.2 %copy-start.8 = (f32[1,1,32,1024]{3,2,1,0:T(8,128)S(1)}, f32[1,1,32,1024]{3,2,1,0:T(8,128)}, u32[]{:S(2)}) copy-start(f32[1,1,32,1024]{3,2,1,0:T(8,128)} %param.16) | copy-start | bytes 393220
  66.7 6.4 %collective-permute-start.11 = (f32[96,1024]{1,0:T(8,128)S(1)}, f32[96,1024]{1,0:T(8,128)S(1)}, u32[]{:S(2)}, u32[]{:S(2)}) collective-permute-start(f32[96,1024]{1,0:T(8,128)S(1)} %get-tuple-element.73), channel_id=1, source_target_pairs={{0,1},{1,0},{2,3},{3,2},{4,5},{5,4},{6,7},{7,6},{8,9},{9,8},{10,11... | collective-permute-start | bytes 1179656 | tf_op jit(solution)/shard_map/ppermute | solution.py:517
  70.2 2.9 %collective-permute-start.13 = (f32[64,128]{1,0:T(8,128)S(1)}, f32[64,128]{1,0:T(8,128)S(1)}, u32[]{:S(2)}, u32[]{:S(2)}) collective-permute-start(f32[64,128]{1,0:T(8,128)S(1)} %shard_map.107), channel_id=1, source_target_pairs={{0,2},{1,3},{4,6},{5,7},{8,10},{9,11},{12,14},{13,15},{16,18},{17,... | collective-permute-start | bytes 98312 | tf_op jit(solution)/shard_map/ppermute | solution.py:520
  73.1 1.2 %collective-permute-start.14 = (f32[64,128]{1,0:T(8,128)S(1)}, f32[64,128]{1,0:T(8,128)S(1)}, u32[]{:S(2)}, u32[]{:S(2)}) collective-permute-start(f32[64,128]{1,0:T(8,128)S(1)} %broadcast_select_fusion.q_keep), channel_id=1, source_target_pairs={{0,1},{1,0},{2,3},{3,2},{4,5},{5,4},{6,7},{7,6},{8,9},{9,8},{10,11... | collective-permute-start | bytes 98312 | tf_op jit(solution)/shard_map/ppermute | solution.py:517
